TPU v7x, 256 devices: a whole 4x4x8 slice. The times are simulated.
256 devices in a mesh: vel: 32 (over z, x_lo, core), gx: 8 (over y, x_hi).
Axes of the slice: x: 4 (x_hi: 2, x_lo: 2; x = x_hi * 2 + x_lo), y: 4, z: 8, core: 2. Of those that a mesh axis runs over, the one named last changes fastest.
Arguments:
- distribution: float32 [4096, 32, 256], P('vel', 'gx'), as said below
Outputs:
- relaxed: float32 [4096, 32, 256], P('vel', 'gx')
Inputs may be any that keep to these rules, and one draw needn't show every extreme that they name: `distribution`: every entry is positive.
All inputs are finite; a program needn't handle non-finite values.
Results may differ from a plain program's by a relative error of at most 0.0003.
Values sent between devices are 32-bit elements; how exact they have to be, the bound alone decides.
No kernel may reach another device: no remote copies, remote signals or barrier semaphores. Data moves between devices by JAX's collectives and lax.ppermute only.
A program may use at most 64 MiB of HBM per device.

v0:
```python
import math

import jax
import jax.numpy as jnp
from jax import lax
from jax.experimental import pallas as pl
from jax.experimental.pallas import tpu as pltpu
from jax.sharding import PartitionSpec as P

NV1 = 16
COLLISIONS = 2

speed_limit = 4.0
time_step = 0.05
knudsen = 0.0125
spacing = 2.0 * speed_limit / (NV1 - 1)
weight = spacing**3 / (2.0 * math.pi) ** 1.5

PLANES = 4
CZ = 8
CX = 8
LANES = 128
YZ = 256


def point(index):
    return -speed_limit + spacing * index.astype(jnp.float32)


def cx_column(half):
    return point(half * CX + lax.broadcasted_iota(jnp.int32, (CX, LANES), 0))


def stream_kernel(vel_ref, up0, up1, up2, down0, down1, down2, up_out, down_out, mom_out):
    vel = vel_ref[0]
    iy = vel // 2
    zhalf = vel % 2
    cy = point(iy)
    ay = time_step * jnp.abs(cy)
    ypos = iy >= NV1 // 2
    zpos = zhalf == 1
    lane = lax.broadcasted_iota(jnp.int32, (CX, LANES), 1)
    zlane = lane % 16
    ylane = jnp.where(ypos, lane, LANES - 1 - lane)
    zlane = jnp.where(zpos, zlane, 15 - zlane)
    masks_y = (ylane < 16, ylane < 32)
    masks_z = (zlane < 1, zlane < 2)
    rolls_y = (jnp.where(ypos, 16, 112), jnp.where(ypos, 32, 96))
    rolls_z = (jnp.where(zpos, 1, 127), jnp.where(zpos, 2, 126))
    wraps_z = (jnp.where(zpos, 113, 15), jnp.where(zpos, 114, 14))

    def shift_y(pair, by):
        rolled = [pltpu.roll(part, rolls_y[by], 1) for part in pair]
        mask = masks_y[by]
        return (jnp.where(mask, rolled[1], rolled[0]), jnp.where(mask, rolled[0], rolled[1]))

    def shift_z(part, by):
        return jnp.where(
            masks_z[by], pltpu.roll(part, wraps_z[by], 1), pltpu.roll(part, rolls_z[by], 1)
        )

    def block(iz, _):
        cz = point(zhalf * CZ + iz)
        az = time_step * jnp.abs(cz)
        for half in (0, 1):
            ax = time_step * jnp.abs(cx_column(half))
            keep = 1.0 - 1.5 * (ax + (ay + az))

            def section(now, one, two):
                y1, y2 = shift_y(now, 0), shift_y(now, 1)
                out = []
                for t in (0, 1):
                    along_x = (2.0 * ax) * one[t] - (0.5 * ax) * two[t]
                    along_y = (2.0 * ay) * y1[t] - (0.5 * ay) * y2[t]
                    along_z = (2.0 * az) * shift_z(now[t], 0) - (0.5 * az) * shift_z(now[t], 1)
                    out.append(keep * now[t] + (along_x + (along_y + along_z)))
                return out

            if half:
                planes = [(up2, 0), (up2, 1)] + [(up1, p) for p in range(PLANES)]
                planes += [(up0, p) for p in range(PLANES)]
            else:
                planes = [(down2, 1), (down2, 0)] + [(down1, p) for p in reversed(range(PLANES))]
                planes += [(down0, p) for p in reversed(range(PLANES))]
            sixth, first, second = {}, {}, {}
            for p, (ref, plane) in enumerate(planes):
                sixth[p] = [
                    ref[plane, iz, :, t * LANES : (t + 1) * LANES] * (1.0 / 6.0) for t in (0, 1)
                ]
                if p >= 2:
                    first[p] = section(sixth[p], sixth[p - 1], sixth[p - 2])
                if p >= 4:
                    moved = section(first[p], first[p - 1], first[p - 2])
                    second[p] = [3.0 * a + b for a, b in zip(sixth[p], moved)]
                if p >= 6:
                    moved = section(second[p], second[p - 1], second[p - 2])
                    out = up_out if half else down_out
                    for t in (0, 1):
                        out[plane, iz, :, t * LANES : (t + 1) * LANES] = (
                            2.0 * sixth[p][t] + moved[t]
                        )
        return 0

    lax.fori_loop(0, CZ, block, 0)

    for plane in range(PLANES):
        for t in (0, 1):
            cols = slice(t * LANES, (t + 1) * LANES)
            total = [0.0] * 5
            for half, out in ((0, down_out), (1, up_out)):
                zero = jnp.zeros((CX, LANES), jnp.float32)
                plain, lin, quad = zero, zero, zero
                for iz in range(CZ):
                    cz = point(zhalf * CZ + iz)
                    read = out[plane, iz, :, cols]
                    plain += read
                    lin += cz * read
                    quad += (cz * cz) * read
                cx = cx_column(half)
                terms = (plain, cx * plain, cy * plain, lin, (cx * cx + cy * cy) * plain + quad)
                total = [a + b for a, b in zip(total, terms)]
            for which in range(5):
                row = plane * 2 + t
                mom_out[which, row : row + 1, :] = weight * jnp.sum(
                    total[which], axis=0, keepdims=True
                )


def relax_kernel(last, vel_ref, mom_ref, up_in, down_in, *outs_and_scratch):
    *outs, rows = outs_and_scratch
    vel = vel_ref[0]
    cy = point(vel // 2)
    zhalf = vel % 2
    rho = mom_ref[0]
    ux = mom_ref[1] / rho
    uy = mom_ref[2] / rho
    uz = mom_ref[3] / rho
    temp = (mom_ref[4] / rho - (ux * ux + uy * uy + uz * uz)) / 3.0
    minus_half = -0.5 / temp

    def factor(c, u, scale):
        return jnp.exp((c - u) * (c - u) * scale)

    def total(u):
        out = jnp.zeros_like(u)
        for i in range(NV1):
            out += factor(-speed_limit + spacing * i, u, minus_half)
        return out

    root = jnp.sqrt(temp)
    peak = rho / (temp * root)
    mass = weight * peak * total(ux) * total(uy) * total(uz)
    nu = time_step * rho * root / knudsen
    shrink = 1.0 / (1.0 + nu)
    common = nu * shrink * peak * (rho / mass) * factor(cy, uy, minus_half)
    for iz in range(CZ):
        rows[iz] = common * factor(point(zhalf * CZ + iz), uz, minus_half)
    rows[CZ] = shrink
    rows[CZ + 1] = ux
    rows[CZ + 2] = minus_half

    def row(which, index):
        return jnp.broadcast_to(rows[which, index : index + 1, :], (CX, LANES))

    for plane in range(PLANES):
        for t in (0, 1):
            cols = slice(t * LANES, (t + 1) * LANES)
            index = plane * 2 + t
            keep, drift, scale = (row(CZ + k, index) for k in range(3))
            both = [factor(cx_column(half), drift, scale) for half in (0, 1)]
            for iz in range(CZ):
                gain = row(iz, index)
                for half, ref in ((0, down_in), (1, up_in)):
                    value = ref[plane, iz, :, cols] * keep + both[half] * gain
                    if last:
                        outs[0][plane, iz, half, :, cols] = value
                    else:
                        outs[half][plane, iz, :, cols] = value
                        if half == 0 and plane < 2:
                            outs[2][plane, iz, :, cols] = value
                        if half == 1 and plane >= 2:
                            outs[3][plane - 2, iz, :, cols] = value


def vmem():
    return pl.BlockSpec(memory_space=pltpu.VMEM)


def smem():
    return pl.BlockSpec(memory_space=pltpu.SMEM)


def shape(*sizes):
    return jax.ShapeDtypeStruct(sizes, jnp.float32)


def stream(vel, up, down):
    return pl.pallas_call(
        stream_kernel,
        in_specs=[smem()] + [vmem()] * 6,
        out_specs=[vmem()] * 3,
        out_shape=[
            shape(PLANES, CZ, CX, YZ),
            shape(PLANES, CZ, CX, YZ),
            shape(5, 2 * PLANES, LANES),
        ],
        name="stream",
    )(vel, *up, *down)


def relax(vel, moments, up, down, last):
    if last:
        out_shape = [shape(PLANES, CZ, 2, CX, YZ)]
    else:
        out_shape = [shape(PLANES, CZ, CX, YZ)] * 2 + [shape(2, CZ, CX, YZ)] * 2

    def body(*refs):
        relax_kernel(last, *refs)

    return pl.pallas_call(
        body,
        in_specs=[smem()] + [vmem()] * 3,
        out_specs=[vmem()] * len(out_shape),
        out_shape=out_shape,
        scratch_shapes=[pltpu.VMEM((CZ + 3, 2 * PLANES, LANES), jnp.float32)],
        name="relax_last" if last else "relax",
    )(vel, moments, up, down)


def passed_along(value, by):
    size = lax.axis_size("gx")
    return lax.ppermute(value, "gx", [(i, (i + by) % size) for i in range(size)])


def summed_over_velocities(value):
    size = lax.axis_size("vel")
    bit = 1
    while bit < size:
        value = value + lax.ppermute(value, "vel", [(i, i ^ bit) for i in range(size)])
        bit *= 2
    return value


def on_device(distribution):
    vel = lax.axis_index("vel").astype(jnp.int32).reshape(1)
    field = distribution.reshape(CZ, 2, CX, PLANES, YZ)
    up = field[:, 1].transpose(2, 0, 1, 3)
    down = field[:, 0].transpose(2, 0, 1, 3)
    up_far, down_far = up[2:], down[:2]
    for step in range(COLLISIONS):
        ups = (up, passed_along(up, 1), passed_along(up_far, 2))
        downs = (down, passed_along(down, -1), passed_along(down_far, -2))
        up_read, down_read, moments = stream(vel, ups, downs)
        moments = summed_over_velocities(moments)
        outs = relax(vel, moments, up_read, down_read, step == COLLISIONS - 1)
        if step < COLLISIONS - 1:
            down, up, down_far, up_far = outs
    return outs[0].transpose(1, 2, 3, 0, 4).reshape(distribution.shape)


def solution(mesh):
    return jax.shard_map(
        on_device,
        mesh=mesh,
        in_specs=(P("vel", "gx", None),),
        out_specs=P("vel", "gx", None),
        check_vma=False,
    )
```

profile of v0, /device:TPU:30, one launch (start us, length us, event | category | flops | bytes accessed | tf_op | source)
XLA Modules:
  0.0 112.8 jit_solution(9701348500541300640)
XLA Ops:
  0.0 1.1 fusion
  1.1 0.1 copy.14
  1.1 1.1 %collective-permute-start = (f32[4,8,8,256]{3,2,1,0:T(8,128)S(1)}, f32[4,8,8,256]{3,2,1,0:T(8,128)S(1)}, u32[]{:S(2)}, u32[]{:S(2)}) collective-permute-start(f32[4,8,8,256]{3,2,1,0:T(8,128)S(1)} %bitcast.16), channel_id=1, source_target_pairs={{0,1},{1,2},{2,3},{3,4},{4,5},{5,6},{6,7},{7,0},{8,9},{9,10},{10,1... | collective-permute-start | bytes 786440 | tf_op jit(solution)/shard_map/ppermute | solution.py:232
  2.3 0.1 copy.13
  2.4 2.5 %collective-permute-start.2 = (f32[4,8,8,256]{3,2,1,0:T(8,128)S(1)}, f32[4,8,8,256]{3,2,1,0:T(8,128)S(1)}, u32[]{:S(2)}, u32[]{:S(2)}) collective-permute-start(f32[4,8,8,256]{3,2,1,0:T(8,128)S(1)} %bitcast.19), channel_id=1, source_target_pairs={{0,7},{1,0},{2,1},{3,2},{4,3},{5,4},{6,5},{7,6},{8,15},{9,8},{10,9... | collective-permute-start | bytes 786440 | tf_op jit(solution)/shard_map/ppermute | solution.py:232
  4.9 0.8 collective-permute-start.3
  5.8 2.6 %collective-permute-start.1 = (f32[2,8,8,256]{3,2,1,0:T(8,128)S(1)}, f32[2,8,8,256]{3,2,1,0:T(8,128)S(1)}, u32[]{:S(2)}, u32[]{:S(2)}) collective-permute-start(f32[2,8,8,256]{3,2,1,0:T(8,128)S(1)} %slice.17), channel_id=1, source_target_pairs={{0,2},{1,3},{2,4},{3,5},{4,6},{5,7},{6,0},{7,1},{8,10},{9,11},{10,... | collective-permute-start | bytes 393224 | tf_op jit(solution)/shard_map/ppermute | solution.py:232
  8.3 8.2 %collective-permute-done.3.down2 = f32[2,8,8,256]{3,2,1,0:T(8,128)S(1)} collective-permute-done((f32[2,8,8,256]{3,2,1,0:T(8,128)S(1)}, f32[2,8,8,256]{3,2,1,0:T(8,128)S(1)}, u32[]{:S(2)}, u32[]{:S(2)}) %collective-permute-start.3) | collective-permute-done | bytes 131104 | tf_op jit(solution)/shard_map/ppermute | solution.py:232
  16.6 0.6 copy-done.6
  17.2 0.0 copy-done.7
  17.2 0.1 copy-done.2
  17.4 0.1 copy-done.3
  17.5 13.6 %stream.2 = (f32[4,8,8,256]{3,2,1,0:T(8,128)}, f32[4,8,8,256]{3,2,1,0:T(8,128)}, f32[5,8,128]{2,1,0:T(8,128)}) custom-call(s32[1]{0:T(128)} %bitcast.vel_ref.refs_0_, f32[4,8,8,256]{3,2,1,0:T(8,128)} %bitcast.18, f32[4,8,8,256]{3,2,1,0:T(8,128)} %copy-done.2, f32[2,8,8,256]{3,2,1,0:T(8,128)} %copy-done.7, f32[4,8,8,256]{3,2,1,0:T(8,128)} %bitcast.21, ...), custom_call_target="tpu_custom_call" | custom-call | tf_op jit(solution)/shard_map/stream/pallas_call | solution.py:198
  31.1 1.4 %collective-permute-done.4 = f32[5,8,128]{2,1,0:T(8,128)S(1)} collective-permute-done((f32[5,8,128]{2,1,0:T(8,128)}, f32[5,8,128]{2,1,0:T(8,128)S(1)}, u32[]{:S(2)}, u32[]{:S(2)}) %collective-permute-start.4) | collective-permute-done | bytes 20512 | tf_op jit(solution)/shard_map/ppermute | solution.py:239
  32.5 0.7 add.30
  33.2 0.8 collective-permute-start.5
  34.1 3.0 %collective-permute-done.5 = f32[5,8,128]{2,1,0:T(8,128)S(1)} collective-permute-done((f32[5,8,128]{2,1,0:T(8,128)S(1)}, f32[5,8,128]{2,1,0:T(8,128)S(1)}, u32[]{:S(2)}, u32[]{:S(2)}) %collective-permute-start.5) | collective-permute-done | bytes 20512 | tf_op jit(solution)/shard_map/ppermute | solution.py:239
  37.0 1.9 %collective-permute-start.6 = (f32[5,8,128]{2,1,0:T(8,128)S(1)}, f32[5,8,128]{2,1,0:T(8,128)S(1)}, u32[]{:S(2)}, u32[]{:S(2)}) collective-permute-start(f32[5,8,128]{2,1,0:T(8,128)S(1)} %add.31), channel_id=1, source_target_pairs={{0,32},{8,40},{16,48},{24,56},{32,0},{40,8},{48,16},{56,24},{64,96... | collective-permute-start | bytes 61448 | tf_op jit(solution)/shard_map/ppermute | solution.py:239
  38.9 1.9 %collective-permute-done.6 = f32[5,8,128]{2,1,0:T(8,128)S(1)} collective-permute-done((f32[5,8,128]{2,1,0:T(8,128)S(1)}, f32[5,8,128]{2,1,0:T(8,128)S(1)}, u32[]{:S(2)}, u32[]{:S(2)}) %collective-permute-start.6) | collective-permute-done | bytes 20512 | tf_op jit(solution)/shard_map/ppermute | solution.py:239
  40.8 3.3 %collective-permute-start.7 = (f32[5,8,128]{2,1,0:T(8,128)S(1)}, f32[5,8,128]{2,1,0:T(8,128)S(1)}, u32[]{:S(2)}, u32[]{:S(2)}) collective-permute-start(f32[5,8,128]{2,1,0:T(8,128)S(1)} %add.32), channel_id=1, source_target_pairs={{0,64},{8,72},{16,80},{24,88},{32,96},{40,104},{48,112},{56,120},{... | collective-permute-start | bytes 61448 | tf_op jit(solution)/shard_map/ppermute | solution.py:239
  44.1 1.8 %collective-permute-done.7 = f32[5,8,128]{2,1,0:T(8,128)S(1)} collective-permute-done((f32[5,8,128]{2,1,0:T(8,128)S(1)}, f32[5,8,128]{2,1,0:T(8,128)S(1)}, u32[]{:S(2)}, u32[]{:S(2)}) %collective-permute-start.7) | collective-permute-done | bytes 20512 | tf_op jit(solution)/shard_map/ppermute | solution.py:239
  45.8 6.8 %collective-permute-start.8 = (f32[5,8,128]{2,1,0:T(8,128)S(1)}, f32[5,8,128]{2,1,0:T(8,128)S(1)}, u32[]{:S(2)}, u32[]{:S(2)}) collective-permute-start(f32[5,8,128]{2,1,0:T(8,128)S(1)} %add.33), channel_id=1, source_target_pairs={{0,128},{8,136},{16,144},{24,152},{32,160},{40,168},{48,176},{56,1... | collective-permute-start | bytes 61448 | tf_op jit(solution)/shard_map/ppermute | solution.py:239
  52.7 1.8 %collective-permute-done.8 = f32[5,8,128]{2,1,0:T(8,128)S(1)} collective-permute-done((f32[5,8,128]{2,1,0:T(8,128)S(1)}, f32[5,8,128]{2,1,0:T(8,128)S(1)}, u32[]{:S(2)}, u32[]{:S(2)}) %collective-permute-start.8) | collective-permute-done | bytes 20512 | tf_op jit(solution)/shard_map/ppermute | solution.py:239
  54.4 0.6 add.34.refs_1_
  55.0 2.0 %relax.1 = (f32[4,8,8,256]{3,2,1,0:T(8,128)}, f32[4,8,8,256]{3,2,1,0:T(8,128)}, f32[2,8,8,256]{3,2,1,0:T(8,128)}, f32[2,8,8,256]{3,2,1,0:T(8,128)}) custom-call(s32[1]{0:T(128)} %bitcast.vel_ref.refs_0_, f32[5,8,128]{2,1,0:T(8,128)} %add.34.refs_1_, f32[4,8,8,256]{3,2,1,0:T(8,128)} %get-tuple-element.16.refs_2_, f32[4,8,8,256]{3,2,1,0:T(8,128)} %get-tuple-element.17.refs_3_), custom_call_target="tpu_custom_call" | custom-call | tf_op jit(solution)/shard_map/relax/pallas_call | solution.py:220
  57.1 1.7 %collective-permute-start.9 = (f32[4,8,8,256]{3,2,1,0:T(8,128)}, f32[4,8,8,256]{3,2,1,0:T(8,128)S(1)}, u32[]{:S(2)}, u32[]{:S(2)}) collective-permute-start(f32[4,8,8,256]{3,2,1,0:T(8,128)} %get-tuple-element.18.up0), channel_id=1, source_target_pairs={{0,1},{1,2},{2,3},{3,4},{4,5},{5,6},{6,7},{7,0},{8,9},{9,10},{10,1... | collective-permute-start | bytes 786440 | tf_op jit(solution)/shard_map/ppermute | solution.py:232
  58.8 1.8 %collective-permute-start.11 = (f32[4,8,8,256]{3,2,1,0:T(8,128)}, f32[4,8,8,256]{3,2,1,0:T(8,128)S(1)}, u32[]{:S(2)}, u32[]{:S(2)}) collective-permute-start(f32[4,8,8,256]{3,2,1,0:T(8,128)} %get-tuple-element.20.down0), channel_id=1, source_target_pairs={{0,7},{1,0},{2,1},{3,2},{4,3},{5,4},{6,5},{7,6},{8,15},{9,8},{10,9... | collective-permute-start | bytes 786440 | tf_op jit(solution)/shard_map/ppermute | solution.py:232
  60.6 0.8 collective-permute-start.10
  61.5 1.2 %collective-permute-start.12 = (f32[2,8,8,256]{3,2,1,0:T(8,128)}, f32[2,8,8,256]{3,2,1,0:T(8,128)S(1)}, u32[]{:S(2)}, u32[]{:S(2)}) collective-permute-start(f32[2,8,8,256]{3,2,1,0:T(8,128)} %get-tuple-element.21), channel_id=1, source_target_pairs={{0,6},{1,7},{2,0},{3,1},{4,2},{5,3},{6,4},{7,5},{8,14},{9,15},{10,... | collective-permute-start | bytes 393224 | tf_op jit(solution)/shard_map/ppermute | solution.py:232
  62.6 3.2 %collective-permute-done.10.up2 = f32[2,8,8,256]{3,2,1,0:T(8,128)S(1)} collective-permute-done((f32[2,8,8,256]{3,2,1,0:T(8,128)}, f32[2,8,8,256]{3,2,1,0:T(8,128)S(1)}, u32[]{:S(2)}, u32[]{:S(2)}) %collective-permute-start.10) | collective-permute-done | bytes 131104 | tf_op jit(solution)/shard_map/ppermute | solution.py:232
  65.8 4.8 %collective-permute-done.12.down2 = f32[2,8,8,256]{3,2,1,0:T(8,128)S(1)} collective-permute-done((f32[2,8,8,256]{3,2,1,0:T(8,128)}, f32[2,8,8,256]{3,2,1,0:T(8,128)S(1)}, u32[]{:S(2)}, u32[]{:S(2)}) %collective-permute-start.12) | collective-permute-done | bytes 131104 | tf_op jit(solution)/shard_map/ppermute | solution.py:232
  70.6 0.6 copy-done.9
  71.2 0.1 copy-done.4
  71.4 0.7 copy-done.5
  72.1 13.6 %stream.3 = (f32[4,8,8,256]{3,2,1,0:T(8,128)}, f32[4,8,8,256]{3,2,1,0:T(8,128)}, f32[5,8,128]{2,1,0:T(8,128)}) custom-call(s32[1]{0:T(128)} %bitcast.vel_ref.refs_0_, f32[4,8,8,256]{3,2,1,0:T(8,128)} %get-tuple-element.18.up0, f32[4,8,8,256]{3,2,1,0:T(8,128)} %copy-done.4, f32[2,8,8,256]{3,2,1,0:T(8,128)} %copy-done.8, ...), custom_call_target="tpu_custom_call" | custom-call | tf_op jit(solution)/shard_map/stream/pallas_call | solution.py:198
  85.7 1.4 %collective-permute-done.13 = f32[5,8,128]{2,1,0:T(8,128)S(1)} collective-permute-done((f32[5,8,128]{2,1,0:T(8,128)}, f32[5,8,128]{2,1,0:T(8,128)S(1)}, u32[]{:S(2)}, u32[]{:S(2)}) %collective-permute-start.13) | collective-permute-done | bytes 20512 | tf_op jit(solution)/shard_map/ppermute | solution.py:239
  87.1 0.7 add.35
  87.8 0.4 collective-permute-start.14
  88.3 3.3 %collective-permute-done.14 = f32[5,8,128]{2,1,0:T(8,128)S(1)} collective-permute-done((f32[5,8,128]{2,1,0:T(8,128)S(1)}, f32[5,8,128]{2,1,0:T(8,128)S(1)}, u32[]{:S(2)}, u32[]{:S(2)}) %collective-permute-start.14) | collective-permute-done | bytes 20512 | tf_op jit(solution)/shard_map/ppermute | solution.py:239
  91.6 1.0 collective-permute-start.15
  92.6 2.8 %collective-permute-done.15 = f32[5,8,128]{2,1,0:T(8,128)S(1)} collective-permute-done((f32[5,8,128]{2,1,0:T(8,128)S(1)}, f32[5,8,128]{2,1,0:T(8,128)S(1)}, u32[]{:S(2)}, u32[]{:S(2)}) %collective-permute-start.15) | collective-permute-done | bytes 20512 | tf_op jit(solution)/shard_map/ppermute | solution.py:239
  95.4 1.9 %collective-permute-start.16 = (f32[5,8,128]{2,1,0:T(8,128)S(1)}, f32[5,8,128]{2,1,0:T(8,128)S(1)}, u32[]{:S(2)}, u32[]{:S(2)}) collective-permute-start(f32[5,8,128]{2,1,0:T(8,128)S(1)} %add.37), channel_id=1, source_target_pairs={{0,64},{8,72},{16,80},{24,88},{32,96},{40,104},{48,112},{56,120},{... | collective-permute-start | bytes 61448 | tf_op jit(solution)/shard_map/ppermute | solution.py:239
  97.3 2.8 %collective-permute-done.16 = f32[5,8,128]{2,1,0:T(8,128)S(1)} collective-permute-done((f32[5,8,128]{2,1,0:T(8,128)S(1)}, f32[5,8,128]{2,1,0:T(8,128)S(1)}, u32[]{:S(2)}, u32[]{:S(2)}) %collective-permute-start.16) | collective-permute-done | bytes 20512 | tf_op jit(solution)/shard_map/ppermute | solution.py:239
  100.1 5.7 %collective-permute-start.17 = (f32[5,8,128]{2,1,0:T(8,128)S(1)}, f32[5,8,128]{2,1,0:T(8,128)S(1)}, u32[]{:S(2)}, u32[]{:S(2)}) collective-permute-start(f32[5,8,128]{2,1,0:T(8,128)S(1)} %add.38), channel_id=1, source_target_pairs={{0,128},{8,136},{16,144},{24,152},{32,160},{40,168},{48,176},{56,1... | collective-permute-start | bytes 61448 | tf_op jit(solution)/shard_map/ppermute | solution.py:239
  105.8 2.2 %collective-permute-done.17 = f32[5,8,128]{2,1,0:T(8,128)S(1)} collective-permute-done((f32[5,8,128]{2,1,0:T(8,128)S(1)}, f32[5,8,128]{2,1,0:T(8,128)S(1)}, u32[]{:S(2)}, u32[]{:S(2)}) %collective-permute-start.17) | collective-permute-done | bytes 20512 | tf_op jit(solution)/shard_map/ppermute | solution.py:239
  108.0 0.6 add.39.refs_1_
  108.6 2.0 %relax_last.1 = f32[4,8,2,8,256]{4,3,2,1,0:T(8,128)} custom-call(s32[1]{0:T(128)} %bitcast.vel_ref.refs_0_, f32[5,8,128]{2,1,0:T(8,128)} %add.39.refs_1_, f32[4,8,8,256]{3,2,1,0:T(8,128)} %get-tuple-element.23.refs_2_, f32[4,8,8,256]{3,2,1,0:T(8,128)} %get-tuple-element.24.refs_3_), custom_call_target="tpu_custom_call" | custom-call | tf_op jit(solution)/shard_map/relax_last/pallas_call | solution.py:220
  110.6 2.2 %copy.6 = f32[128,4,256]{2,1,0:T(4,128)} copy(f32[128,4,256]{2,0,1:T(8,128)} %bitcast.15) | data formatting | bytes 1048576 | tf_op jit(solution)/shard_map/reshape | solution.py:258
  (28 shorter events, 0.1 us)
Async XLA Ops:
  1.1 4.6 %copy-start = (f32[8,1,8,4,256]{4,2,0,3,1:T(8,128)}, f32[8,1,8,4,256]{4,2,0,3,1:T(8,128)S(1)}, u32[]{:S(2)}) copy-start(f32[8,1,8,4,256]{4,2,0,3,1:T(8,128)S(1)} %copy.14) | copy-start | bytes 786436
  1.1 15.4 %collective-permute-start = (f32[4,8,8,256]{3,2,1,0:T(8,128)S(1)}, f32[4,8,8,256]{3,2,1,0:T(8,128)S(1)}, u32[]{:S(2)}, u32[]{:S(2)}) collective-permute-start(f32[4,8,8,256]{3,2,1,0:T(8,128)S(1)} %bitcast.16), channel_id=1, source_target_pairs={{0,1},{1,2},{2,3},{3,4},{4,5},{5,6},{6,7},{7,0},{8,9},{9,10},{10,1... | collective-permute-start | bytes 786440 | tf_op jit(solution)/shard_map/ppermute | solution.py:232
  2.3 3.4 %copy-start.1 = (f32[8,1,8,4,256]{4,2,0,3,1:T(8,128)}, f32[8,1,8,4,256]{4,2,0,3,1:T(8,128)S(1)}, u32[]{:S(2)}) copy-start(f32[8,1,8,4,256]{4,2,0,3,1:T(8,128)S(1)} %copy.13) | copy-start | bytes 786436
  2.4 14.2 %collective-permute-start.2 = (f32[4,8,8,256]{3,2,1,0:T(8,128)S(1)}, f32[4,8,8,256]{3,2,1,0:T(8,128)S(1)}, u32[]{:S(2)}, u32[]{:S(2)}) collective-permute-start(f32[4,8,8,256]{3,2,1,0:T(8,128)S(1)} %bitcast.19), channel_id=1, source_target_pairs={{0,7},{1,0},{2,1},{3,2},{4,3},{5,4},{6,5},{7,6},{8,15},{9,8},{10,9... | collective-permute-start | bytes 786440 | tf_op jit(solution)/shard_map/ppermute | solution.py:232
  4.9 11.6 %collective-permute-start.3 = (f32[2,8,8,256]{3,2,1,0:T(8,128)S(1)}, f32[2,8,8,256]{3,2,1,0:T(8,128)S(1)}, u32[]{:S(2)}, u32[]{:S(2)}) collective-permute-start(f32[2,8,8,256]{3,2,1,0:T(8,128)S(1)} %slice.19), channel_id=1, source_target_pairs={{0,6},{1,7},{2,0},{3,1},{4,2},{5,3},{6,4},{7,5},{8,14},{9,15},{10,... | collective-permute-start | bytes 393224 | tf_op jit(solution)/shard_map/ppermute | solution.py:232
  5.8 10.8 %collective-permute-start.1 = (f32[2,8,8,256]{3,2,1,0:T(8,128)S(1)}, f32[2,8,8,256]{3,2,1,0:T(8,128)S(1)}, u32[]{:S(2)}, u32[]{:S(2)}) collective-permute-start(f32[2,8,8,256]{3,2,1,0:T(8,128)S(1)} %slice.17), channel_id=1, source_target_pairs={{0,2},{1,3},{2,4},{3,5},{4,6},{5,7},{6,0},{7,1},{8,10},{9,11},{10,... | collective-permute-start | bytes 393224 | tf_op jit(solution)/shard_map/ppermute | solution.py:232
  16.6 0.7 copy-start.6
  16.6 0.7 copy-start.7
  16.6 0.8 copy-start.2
  16.6 0.9 copy-start.3
  31.1 1.4 %collective-permute-start.4 = (f32[5,8,128]{2,1,0:T(8,128)}, f32[5,8,128]{2,1,0:T(8,128)S(1)}, u32[]{:S(2)}, u32[]{:S(2)}) collective-permute-start(f32[5,8,128]{2,1,0:T(8,128)} %get-tuple-element.15), channel_id=1, source_target_pairs={{0,8},{8,0},{16,24},{24,16},{32,40},{40,32},{48,56},{56,48},{64,72... | collective-permute-start | bytes 61448 | tf_op jit(solution)/shard_map/ppermute | solution.py:239
  33.2 3.8 %collective-permute-start.5 = (f32[5,8,128]{2,1,0:T(8,128)S(1)}, f32[5,8,128]{2,1,0:T(8,128)S(1)}, u32[]{:S(2)}, u32[]{:S(2)}) collective-permute-start(f32[5,8,128]{2,1,0:T(8,128)S(1)} %add.30), channel_id=1, source_target_pairs={{0,16},{8,24},{16,0},{24,8},{32,48},{40,56},{48,32},{56,40},{64,80... | collective-permute-start | bytes 61448 | tf_op jit(solution)/shard_map/ppermute | solution.py:239
  37.0 3.8 %collective-permute-start.6 = (f32[5,8,128]{2,1,0:T(8,128)S(1)}, f32[5,8,128]{2,1,0:T(8,128)S(1)}, u32[]{:S(2)}, u32[]{:S(2)}) collective-permute-start(f32[5,8,128]{2,1,0:T(8,128)S(1)} %add.31), channel_id=1, source_target_pairs={{0,32},{8,40},{16,48},{24,56},{32,0},{40,8},{48,16},{56,24},{64,96... | collective-permute-start | bytes 61448 | tf_op jit(solution)/shard_map/ppermute | solution.py:239
  40.8 5.0 %collective-permute-start.7 = (f32[5,8,128]{2,1,0:T(8,128)S(1)}, f32[5,8,128]{2,1,0:T(8,128)S(1)}, u32[]{:S(2)}, u32[]{:S(2)}) collective-permute-start(f32[5,8,128]{2,1,0:T(8,128)S(1)} %add.32), channel_id=1, source_target_pairs={{0,64},{8,72},{16,80},{24,88},{32,96},{40,104},{48,112},{56,120},{... | collective-permute-start | bytes 61448 | tf_op jit(solution)/shard_map/ppermute | solution.py:239
  45.8 8.6 %collective-permute-start.8 = (f32[5,8,128]{2,1,0:T(8,128)S(1)}, f32[5,8,128]{2,1,0:T(8,128)S(1)}, u32[]{:S(2)}, u32[]{:S(2)}) collective-permute-start(f32[5,8,128]{2,1,0:T(8,128)S(1)} %add.33), channel_id=1, source_target_pairs={{0,128},{8,136},{16,144},{24,152},{32,160},{40,168},{48,176},{56,1... | collective-permute-start | bytes 61448 | tf_op jit(solution)/shard_map/ppermute | solution.py:239
  57.1 13.5 %collective-permute-start.9 = (f32[4,8,8,256]{3,2,1,0:T(8,128)}, f32[4,8,8,256]{3,2,1,0:T(8,128)S(1)}, u32[]{:S(2)}, u32[]{:S(2)}) collective-permute-start(f32[4,8,8,256]{3,2,1,0:T(8,128)} %get-tuple-element.18.up0), channel_id=1, source_target_pairs={{0,1},{1,2},{2,3},{3,4},{4,5},{5,6},{6,7},{7,0},{8,9},{9,10},{10,1... | collective-permute-start | bytes 786440 | tf_op jit(solution)/shard_map/ppermute | solution.py:232
  58.8 11.8 %collective-permute-start.11 = (f32[4,8,8,256]{3,2,1,0:T(8,128)}, f32[4,8,8,256]{3,2,1,0:T(8,128)S(1)}, u32[]{:S(2)}, u32[]{:S(2)}) collective-permute-start(f32[4,8,8,256]{3,2,1,0:T(8,128)} %get-tuple-element.20.down0), channel_id=1, source_target_pairs={{0,7},{1,0},{2,1},{3,2},{4,3},{5,4},{6,5},{7,6},{8,15},{9,8},{10,9... | collective-permute-start | bytes 786440 | tf_op jit(solution)/shard_map/ppermute | solution.py:232
  60.6 5.2 %collective-permute-start.10 = (f32[2,8,8,256]{3,2,1,0:T(8,128)}, f32[2,8,8,256]{3,2,1,0:T(8,128)S(1)}, u32[]{:S(2)}, u32[]{:S(2)}) collective-permute-start(f32[2,8,8,256]{3,2,1,0:T(8,128)} %get-tuple-element.19), channel_id=1, source_target_pairs={{0,2},{1,3},{2,4},{3,5},{4,6},{5,7},{6,0},{7,1},{8,10},{9,11},{10,... | collective-permute-start | bytes 393224 | tf_op jit(solution)/shard_map/ppermute | solution.py:232
  61.5 9.1 %collective-permute-start.12 = (f32[2,8,8,256]{3,2,1,0:T(8,128)}, f32[2,8,8,256]{3,2,1,0:T(8,128)S(1)}, u32[]{:S(2)}, u32[]{:S(2)}) collective-permute-start(f32[2,8,8,256]{3,2,1,0:T(8,128)} %get-tuple-element.21), channel_id=1, source_target_pairs={{0,6},{1,7},{2,0},{3,1},{4,2},{5,3},{6,4},{7,5},{8,14},{9,15},{10,... | collective-permute-start | bytes 393224 | tf_op jit(solution)/shard_map/ppermute | solution.py:232
  65.8 4.8 %copy-start.8 = (f32[2,8,8,256]{3,2,1,0:T(8,128)}, f32[2,8,8,256]{3,2,1,0:T(8,128)S(1)}, u32[]{:S(2)}) copy-start(f32[2,8,8,256]{3,2,1,0:T(8,128)S(1)} %collective-permute-done.10.up2) | copy-start | bytes 393220
  70.6 0.7 copy-start.9
  70.6 0.8 copy-start.4
  71.4 0.7 copy-start.5
  85.7 1.4 %collective-permute-start.13 = (f32[5,8,128]{2,1,0:T(8,128)}, f32[5,8,128]{2,1,0:T(8,128)S(1)}, u32[]{:S(2)}, u32[]{:S(2)}) collective-permute-start(f32[5,8,128]{2,1,0:T(8,128)} %get-tuple-element.22), channel_id=1, source_target_pairs={{0,8},{8,0},{16,24},{24,16},{32,40},{40,32},{48,56},{56,48},{64,72... | collective-permute-start | bytes 61448 | tf_op jit(solution)/shard_map/ppermute | solution.py:239
  87.8 3.8 %collective-permute-start.14 = (f32[5,8,128]{2,1,0:T(8,128)S(1)}, f32[5,8,128]{2,1,0:T(8,128)S(1)}, u32[]{:S(2)}, u32[]{:S(2)}) collective-permute-start(f32[5,8,128]{2,1,0:T(8,128)S(1)} %add.35), channel_id=1, source_target_pairs={{0,16},{8,24},{16,0},{24,8},{32,48},{40,56},{48,32},{56,40},{64,80... | collective-permute-start | bytes 61448 | tf_op jit(solution)/shard_map/ppermute | solution.py:239
  91.6 3.8 %collective-permute-start.15 = (f32[5,8,128]{2,1,0:T(8,128)S(1)}, f32[5,8,128]{2,1,0:T(8,128)S(1)}, u32[]{:S(2)}, u32[]{:S(2)}) collective-permute-start(f32[5,8,128]{2,1,0:T(8,128)S(1)} %add.36), channel_id=1, source_target_pairs={{0,32},{8,40},{16,48},{24,56},{32,0},{40,8},{48,16},{56,24},{64,96... | collective-permute-start | bytes 61448 | tf_op jit(solution)/shard_map/ppermute | solution.py:239
  95.4 4.7 %collective-permute-start.16 = (f32[5,8,128]{2,1,0:T(8,128)S(1)}, f32[5,8,128]{2,1,0:T(8,128)S(1)}, u32[]{:S(2)}, u32[]{:S(2)}) collective-permute-start(f32[5,8,128]{2,1,0:T(8,128)S(1)} %add.37), channel_id=1, source_target_pairs={{0,64},{8,72},{16,80},{24,88},{32,96},{40,104},{48,112},{56,120},{... | collective-permute-start | bytes 61448 | tf_op jit(solution)/shard_map/ppermute | solution.py:239
  100.1 7.9 %collective-permute-start.17 = (f32[5,8,128]{2,1,0:T(8,128)S(1)}, f32[5,8,128]{2,1,0:T(8,128)S(1)}, u32[]{:S(2)}, u32[]{:S(2)}) collective-permute-start(f32[5,8,128]{2,1,0:T(8,128)S(1)} %add.38), channel_id=1, source_target_pairs={{0,128},{8,136},{16,144},{24,152},{32,160},{40,168},{48,176},{56,1... | collective-permute-start | bytes 61448 | tf_op jit(solution)/shard_map/ppermute | solution.py:239
where the time goes:
time: 113 us
  waiting for transfers between devices  38.4 us (34%)
  starting transfers between devices  34.6 us (31%)
  Pallas kernels  31.3 us (28%)
  local copies, waits for them, and re-layouts  5.72 us (5%)
  other arithmetic  2.7 us (2%)
    pallas_call x2, Pallas kernels, stream(): pl.pallas_call(stream_kernel, in_specs=[smem()] + [vmem()] * 6, out_specs...  27.2 us
    ppermute x10, waiting for transfers between devices, summed_over_velocities(): lax.ppermute(value, 'vel', [(i, i ^ bit) for i in range(size)])  22.2 us
    ppermute x10, starting transfers between devices, summed_over_velocities(): lax.ppermute(value, 'vel', [(i, i ^ bit) for i in range(size)])  21.9 us
    ppermute x8, waiting for transfers between devices, passed_along(): lax.ppermute(value, 'gx', [(i, (i + by) % size) for i in range(size)])  16.2 us
    ppermute x8, starting transfers between devices, passed_along(): lax.ppermute(value, 'gx', [(i, (i + by) % size) for i in range(size)])  12.6 us
    pallas_call x2, Pallas kernels, relax(): pl.pallas_call(body, in_specs=[smem()] + [vmem()] * 3, out_specs=[vmem()]...  4.04 us
    add x10, other arithmetic, summed_over_velocities(): value + lax.ppermute(value, 'vel', [(i, i ^ bit) for i in range(size)])  2.7 us
    unnamed x22, local copies, waits for them, and re-layouts  2.46 us
  transfers between devices with their start and end apart: 18, of which 13 were waited for; matrix products, arithmetic and copies ran while one was open for 0% of the time, Pallas kernels for 0%

commit v1 on v0

--- a/solution.py
+++ b/solution.py
@@ -205,6 +205,7 @@
             shape(5, 2 * PLANES, LANES),
         ],
         name="stream",
+        compiler_params=pltpu.CompilerParams(vmem_limit_bytes=8 << 20),
     )(vel, *up, *down)
 
 
@@ -224,6 +225,7 @@
         out_shape=out_shape,
         scratch_shapes=[pltpu.VMEM((CZ + 3, 2 * PLANES, LANES), jnp.float32)],
         name="relax_last" if last else "relax",
+        compiler_params=pltpu.CompilerParams(vmem_limit_bytes=8 << 20),
     )(vel, moments, up, down)
 
 

time: 113 us -> 99.1 us (0.88)
  Pallas kernels: 31.3 us -> 23.8 us
  local copies, waits for them, and re-layouts: 5.72 us -> 2.32 us
  other arithmetic: 2.7 us -> 0.04 us
    pallas_call x2, Pallas kernels: 4.04 us -> 0.29 us  [relax(): pl.pallas_call(body, in_specs=[smem()] + [vmem()] * 3, out_specs=[vmem()]...]
    pallas_call x2, Pallas kernels: 27.2 us -> 23.5 us  [stream(): pl.pallas_call(stream_kernel, in_specs=[smem()] + [vmem()] * 6, out_specs...]
    add x10, other arithmetic: 2.7 us -> 0.04 us  [summed_over_velocities(): value + lax.ppermute(value, 'vel', [(i, i ^ bit) for i in range(size)])]
    unnamed x22 -> x2, local copies, waits for them, and re-layouts: 2.46 us -> 0.1 us
where the time goes in v1:
time: 99.1 us; the launch traced here: 99 us
  waiting for transfers between devices  38 us (38%)
  starting transfers between devices  34.8 us (35%)
  Pallas kernels  23.8 us (24%)
  local copies, waits for them, and re-layouts  2.32 us (2%)
    pallas_call x2, Pallas kernels, stream(): pl.pallas_call(stream_kernel, in_specs=[smem()] + [vmem()] * 6, out_specs...  23.5 us
    ppermute x10, starting transfers between devices, summed_over_velocities(): lax.ppermute(value, 'vel', [(i, i ^ bit) for i in range(size)])  22.1 us
    ppermute x10, waiting for transfers between devices, summed_over_velocities(): lax.ppermute(value, 'vel', [(i, i ^ bit) for i in range(size)])  21.8 us
    ppermute x8, waiting for transfers between devices, passed_along(): lax.ppermute(value, 'gx', [(i, (i + by) % size) for i in range(size)])  16.2 us
    ppermute x8, starting transfers between devices, passed_along(): lax.ppermute(value, 'gx', [(i, (i + by) % size) for i in range(size)])  12.7 us
  transfers between devices with their start and end apart: 18, of which 13 were waited for; matrix products, arithmetic and copies ran while one was open for 0% of the time, Pallas kernels for 0%

profile of v1, /device:TPU:30, one launch (start us, length us, event | category | flops | bytes accessed | tf_op | source)
XLA Modules:
  0.0 99.0 jit_solution(7628704889796914971)
XLA Ops:
  0.0 1.1 %fusion = (f32[8,1,8,4,256]{4,3,2,1,0:T(4,128)S(1)}, f32[8,1,8,4,256]{4,3,2,1,0:T(4,128)S(1)}) fusion(f32[8,2,8,4,256]{4,3,2,1,0:T(4,128)} %bitcast.22), kind=kLoop, calls=%fused_computation.2 | loop fusion | bytes 1048576 | tf_op jit(solution)/shard_map/slice | solution.py:250
  1.1 0.1 copy.14
  1.1 1.1 %collective-permute-start = (f32[4,8,8,256]{3,2,1,0:T(8,128)S(1)}, f32[4,8,8,256]{3,2,1,0:T(8,128)S(1)}, u32[]{:S(2)}, u32[]{:S(2)}) collective-permute-start(f32[4,8,8,256]{3,2,1,0:T(8,128)S(1)} %bitcast.16), channel_id=1, source_target_pairs={{0,1},{1,2},{2,3},{3,4},{4,5},{5,6},{6,7},{7,0},{8,9},{9,10},{10,1... | collective-permute-start | bytes 786440 | tf_op jit(solution)/shard_map/ppermute | solution.py:234
  2.3 0.1 copy.13
  2.3 2.5 %collective-permute-start.2 = (f32[4,8,8,256]{3,2,1,0:T(8,128)S(1)}, f32[4,8,8,256]{3,2,1,0:T(8,128)S(1)}, u32[]{:S(2)}, u32[]{:S(2)}) collective-permute-start(f32[4,8,8,256]{3,2,1,0:T(8,128)S(1)} %bitcast.19), channel_id=1, source_target_pairs={{0,7},{1,0},{2,1},{3,2},{4,3},{5,4},{6,5},{7,6},{8,15},{9,8},{10,9... | collective-permute-start | bytes 786440 | tf_op jit(solution)/shard_map/ppermute | solution.py:234
  4.9 0.8 collective-permute-start.3
  5.7 2.6 %collective-permute-start.1 = (f32[2,8,8,256]{3,2,1,0:T(8,128)S(1)}, f32[2,8,8,256]{3,2,1,0:T(8,128)S(1)}, u32[]{:S(2)}, u32[]{:S(2)}) collective-permute-start(f32[2,8,8,256]{3,2,1,0:T(8,128)S(1)} %slice.17), channel_id=1, source_target_pairs={{0,2},{1,3},{2,4},{3,5},{4,6},{5,7},{6,0},{7,1},{8,10},{9,11},{10,... | collective-permute-start | bytes 393224 | tf_op jit(solution)/shard_map/ppermute | solution.py:234
  8.3 8.2 %collective-permute-done.3.down2 = f32[2,8,8,256]{3,2,1,0:T(8,128)S(1)} collective-permute-done((f32[2,8,8,256]{3,2,1,0:T(8,128)S(1)}, f32[2,8,8,256]{3,2,1,0:T(8,128)S(1)}, u32[]{:S(2)}, u32[]{:S(2)}) %collective-permute-start.3) | collective-permute-done | bytes 131104 | tf_op jit(solution)/shard_map/ppermute | solution.py:234
  16.5 0.0 collective-permute-done.1.up2
  16.5 0.0 collective-permute-done.up1
  16.5 0.0 collective-permute-done.2.down1
  16.5 11.7 %stream.2 = (f32[4,8,8,256]{3,2,1,0:T(8,128)S(1)}, f32[4,8,8,256]{3,2,1,0:T(8,128)S(1)}, f32[5,8,128]{2,1,0:T(8,128)S(1)}) custom-call(s32[1]{0:T(128)} %bitcast.vel_ref.refs_0_, f32[4,8,8,256]{3,2,1,0:T(8,128)S(1)} %bitcast.18, f32[4,8,8,256]{3,2,1,0:T(8,128)S(1)} %collective-permute-done.up1, f32[2,8,8,256]{3,2,1,0:T(8,128)S(1)} %collective-permute-done.1.up2, ...), custom_call_target="tpu_custom_call" | custom-call | tf_op jit(solution)/shard_map/stream/pallas_call | solution.py:198
  28.3 0.1 collective-permute-start.4
  28.4 1.2 %collective-permute-done.4 = f32[5,8,128]{2,1,0:T(8,128)S(1)} collective-permute-done((f32[5,8,128]{2,1,0:T(8,128)S(1)}, f32[5,8,128]{2,1,0:T(8,128)S(1)}, u32[]{:S(2)}, u32[]{:S(2)}) %collective-permute-start.4) | collective-permute-done | bytes 20512 | tf_op jit(solution)/shard_map/ppermute | solution.py:241
  29.6 0.8 collective-permute-start.5
  30.4 3.0 %collective-permute-done.5 = f32[5,8,128]{2,1,0:T(8,128)S(1)} collective-permute-done((f32[5,8,128]{2,1,0:T(8,128)S(1)}, f32[5,8,128]{2,1,0:T(8,128)S(1)}, u32[]{:S(2)}, u32[]{:S(2)}) %collective-permute-start.5) | collective-permute-done | bytes 20512 | tf_op jit(solution)/shard_map/ppermute | solution.py:241
  33.4 1.9 %collective-permute-start.6 = (f32[5,8,128]{2,1,0:T(8,128)S(1)}, f32[5,8,128]{2,1,0:T(8,128)S(1)}, u32[]{:S(2)}, u32[]{:S(2)}) collective-permute-start(f32[5,8,128]{2,1,0:T(8,128)S(1)} %add.31), channel_id=1, source_target_pairs={{0,32},{8,40},{16,48},{24,56},{32,0},{40,8},{48,16},{56,24},{64,96... | collective-permute-start | bytes 61448 | tf_op jit(solution)/shard_map/ppermute | solution.py:241
  35.3 1.9 %collective-permute-done.6 = f32[5,8,128]{2,1,0:T(8,128)S(1)} collective-permute-done((f32[5,8,128]{2,1,0:T(8,128)S(1)}, f32[5,8,128]{2,1,0:T(8,128)S(1)}, u32[]{:S(2)}, u32[]{:S(2)}) %collective-permute-start.6) | collective-permute-done | bytes 20512 | tf_op jit(solution)/shard_map/ppermute | solution.py:241
  37.2 3.3 %collective-permute-start.7 = (f32[5,8,128]{2,1,0:T(8,128)S(1)}, f32[5,8,128]{2,1,0:T(8,128)S(1)}, u32[]{:S(2)}, u32[]{:S(2)}) collective-permute-start(f32[5,8,128]{2,1,0:T(8,128)S(1)} %add.32), channel_id=1, source_target_pairs={{0,64},{8,72},{16,80},{24,88},{32,96},{40,104},{48,112},{56,120},{... | collective-permute-start | bytes 61448 | tf_op jit(solution)/shard_map/ppermute | solution.py:241
  40.4 1.8 %collective-permute-done.7 = f32[5,8,128]{2,1,0:T(8,128)S(1)} collective-permute-done((f32[5,8,128]{2,1,0:T(8,128)S(1)}, f32[5,8,128]{2,1,0:T(8,128)S(1)}, u32[]{:S(2)}, u32[]{:S(2)}) %collective-permute-start.7) | collective-permute-done | bytes 20512 | tf_op jit(solution)/shard_map/ppermute | solution.py:241
  42.2 6.8 %collective-permute-start.8 = (f32[5,8,128]{2,1,0:T(8,128)S(1)}, f32[5,8,128]{2,1,0:T(8,128)S(1)}, u32[]{:S(2)}, u32[]{:S(2)}) collective-permute-start(f32[5,8,128]{2,1,0:T(8,128)S(1)} %add.33), channel_id=1, source_target_pairs={{0,128},{8,136},{16,144},{24,152},{32,160},{40,168},{48,176},{56,1... | collective-permute-start | bytes 61448 | tf_op jit(solution)/shard_map/ppermute | solution.py:241
  49.0 1.8 %collective-permute-done.8 = f32[5,8,128]{2,1,0:T(8,128)S(1)} collective-permute-done((f32[5,8,128]{2,1,0:T(8,128)S(1)}, f32[5,8,128]{2,1,0:T(8,128)S(1)}, u32[]{:S(2)}, u32[]{:S(2)}) %collective-permute-start.8) | collective-permute-done | bytes 20512 | tf_op jit(solution)/shard_map/ppermute | solution.py:241
  50.8 0.1 relax.1
  50.9 2.0 %collective-permute-start.9 = (f32[4,8,8,256]{3,2,1,0:T(8,128)S(1)}, f32[4,8,8,256]{3,2,1,0:T(8,128)S(1)}, u32[]{:S(2)}, u32[]{:S(2)}) collective-permute-start(f32[4,8,8,256]{3,2,1,0:T(8,128)S(1)} %get-tuple-element.18.up0), channel_id=1, source_target_pairs={{0,1},{1,2},{2,3},{3,4},{4,5},{5,6},{6,7},{7,0},{8,9},{9,10},{10,1... | collective-permute-start | bytes 786440 | tf_op jit(solution)/shard_map/ppermute | solution.py:234
  52.9 1.6 %collective-permute-start.11 = (f32[4,8,8,256]{3,2,1,0:T(8,128)S(1)}, f32[4,8,8,256]{3,2,1,0:T(8,128)S(1)}, u32[]{:S(2)}, u32[]{:S(2)}) collective-permute-start(f32[4,8,8,256]{3,2,1,0:T(8,128)S(1)} %get-tuple-element.20.down0), channel_id=1, source_target_pairs={{0,7},{1,0},{2,1},{3,2},{4,3},{5,4},{6,5},{7,6},{8,15},{9,8},{10,9... | collective-permute-start | bytes 786440 | tf_op jit(solution)/shard_map/ppermute | solution.py:234
  54.6 1.1 %collective-permute-start.10 = (f32[2,8,8,256]{3,2,1,0:T(8,128)S(1)}, f32[2,8,8,256]{3,2,1,0:T(8,128)S(1)}, u32[]{:S(2)}, u32[]{:S(2)}) collective-permute-start(f32[2,8,8,256]{3,2,1,0:T(8,128)S(1)} %get-tuple-element.19), channel_id=1, source_target_pairs={{0,2},{1,3},{2,4},{3,5},{4,6},{5,7},{6,0},{7,1},{8,10},{9,11},{10,... | collective-permute-start | bytes 393224 | tf_op jit(solution)/shard_map/ppermute | solution.py:234
  55.6 1.0 collective-permute-start.12
  56.6 2.9 %collective-permute-done.10.up2 = f32[2,8,8,256]{3,2,1,0:T(8,128)S(1)} collective-permute-done((f32[2,8,8,256]{3,2,1,0:T(8,128)S(1)}, f32[2,8,8,256]{3,2,1,0:T(8,128)S(1)}, u32[]{:S(2)}, u32[]{:S(2)}) %collective-permute-start.10) | collective-permute-done | bytes 131104 | tf_op jit(solution)/shard_map/ppermute | solution.py:234
  59.5 5.0 %collective-permute-done.12.down2 = f32[2,8,8,256]{3,2,1,0:T(8,128)S(1)} collective-permute-done((f32[2,8,8,256]{3,2,1,0:T(8,128)S(1)}, f32[2,8,8,256]{3,2,1,0:T(8,128)S(1)}, u32[]{:S(2)}, u32[]{:S(2)}) %collective-permute-start.12) | collective-permute-done | bytes 131104 | tf_op jit(solution)/shard_map/ppermute | solution.py:234
  64.5 0.0 collective-permute-done.9.up1
  64.5 0.0 collective-permute-done.11.down1
  64.5 11.7 %stream.3 = (f32[4,8,8,256]{3,2,1,0:T(8,128)S(1)}, f32[4,8,8,256]{3,2,1,0:T(8,128)S(1)}, f32[5,8,128]{2,1,0:T(8,128)S(1)}) custom-call(s32[1]{0:T(128)} %bitcast.vel_ref.refs_0_, f32[4,8,8,256]{3,2,1,0:T(8,128)S(1)} %get-tuple-element.18.up0, f32[4,8,8,256]{3,2,1,0:T(8,128)S(1)} %collective-permute-done.9.up1, ...), custom_call_target="tpu_custom_call" | custom-call | tf_op jit(solution)/shard_map/stream/pallas_call | solution.py:198
  76.3 0.1 collective-permute-start.13
  76.4 1.2 %collective-permute-done.13 = f32[5,8,128]{2,1,0:T(8,128)S(1)} collective-permute-done((f32[5,8,128]{2,1,0:T(8,128)S(1)}, f32[5,8,128]{2,1,0:T(8,128)S(1)}, u32[]{:S(2)}, u32[]{:S(2)}) %collective-permute-start.13) | collective-permute-done | bytes 20512 | tf_op jit(solution)/shard_map/ppermute | solution.py:241
  77.6 0.4 collective-permute-start.14
  78.0 3.3 %collective-permute-done.14 = f32[5,8,128]{2,1,0:T(8,128)S(1)} collective-permute-done((f32[5,8,128]{2,1,0:T(8,128)S(1)}, f32[5,8,128]{2,1,0:T(8,128)S(1)}, u32[]{:S(2)}, u32[]{:S(2)}) %collective-permute-start.14) | collective-permute-done | bytes 20512 | tf_op jit(solution)/shard_map/ppermute | solution.py:241
  81.3 1.0 %collective-permute-start.15 = (f32[5,8,128]{2,1,0:T(8,128)S(1)}, f32[5,8,128]{2,1,0:T(8,128)S(1)}, u32[]{:S(2)}, u32[]{:S(2)}) collective-permute-start(f32[5,8,128]{2,1,0:T(8,128)S(1)} %add.36), channel_id=1, source_target_pairs={{0,32},{8,40},{16,48},{24,56},{32,0},{40,8},{48,16},{56,24},{64,96... | collective-permute-start | bytes 61448 | tf_op jit(solution)/shard_map/ppermute | solution.py:241
  82.4 2.8 %collective-permute-done.15 = f32[5,8,128]{2,1,0:T(8,128)S(1)} collective-permute-done((f32[5,8,128]{2,1,0:T(8,128)S(1)}, f32[5,8,128]{2,1,0:T(8,128)S(1)}, u32[]{:S(2)}, u32[]{:S(2)}) %collective-permute-start.15) | collective-permute-done | bytes 20512 | tf_op jit(solution)/shard_map/ppermute | solution.py:241
  85.1 1.9 %collective-permute-start.16 = (f32[5,8,128]{2,1,0:T(8,128)S(1)}, f32[5,8,128]{2,1,0:T(8,128)S(1)}, u32[]{:S(2)}, u32[]{:S(2)}) collective-permute-start(f32[5,8,128]{2,1,0:T(8,128)S(1)} %add.37), channel_id=1, source_target_pairs={{0,64},{8,72},{16,80},{24,88},{32,96},{40,104},{48,112},{56,120},{... | collective-permute-start | bytes 61448 | tf_op jit(solution)/shard_map/ppermute | solution.py:241
  87.0 2.8 %collective-permute-done.16 = f32[5,8,128]{2,1,0:T(8,128)S(1)} collective-permute-done((f32[5,8,128]{2,1,0:T(8,128)S(1)}, f32[5,8,128]{2,1,0:T(8,128)S(1)}, u32[]{:S(2)}, u32[]{:S(2)}) %collective-permute-start.16) | collective-permute-done | bytes 20512 | tf_op jit(solution)/shard_map/ppermute | solution.py:241
  89.8 5.7 %collective-permute-start.17 = (f32[5,8,128]{2,1,0:T(8,128)S(1)}, f32[5,8,128]{2,1,0:T(8,128)S(1)}, u32[]{:S(2)}, u32[]{:S(2)}) collective-permute-start(f32[5,8,128]{2,1,0:T(8,128)S(1)} %add.38), channel_id=1, source_target_pairs={{0,128},{8,136},{16,144},{24,152},{32,160},{40,168},{48,176},{56,1... | collective-permute-start | bytes 61448 | tf_op jit(solution)/shard_map/ppermute | solution.py:241
  95.5 2.2 %collective-permute-done.17 = f32[5,8,128]{2,1,0:T(8,128)S(1)} collective-permute-done((f32[5,8,128]{2,1,0:T(8,128)S(1)}, f32[5,8,128]{2,1,0:T(8,128)S(1)}, u32[]{:S(2)}, u32[]{:S(2)}) %collective-permute-start.17) | collective-permute-done | bytes 20512 | tf_op jit(solution)/shard_map/ppermute | solution.py:241
  97.7 0.1 relax_last.1
  97.9 1.1 %copy.6 = f32[128,4,256]{2,1,0:T(4,128)} copy(f32[128,4,256]{2,0,1:T(8,128)S(1)} %bitcast.15) | data formatting | bytes 1048576 | tf_op jit(solution)/shard_map/reshape | solution.py:260
  (12 shorter events, 0.1 us)
Async XLA Ops:
  1.1 15.4 %collective-permute-start = (f32[4,8,8,256]{3,2,1,0:T(8,128)S(1)}, f32[4,8,8,256]{3,2,1,0:T(8,128)S(1)}, u32[]{:S(2)}, u32[]{:S(2)}) collective-permute-start(f32[4,8,8,256]{3,2,1,0:T(8,128)S(1)} %bitcast.16), channel_id=1, source_target_pairs={{0,1},{1,2},{2,3},{3,4},{4,5},{5,6},{6,7},{7,0},{8,9},{9,10},{10,1... | collective-permute-start | bytes 786440 | tf_op jit(solution)/shard_map/ppermute | solution.py:234
  2.3 14.2 %collective-permute-start.2 = (f32[4,8,8,256]{3,2,1,0:T(8,128)S(1)}, f32[4,8,8,256]{3,2,1,0:T(8,128)S(1)}, u32[]{:S(2)}, u32[]{:S(2)}) collective-permute-start(f32[4,8,8,256]{3,2,1,0:T(8,128)S(1)} %bitcast.19), channel_id=1, source_target_pairs={{0,7},{1,0},{2,1},{3,2},{4,3},{5,4},{6,5},{7,6},{8,15},{9,8},{10,9... | collective-permute-start | bytes 786440 | tf_op jit(solution)/shard_map/ppermute | solution.py:234
  4.9 11.6 %collective-permute-start.3 = (f32[2,8,8,256]{3,2,1,0:T(8,128)S(1)}, f32[2,8,8,256]{3,2,1,0:T(8,128)S(1)}, u32[]{:S(2)}, u32[]{:S(2)}) collective-permute-start(f32[2,8,8,256]{3,2,1,0:T(8,128)S(1)} %slice.19), channel_id=1, source_target_pairs={{0,6},{1,7},{2,0},{3,1},{4,2},{5,3},{6,4},{7,5},{8,14},{9,15},{10,... | collective-permute-start | bytes 393224 | tf_op jit(solution)/shard_map/ppermute | solution.py:234
  5.7 10.8 %collective-permute-start.1 = (f32[2,8,8,256]{3,2,1,0:T(8,128)S(1)}, f32[2,8,8,256]{3,2,1,0:T(8,128)S(1)}, u32[]{:S(2)}, u32[]{:S(2)}) collective-permute-start(f32[2,8,8,256]{3,2,1,0:T(8,128)S(1)} %slice.17), channel_id=1, source_target_pairs={{0,2},{1,3},{2,4},{3,5},{4,6},{5,7},{6,0},{7,1},{8,10},{9,11},{10,... | collective-permute-start | bytes 393224 | tf_op jit(solution)/shard_map/ppermute | solution.py:234
  28.3 1.3 %collective-permute-start.4 = (f32[5,8,128]{2,1,0:T(8,128)S(1)}, f32[5,8,128]{2,1,0:T(8,128)S(1)}, u32[]{:S(2)}, u32[]{:S(2)}) collective-permute-start(f32[5,8,128]{2,1,0:T(8,128)S(1)} %get-tuple-element.15), channel_id=1, source_target_pairs={{0,8},{8,0},{16,24},{24,16},{32,40},{40,32},{48,56},{56,48},{64,72... | collective-permute-start | bytes 61448 | tf_op jit(solution)/shard_map/ppermute | solution.py:241
  29.6 3.8 %collective-permute-start.5 = (f32[5,8,128]{2,1,0:T(8,128)S(1)}, f32[5,8,128]{2,1,0:T(8,128)S(1)}, u32[]{:S(2)}, u32[]{:S(2)}) collective-permute-start(f32[5,8,128]{2,1,0:T(8,128)S(1)} %add.30), channel_id=1, source_target_pairs={{0,16},{8,24},{16,0},{24,8},{32,48},{40,56},{48,32},{56,40},{64,80... | collective-permute-start | bytes 61448 | tf_op jit(solution)/shard_map/ppermute | solution.py:241
  33.4 3.8 %collective-permute-start.6 = (f32[5,8,128]{2,1,0:T(8,128)S(1)}, f32[5,8,128]{2,1,0:T(8,128)S(1)}, u32[]{:S(2)}, u32[]{:S(2)}) collective-permute-start(f32[5,8,128]{2,1,0:T(8,128)S(1)} %add.31), channel_id=1, source_target_pairs={{0,32},{8,40},{16,48},{24,56},{32,0},{40,8},{48,16},{56,24},{64,96... | collective-permute-start | bytes 61448 | tf_op jit(solution)/shard_map/ppermute | solution.py:241
  37.2 5.0 %collective-permute-start.7 = (f32[5,8,128]{2,1,0:T(8,128)S(1)}, f32[5,8,128]{2,1,0:T(8,128)S(1)}, u32[]{:S(2)}, u32[]{:S(2)}) collective-permute-start(f32[5,8,128]{2,1,0:T(8,128)S(1)} %add.32), channel_id=1, source_target_pairs={{0,64},{8,72},{16,80},{24,88},{32,96},{40,104},{48,112},{56,120},{... | collective-permute-start | bytes 61448 | tf_op jit(solution)/shard_map/ppermute | solution.py:241
  42.2 8.6 %collective-permute-start.8 = (f32[5,8,128]{2,1,0:T(8,128)S(1)}, f32[5,8,128]{2,1,0:T(8,128)S(1)}, u32[]{:S(2)}, u32[]{:S(2)}) collective-permute-start(f32[5,8,128]{2,1,0:T(8,128)S(1)} %add.33), channel_id=1, source_target_pairs={{0,128},{8,136},{16,144},{24,152},{32,160},{40,168},{48,176},{56,1... | collective-permute-start | bytes 61448 | tf_op jit(solution)/shard_map/ppermute | solution.py:241
  50.9 13.6 %collective-permute-start.9 = (f32[4,8,8,256]{3,2,1,0:T(8,128)S(1)}, f32[4,8,8,256]{3,2,1,0:T(8,128)S(1)}, u32[]{:S(2)}, u32[]{:S(2)}) collective-permute-start(f32[4,8,8,256]{3,2,1,0:T(8,128)S(1)} %get-tuple-element.18.up0), channel_id=1, source_target_pairs={{0,1},{1,2},{2,3},{3,4},{4,5},{5,6},{6,7},{7,0},{8,9},{9,10},{10,1... | collective-permute-start | bytes 786440 | tf_op jit(solution)/shard_map/ppermute | solution.py:234
  52.9 11.6 %collective-permute-start.11 = (f32[4,8,8,256]{3,2,1,0:T(8,128)S(1)}, f32[4,8,8,256]{3,2,1,0:T(8,128)S(1)}, u32[]{:S(2)}, u32[]{:S(2)}) collective-permute-start(f32[4,8,8,256]{3,2,1,0:T(8,128)S(1)} %get-tuple-element.20.down0), channel_id=1, source_target_pairs={{0,7},{1,0},{2,1},{3,2},{4,3},{5,4},{6,5},{7,6},{8,15},{9,8},{10,9... | collective-permute-start | bytes 786440 | tf_op jit(solution)/shard_map/ppermute | solution.py:234
  54.6 5.0 %collective-permute-start.10 = (f32[2,8,8,256]{3,2,1,0:T(8,128)S(1)}, f32[2,8,8,256]{3,2,1,0:T(8,128)S(1)}, u32[]{:S(2)}, u32[]{:S(2)}) collective-permute-start(f32[2,8,8,256]{3,2,1,0:T(8,128)S(1)} %get-tuple-element.19), channel_id=1, source_target_pairs={{0,2},{1,3},{2,4},{3,5},{4,6},{5,7},{6,0},{7,1},{8,10},{9,11},{10,... | collective-permute-start | bytes 393224 | tf_op jit(solution)/shard_map/ppermute | solution.py:234
  55.6 8.9 %collective-permute-start.12 = (f32[2,8,8,256]{3,2,1,0:T(8,128)S(1)}, f32[2,8,8,256]{3,2,1,0:T(8,128)S(1)}, u32[]{:S(2)}, u32[]{:S(2)}) collective-permute-start(f32[2,8,8,256]{3,2,1,0:T(8,128)S(1)} %get-tuple-element.21), channel_id=1, source_target_pairs={{0,6},{1,7},{2,0},{3,1},{4,2},{5,3},{6,4},{7,5},{8,14},{9,15},{10,... | collective-permute-start | bytes 393224 | tf_op jit(solution)/shard_map/ppermute | solution.py:234
  76.3 1.3 %collective-permute-start.13 = (f32[5,8,128]{2,1,0:T(8,128)S(1)}, f32[5,8,128]{2,1,0:T(8,128)S(1)}, u32[]{:S(2)}, u32[]{:S(2)}) collective-permute-start(f32[5,8,128]{2,1,0:T(8,128)S(1)} %get-tuple-element.22), channel_id=1, source_target_pairs={{0,8},{8,0},{16,24},{24,16},{32,40},{40,32},{48,56},{56,48},{64,72... | collective-permute-start | bytes 61448 | tf_op jit(solution)/shard_map/ppermute | solution.py:241
  77.6 3.8 %collective-permute-start.14 = (f32[5,8,128]{2,1,0:T(8,128)S(1)}, f32[5,8,128]{2,1,0:T(8,128)S(1)}, u32[]{:S(2)}, u32[]{:S(2)}) collective-permute-start(f32[5,8,128]{2,1,0:T(8,128)S(1)} %add.35), channel_id=1, source_target_pairs={{0,16},{8,24},{16,0},{24,8},{32,48},{40,56},{48,32},{56,40},{64,80... | collective-permute-start | bytes 61448 | tf_op jit(solution)/shard_map/ppermute | solution.py:241
  81.3 3.8 %collective-permute-start.15 = (f32[5,8,128]{2,1,0:T(8,128)S(1)}, f32[5,8,128]{2,1,0:T(8,128)S(1)}, u32[]{:S(2)}, u32[]{:S(2)}) collective-permute-start(f32[5,8,128]{2,1,0:T(8,128)S(1)} %add.36), channel_id=1, source_target_pairs={{0,32},{8,40},{16,48},{24,56},{32,0},{40,8},{48,16},{56,24},{64,96... | collective-permute-start | bytes 61448 | tf_op jit(solution)/shard_map/ppermute | solution.py:241
  85.1 4.7 %collective-permute-start.16 = (f32[5,8,128]{2,1,0:T(8,128)S(1)}, f32[5,8,128]{2,1,0:T(8,128)S(1)}, u32[]{:S(2)}, u32[]{:S(2)}) collective-permute-start(f32[5,8,128]{2,1,0:T(8,128)S(1)} %add.37), channel_id=1, source_target_pairs={{0,64},{8,72},{16,80},{24,88},{32,96},{40,104},{48,112},{56,120},{... | collective-permute-start | bytes 61448 | tf_op jit(solution)/shard_map/ppermute | solution.py:241
  89.8 7.9 %collective-permute-start.17 = (f32[5,8,128]{2,1,0:T(8,128)S(1)}, f32[5,8,128]{2,1,0:T(8,128)S(1)}, u32[]{:S(2)}, u32[]{:S(2)}) collective-permute-start(f32[5,8,128]{2,1,0:T(8,128)S(1)} %add.38), channel_id=1, source_target_pairs={{0,128},{8,136},{16,144},{24,152},{32,160},{40,168},{48,176},{56,1... | collective-permute-start | bytes 61448 | tf_op jit(solution)/shard_map/ppermute | solution.py:241

commit v2 on v0

v2 whole, which is shorter than its diff:
```python
import math

import jax
import jax.numpy as jnp
from jax import lax
from jax.experimental import pallas as pl
from jax.experimental.pallas import tpu as pltpu
from jax.sharding import PartitionSpec as P

NV1 = 16
COLLISIONS = 2

speed_limit = 4.0
time_step = 0.05
knudsen = 0.0125
spacing = 2.0 * speed_limit / (NV1 - 1)
weight = spacing**3 / (2.0 * math.pi) ** 1.5

PLANES = 4
NY = 16
CZ = 8
CX = 8
COUNT = 2 * CX * CZ
LANES = 128
TILE = (8, LANES)
ROWS = PLANES * NY
SPLIT = (PLANES, 2, COUNT, LANES)


def point(index):
    return -speed_limit + spacing * index.astype(jnp.float32)


def iota(dim):
    return lax.broadcasted_iota(jnp.int32, TILE, dim)


def cx_lanes(half):
    return point(half * CX + iota(1) % 8)


class Device:
    def __init__(self, vel):
        zhalf = vel % 2
        self.ypos = vel // 2 >= NV1 // 2
        self.zpos = zhalf == 1
        self.cy = point(vel // 2)
        self.cz = point(zhalf * CZ + iota(0))

    def row(self, plane, y):
        return plane * NY + jnp.where(self.ypos, y, NY - 1 - y)

    def base(self, yhalf):
        return jnp.where(self.ypos, yhalf, 1 - yhalf) * 8

    def mirror_z(self, tile):
        lane = iota(1)
        source = jnp.where(self.zpos, lane, (15 - lane // 8) * 8 + lane % 8)
        return permuted(tile, source)


def permuted(tile, source):
    return jnp.take_along_axis(tile, source, axis=1, mode="promise_in_bounds")


def swapped(tiles):
    tiles = list(tiles)
    lane = iota(1)
    for w in (1, 2, 4):
        high = (lane // w) % 2 == 1
        for i in range(8):
            if not i & w:
                a, b = tiles[i], tiles[i + w]
                tiles[i] = jnp.where(high, pltpu.roll(b, w, 1), a)
                tiles[i + w] = jnp.where(high, b, pltpu.roll(a, LANES - w, 1))
    return tiles


def pack_kernel(vel_ref, in_ref, up_out, down_out, split):
    device = Device(vel_ref[0])
    lane = iota(1)
    y, z = lane % 8, lane // 8
    source = jnp.where(device.ypos, y, 7 - y) * 16 + jnp.where(device.zpos, z, 15 - z)
    for plane in range(PLANES):
        for yhalf in (0, 1):
            split[plane, yhalf] = in_ref[plane, :, yhalf * LANES : (yhalf + 1) * LANES]
    for plane in range(PLANES):
        for yhalf in (0, 1):
            base = device.base(yhalf)
            for half, out in ((0, down_out), (1, up_out)):
                tiles = []
                for ix in range(CX):
                    rows = pl.ds(half * CX + ix, CZ, stride=2 * CX)
                    tiles.append(permuted(split[plane, yhalf, rows, :], source))
                for j, tile in enumerate(swapped(tiles)):
                    out[plane, base + j] = tile


def stream_kernel(vel_ref, up0, up1, up2, down0, down1, down2, up_out, down_out, mom_out, *scratch):
    first, second, sums = scratch
    device = Device(vel_ref[0])
    ay = time_step * jnp.abs(device.cy)
    az = time_step * jnp.abs(device.cz)

    for half in (0, 1):
        if half:
            field = [(up2, 0), (up2, 1)] + [(up1, p) for p in range(PLANES)]
            field += [(up0, p) for p in range(PLANES)]
            result = [(up_out, p) for p in range(PLANES)]
        else:
            field = [(down2, 1), (down2, 0)] + [(down1, p) for p in reversed(range(PLANES))]
            field += [(down0, p) for p in reversed(range(PLANES))]
            result = [(down_out, p) for p in reversed(range(PLANES))]
        ax = time_step * jnp.abs(cx_lanes(half))
        stages = [
            (field, [(first, p) for p in range(8)], 1.0 / 6.0, 0.0),
            ([(first, p) for p in range(8)], [(second, p) for p in range(6)], 1.0, 0.5),
            ([(second, p) for p in range(6)], result, 1.0, 1.0 / 3.0),
        ]
        for source, target, scale, part in stages:
            keep = scale * (1.0 - 1.5 * (ax + (ay + az)))
            x1, x2 = (2.0 * scale) * ax, (0.5 * scale) * ax
            y1, y2 = (2.0 * scale) * ay, (0.5 * scale) * ay
            z1, z2 = (2.0 * scale) * az, (0.5 * scale) * az
            for p, (out, plane) in enumerate(target):
                now = [source[p + 2][0][source[p + 2][1], y] for y in range(NY)]
                one, one_plane = source[p + 1]
                two, two_plane = source[p]
                start, start_plane = field[p + 10 - len(target)]
                for y in range(NY):
                    along_x = x1 * one[one_plane, y] - x2 * two[two_plane, y]
                    along_y = y1 * now[y - 1] - y2 * now[y - 2]
                    along_z = z1 * pltpu.roll(now[y], 8, 1) - z2 * pltpu.roll(now[y], 16, 1)
                    value = keep * now[y] + (along_x + (along_y + along_z))
                    if part:
                        value += part * start[start_plane, y]
                    out[plane, y] = value

    down_cx, up_cx = cx_lanes(0), cx_lanes(1)
    square = device.cy * device.cy + device.cz * device.cz
    down_square, up_square = square + down_cx * down_cx, square + up_cx * up_cx
    for plane in range(PLANES):
        for y in range(NY):
            down, up = down_out[plane, y], up_out[plane, y]
            both = down + up
            terms = (
                both,
                down_cx * down + up_cx * up,
                device.cz * both,
                down_square * down + up_square * up,
            )
            row = device.row(plane, y)
            for which, term in enumerate(terms):
                sums[which, pl.ds(row, 1), :] = jnp.sum(term, axis=0, keepdims=True)
    slot = iota(1) % 8
    for which, place in ((0, 0), (1, 1), (2, 3), (3, 4)):
        packed = jnp.zeros(TILE, jnp.float32)
        for j in range(8):
            tile = sums[which, 8 * j : 8 * j + 8, :]
            for w in (1, 2, 4):
                tile += pltpu.roll(tile, LANES - w, 1)
            packed = jnp.where(slot == j, pltpu.roll(tile, j, 1) if j else tile, packed)
        packed = weight * device.mirror_z(packed)
        mom_out[place] = packed
        if which == 0:
            mom_out[2] = device.cy * packed


def relax_kernel(last, vel_ref, mom_ref, up_in, down_in, *outs_and_scratch):
    *outs, rows, split = outs_and_scratch
    device = Device(vel_ref[0])
    rho = mom_ref[0]
    ux = mom_ref[1] / rho
    uy = mom_ref[2] / rho
    uz = mom_ref[3] / rho
    temp = (mom_ref[4] / rho - (ux * ux + uy * uy + uz * uz)) / 3.0
    minus_half = -0.5 / temp

    def factor(c, u, scale):
        return jnp.exp((c - u) * (c - u) * scale)

    def total(u):
        out = jnp.zeros_like(u)
        for i in range(NV1):
            out += factor(-speed_limit + spacing * i, u, minus_half)
        return out

    root = jnp.sqrt(temp)
    peak = rho / (temp * root)
    mass = weight * peak * total(ux) * total(uy) * total(uz)
    nu = time_step * rho * root / knudsen
    shrink = 1.0 / (1.0 + nu)
    common = nu * shrink * peak * (rho / mass) * factor(device.cy, uy, minus_half)

    slot = iota(1) % 8
    packed = [device.mirror_z(tile) for tile in (shrink, minus_half, uz, common, ux)]
    for j in range(8):
        spread = []
        for tile in packed:
            tile = jnp.where(slot == 0, pltpu.roll(tile, LANES - j, 1) if j else tile, 0.0)
            for w in (1, 2, 4):
                tile += pltpu.roll(tile, w, 1)
            spread.append(tile)
        keep, scale, drift_z, gain, drift_x = spread
        cells = slice(8 * j, 8 * j + 8)
        rows[0, cells, :] = keep
        rows[1, cells, :] = scale
        rows[2, cells, :] = drift_z
        for half in (0, 1):
            rows[3 + half, cells, :] = gain * factor(cx_lanes(half), drift_x, scale)

    lane = iota(1)
    y_lane, z_lane = lane // 16, lane % 16
    back = jnp.where(device.zpos, z_lane, 15 - z_lane) * 8 + jnp.where(device.ypos, y_lane, 7 - y_lane)
    for plane in range(PLANES):
        for yhalf in (0, 1):
            base = device.base(yhalf) if last else yhalf * 8
            values = ([], [])
            for j in range(8):
                y = base + j
                row = device.row(plane, y)
                keep, scale, drift_z, *gains = (
                    jnp.broadcast_to(rows[k, pl.ds(row, 1), :], TILE) for k in range(5)
                )
                along_z = factor(device.cz, drift_z, scale)
                for half, ref in ((0, down_in), (1, up_in)):
                    value = ref[plane, y] * keep + along_z * gains[half]
                    if last:
                        values[half].append(value)
                        continue
                    outs[half][plane, y] = value
                    if half == 0 and plane < 2:
                        outs[2][plane, y] = value
                    if half == 1 and plane >= 2:
                        outs[3][plane - 2, y] = value
            if last:
                for half in (0, 1):
                    for ix, tile in enumerate(swapped(values[half])):
                        where = pl.ds(half * CX + ix, CZ, stride=2 * CX)
                        split[plane, yhalf, where, :] = permuted(tile, back)
    if last:
        for plane in range(PLANES):
            for yhalf in (0, 1):
                outs[0][plane, :, yhalf * LANES : (yhalf + 1) * LANES] = split[plane, yhalf]


def vmem():
    return pl.BlockSpec(memory_space=pltpu.VMEM)


def smem():
    return pl.BlockSpec(memory_space=pltpu.SMEM)


def shape(*sizes):
    return jax.ShapeDtypeStruct(sizes, jnp.float32)


def call(body, name, out_shape, scratch, vel, *operands):
    return pl.pallas_call(
        body,
        in_specs=[smem()] + [vmem()] * len(operands),
        out_specs=[vmem()] * len(out_shape),
        out_shape=out_shape,
        scratch_shapes=[pltpu.VMEM(sizes, jnp.float32) for sizes in scratch],
        compiler_params=pltpu.CompilerParams(vmem_limit_bytes=8 << 20),
        name=name,
    )(vel, *operands)


def planes(count):
    return (count, NY, CZ, LANES)


def pack(vel, field):
    return call(pack_kernel, "pack", [shape(*planes(PLANES))] * 2, [SPLIT], vel, field)


def stream(vel, up, down):
    return call(
        stream_kernel,
        "stream",
        [shape(*planes(PLANES))] * 2 + [shape(5, *TILE)],
        [planes(8), planes(6), (4, ROWS, LANES)],
        vel,
        *up,
        *down,
    )


def relax(vel, moments, up, down, last):
    if last:
        out_shape = [shape(PLANES, COUNT, 2 * LANES)]
    else:
        out_shape = [shape(*planes(PLANES))] * 2 + [shape(*planes(2))] * 2

    def body(*refs):
        relax_kernel(last, *refs)

    name = "relax_last" if last else "relax"
    return call(body, name, out_shape, [(5, ROWS, LANES), SPLIT], vel, moments, up, down)


def passed_along(value, by):
    size = lax.axis_size("gx")
    return lax.ppermute(value, "gx", [(i, (i + by) % size) for i in range(size)])


def swapped_over(value, partner):
    size = lax.axis_size("vel")
    return lax.ppermute(value, "vel", [(i, partner(i)) for i in range(size)])


def summed_over_velocities(value):
    value = value + sum(swapped_over(value, lambda i, k=k: i ^ k) for k in (1, 2, 3))
    rounds = (
        lambda c: c ^ 1,
        lambda c: (c + 1) % 8 if c % 2 else (c - 1) % 8,
        lambda c: (3, 6, 5, 0, 7, 2, 1, 4)[c],
    )
    for chip in rounds:
        value = value + swapped_over(value, lambda i: 4 * chip(i // 4) + i % 4)
    return value


def on_device(distribution):
    vel = lax.axis_index("vel").astype(jnp.int32).reshape(1)
    up, down = pack(vel, distribution.transpose(1, 0, 2))
    up_far, down_far = up[2:], down[:2]
    for step in range(COLLISIONS):
        ups = (up, passed_along(up, 1), passed_along(up_far, 2))
        downs = (down, passed_along(down, -1), passed_along(down_far, -2))
        up_read, down_read, moments = stream(vel, ups, downs)
        moments = summed_over_velocities(moments)
        outs = relax(vel, moments, up_read, down_read, step == COLLISIONS - 1)
        if step < COLLISIONS - 1:
            down, up, down_far, up_far = outs
    return outs[0].transpose(1, 0, 2)


def solution(mesh):
    return jax.shard_map(
        on_device,
        mesh=mesh,
        in_specs=(P("vel", "gx", None),),
        out_specs=P("vel", "gx", None),
        check_vma=False,
    )
```

time: 113 us -> 80.5 us (0.71)
  Pallas kernels: 31.3 us -> 8.54 us
  local copies, waits for them, and re-layouts: 5.72 us -> 2.3 us
  starting transfers between devices: 34.6 us -> 31.4 us
  other arithmetic: 2.7 us -> 0.04 us
    pallas_call x4 -> x5, Pallas kernels: 31.3 us -> 8.54 us  [call(): pl.pallas_call(body, in_specs=[smem()] + [vmem()] * len(operands), out_sp...]
    ppermute x10 -> x12, starting transfers between devices: 21.9 us -> 18.8 us  [swapped_over(): return lax.ppermute(value, 'vel', [(i, partner(i)) for i in range(size)])]
    add x10 -> x8, other arithmetic: 2.7 us -> 0.04 us  [the longest x6 0.03 us: summed_over_velocities(): value = value + swapped_over(value, lambda i: 4 * chip(i // 4) + i % 4)]
    reshape x1 -> x0, local copies, waits for them, and re-layouts: 2.17 us -> none  [on_device(): return outs[0].transpose(1, 2, 3, 0, 4).reshape(distribution.shape)]
    unnamed x22 -> x1, local copies, waits for them, and re-layouts: 2.46 us -> 1.14 us
    transpose x0 -> x1, local copies, waits for them, and re-layouts: none -> 1.13 us  [on_device(): return outs[0].transpose(1, 0, 2)]
    ppermute x10 -> x12, waiting for transfers between devices: 22.2 us -> 21.1 us  [swapped_over(): return lax.ppermute(value, 'vel', [(i, partner(i)) for i in range(size)])]
  transfers between devices with their start and end apart: 18 -> 20, of which waited for: 13 -> 13; matrix products, arithmetic and copies ran while one was open for 0% -> 0% of each run, Pallas kernels for 0% -> 0%
where the time goes in v2:
time: 80.5 us; the launch traced here: 79.9 us
  waiting for transfers between devices  37.5 us (47%)
  starting transfers between devices  31.4 us (39%)
  Pallas kernels  8.54 us (11%)
  local copies, waits for them, and re-layouts  2.3 us (3%)
    ppermute x12, waiting for transfers between devices, swapped_over(): return lax.ppermute(value, 'vel', [(i, partner(i)) for i in range(size)])  21.1 us
    ppermute x12, starting transfers between devices, swapped_over(): return lax.ppermute(value, 'vel', [(i, partner(i)) for i in range(size)])  18.8 us
    ppermute x8, waiting for transfers between devices, passed_along(): lax.ppermute(value, 'gx', [(i, (i + by) % size) for i in range(size)])  16.4 us
    ppermute x8, starting transfers between devices, passed_along(): lax.ppermute(value, 'gx', [(i, (i + by) % size) for i in range(size)])  12.6 us
    pallas_call x5, Pallas kernels, call(): pl.pallas_call(body, in_specs=[smem()] + [vmem()] * len(operands), out_sp...  8.54 us
  transfers between devices with their start and end apart: 20, of which 13 were waited for; matrix products, arithmetic and copies ran while one was open for 0% of the time, Pallas kernels for 0%

profile of v2, /device:TPU:30, one launch (start us, length us, event | category | flops | bytes accessed | tf_op | source)
XLA Modules:
  0.0 79.9 jit_solution(1046422971638960455)
XLA Ops:
  0.0 1.1 %copy.5 = f32[128,4,256]{2,0,1:T(8,128)S(1)} copy(f32[128,4,256]{2,1,0:T(4,128)} %param.1) | data formatting | bytes 1048576 | tf_op args[0]
  1.1 2.1 %pack.1 = (f32[4,16,8,128]{3,2,1,0:T(8,128)S(1)}, f32[4,16,8,128]{3,2,1,0:T(8,128)S(1)}) custom-call(s32[1]{0:T(128)} %bitcast.vel_ref.refs_0_, f32[4,128,256]{2,1,0:T(8,128)S(1)} %bitcast.6), custom_call_target="tpu_custom_call" | custom-call | tf_op jit(solution)/shard_map/pack/pallas_call | solution.py:260
  3.2 1.1 %collective-permute-start = (f32[4,16,8,128]{3,2,1,0:T(8,128)S(1)}, f32[4,16,8,128]{3,2,1,0:T(8,128)S(1)}, u32[]{:S(2)}, u32[]{:S(2)}) collective-permute-start(f32[4,16,8,128]{3,2,1,0:T(8,128)S(1)} %get-tuple-element.17.up0), channel_id=1, source_target_pairs={{0,1},{1,2},{2,3},{3,4},{4,5},{5,6},{6,7},{7,0},{8,9},{9,10},{10,1... | collective-permute-start | bytes 786440 | tf_op jit(solution)/shard_map/ppermute | solution.py:306
  4.4 2.5 %collective-permute-start.2 = (f32[4,16,8,128]{3,2,1,0:T(8,128)S(1)}, f32[4,16,8,128]{3,2,1,0:T(8,128)S(1)}, u32[]{:S(2)}, u32[]{:S(2)}) collective-permute-start(f32[4,16,8,128]{3,2,1,0:T(8,128)S(1)} %get-tuple-element.18.down0), channel_id=1, source_target_pairs={{0,7},{1,0},{2,1},{3,2},{4,3},{5,4},{6,5},{7,6},{8,15},{9,8},{10,9... | collective-permute-start | bytes 786440 | tf_op jit(solution)/shard_map/ppermute | solution.py:306
  6.9 0.8 %collective-permute-start.3 = (f32[2,16,8,128]{3,2,1,0:T(8,128)S(1)}, f32[2,16,8,128]{3,2,1,0:T(8,128)S(1)}, u32[]{:S(2)}, u32[]{:S(2)}) collective-permute-start(f32[2,16,8,128]{3,2,1,0:T(8,128)S(1)} %slice.7), channel_id=1, source_target_pairs={{0,6},{1,7},{2,0},{3,1},{4,2},{5,3},{6,4},{7,5},{8,14},{9,15},{10,... | collective-permute-start | bytes 393224 | tf_op jit(solution)/shard_map/ppermute | solution.py:306
  7.7 2.6 %collective-permute-start.1 = (f32[2,16,8,128]{3,2,1,0:T(8,128)S(1)}, f32[2,16,8,128]{3,2,1,0:T(8,128)S(1)}, u32[]{:S(2)}, u32[]{:S(2)}) collective-permute-start(f32[2,16,8,128]{3,2,1,0:T(8,128)S(1)} %slice.6), channel_id=1, source_target_pairs={{0,2},{1,3},{2,4},{3,5},{4,6},{5,7},{6,0},{7,1},{8,10},{9,11},{10,... | collective-permute-start | bytes 393224 | tf_op jit(solution)/shard_map/ppermute | solution.py:306
  10.3 8.3 %collective-permute-done.3.down2 = f32[2,16,8,128]{3,2,1,0:T(8,128)S(1)} collective-permute-done((f32[2,16,8,128]{3,2,1,0:T(8,128)S(1)}, f32[2,16,8,128]{3,2,1,0:T(8,128)S(1)}, u32[]{:S(2)}, u32[]{:S(2)}) %collective-permute-start.3) | collective-permute-done | bytes 131104 | tf_op jit(solution)/shard_map/ppermute | solution.py:306
  18.6 0.0 collective-permute-done.1.up2
  18.6 0.0 collective-permute-done.up1
  18.6 0.0 collective-permute-done.2.down1
  18.6 2.3 %stream.2 = (f32[4,16,8,128]{3,2,1,0:T(8,128)S(1)}, f32[4,16,8,128]{3,2,1,0:T(8,128)S(1)}, f32[5,8,128]{2,1,0:T(8,128)S(1)}) custom-call(s32[1]{0:T(128)} %bitcast.vel_ref.refs_0_, f32[4,16,8,128]{3,2,1,0:T(8,128)S(1)} %get-tuple-element.17.up0, f32[4,16,8,128]{3,2,1,0:T(8,128)S(1)} %collective-permute-done.up1, ...), custom_call_target="tpu_custom_call" | custom-call | tf_op jit(solution)/shard_map/stream/pallas_call | solution.py:260
  20.9 0.0 collective-permute-start.6
  20.9 0.9 %collective-permute-start.5 = (f32[5,8,128]{2,1,0:T(8,128)S(1)}, f32[5,8,128]{2,1,0:T(8,128)S(1)}, u32[]{:S(2)}, u32[]{:S(2)}) collective-permute-start(f32[5,8,128]{2,1,0:T(8,128)S(1)} %get-tuple-element.19), channel_id=1, source_target_pairs={{0,16},{8,24},{16,0},{24,8},{32,48},{40,56},{48,32},{56,40},{64,80... | collective-permute-start | bytes 61448 | tf_op jit(solution)/shard_map/ppermute | solution.py:311
  21.8 0.9 %collective-permute-start.4 = (f32[5,8,128]{2,1,0:T(8,128)S(1)}, f32[5,8,128]{2,1,0:T(8,128)S(1)}, u32[]{:S(2)}, u32[]{:S(2)}) collective-permute-start(f32[5,8,128]{2,1,0:T(8,128)S(1)} %get-tuple-element.19), channel_id=1, source_target_pairs={{0,8},{8,0},{16,24},{24,16},{32,40},{40,32},{48,56},{56,48},{64,72... | collective-permute-start | bytes 61448 | tf_op jit(solution)/shard_map/ppermute | solution.py:311
  22.8 1.3 %collective-permute-done.6 = f32[5,8,128]{2,1,0:T(8,128)S(1)} collective-permute-done((f32[5,8,128]{2,1,0:T(8,128)S(1)}, f32[5,8,128]{2,1,0:T(8,128)S(1)}, u32[]{:S(2)}, u32[]{:S(2)}) %collective-permute-start.6) | collective-permute-done | bytes 20512 | tf_op jit(solution)/shard_map/ppermute | solution.py:311
  24.1 0.8 collective-permute-done.5
  24.9 0.0 collective-permute-done.4
  24.9 2.0 %collective-permute-start.7 = (f32[5,8,128]{2,1,0:T(8,128)S(1)}, f32[5,8,128]{2,1,0:T(8,128)S(1)}, u32[]{:S(2)}, u32[]{:S(2)}) collective-permute-start(f32[5,8,128]{2,1,0:T(8,128)S(1)} %add_add_fusion.1), channel_id=1, source_target_pairs={{0,32},{8,40},{16,48},{24,56},{32,0},{40,8},{48,16},{56,24},{64,96... | collective-permute-start | bytes 61448 | tf_op jit(solution)/shard_map/ppermute | solution.py:311
  26.9 1.9 %collective-permute-done.7 = f32[5,8,128]{2,1,0:T(8,128)S(1)} collective-permute-done((f32[5,8,128]{2,1,0:T(8,128)S(1)}, f32[5,8,128]{2,1,0:T(8,128)S(1)}, u32[]{:S(2)}, u32[]{:S(2)}) %collective-permute-start.7) | collective-permute-done | bytes 20512 | tf_op jit(solution)/shard_map/ppermute | solution.py:311
  28.8 5.9 %collective-permute-start.8 = (f32[5,8,128]{2,1,0:T(8,128)S(1)}, f32[5,8,128]{2,1,0:T(8,128)S(1)}, u32[]{:S(2)}, u32[]{:S(2)}) collective-permute-start(f32[5,8,128]{2,1,0:T(8,128)S(1)} %add.39), channel_id=1, source_target_pairs={{0,224},{8,232},{16,240},{24,248},{32,64},{40,72},{48,80},{56,88},... | collective-permute-start | bytes 61448 | tf_op jit(solution)/shard_map/ppermute | solution.py:311
  34.6 1.8 %collective-permute-done.8 = f32[5,8,128]{2,1,0:T(8,128)S(1)} collective-permute-done((f32[5,8,128]{2,1,0:T(8,128)S(1)}, f32[5,8,128]{2,1,0:T(8,128)S(1)}, u32[]{:S(2)}, u32[]{:S(2)}) %collective-permute-start.8) | collective-permute-done | bytes 20512 | tf_op jit(solution)/shard_map/ppermute | solution.py:311
  36.4 2.0 %collective-permute-start.9 = (f32[5,8,128]{2,1,0:T(8,128)S(1)}, f32[5,8,128]{2,1,0:T(8,128)S(1)}, u32[]{:S(2)}, u32[]{:S(2)}) collective-permute-start(f32[5,8,128]{2,1,0:T(8,128)S(1)} %add.40), channel_id=1, source_target_pairs={{0,96},{8,104},{16,112},{24,120},{32,192},{40,200},{48,208},{56,21... | collective-permute-start | bytes 61448 | tf_op jit(solution)/shard_map/ppermute | solution.py:311
  38.4 3.8 %collective-permute-done.9 = f32[5,8,128]{2,1,0:T(8,128)S(1)} collective-permute-done((f32[5,8,128]{2,1,0:T(8,128)S(1)}, f32[5,8,128]{2,1,0:T(8,128)S(1)}, u32[]{:S(2)}, u32[]{:S(2)}) %collective-permute-start.9) | collective-permute-done | bytes 20512 | tf_op jit(solution)/shard_map/ppermute | solution.py:311
  42.2 0.6 relax.1
  42.8 1.9 %collective-permute-start.10 = (f32[4,16,8,128]{3,2,1,0:T(8,128)S(1)}, f32[4,16,8,128]{3,2,1,0:T(8,128)S(1)}, u32[]{:S(2)}, u32[]{:S(2)}) collective-permute-start(f32[4,16,8,128]{3,2,1,0:T(8,128)S(1)} %get-tuple-element.22.up0), channel_id=1, source_target_pairs={{0,1},{1,2},{2,3},{3,4},{4,5},{5,6},{6,7},{7,0},{8,9},{9,10},{10,1... | collective-permute-start | bytes 786440 | tf_op jit(solution)/shard_map/ppermute | solution.py:306
  44.7 1.7 %collective-permute-start.12 = (f32[4,16,8,128]{3,2,1,0:T(8,128)S(1)}, f32[4,16,8,128]{3,2,1,0:T(8,128)S(1)}, u32[]{:S(2)}, u32[]{:S(2)}) collective-permute-start(f32[4,16,8,128]{3,2,1,0:T(8,128)S(1)} %get-tuple-element.24.down0), channel_id=1, source_target_pairs={{0,7},{1,0},{2,1},{3,2},{4,3},{5,4},{6,5},{7,6},{8,15},{9,8},{10,9... | collective-permute-start | bytes 786440 | tf_op jit(solution)/shard_map/ppermute | solution.py:306
  46.4 1.1 %collective-permute-start.11 = (f32[2,16,8,128]{3,2,1,0:T(8,128)S(1)}, f32[2,16,8,128]{3,2,1,0:T(8,128)S(1)}, u32[]{:S(2)}, u32[]{:S(2)}) collective-permute-start(f32[2,16,8,128]{3,2,1,0:T(8,128)S(1)} %get-tuple-element.23), channel_id=1, source_target_pairs={{0,2},{1,3},{2,4},{3,5},{4,6},{5,7},{6,0},{7,1},{8,10},{9,11},{10,... | collective-permute-start | bytes 393224 | tf_op jit(solution)/shard_map/ppermute | solution.py:306
  47.5 0.9 %collective-permute-start.13 = (f32[2,16,8,128]{3,2,1,0:T(8,128)S(1)}, f32[2,16,8,128]{3,2,1,0:T(8,128)S(1)}, u32[]{:S(2)}, u32[]{:S(2)}) collective-permute-start(f32[2,16,8,128]{3,2,1,0:T(8,128)S(1)} %get-tuple-element.25), channel_id=1, source_target_pairs={{0,6},{1,7},{2,0},{3,1},{4,2},{5,3},{6,4},{7,5},{8,14},{9,15},{10,... | collective-permute-start | bytes 393224 | tf_op jit(solution)/shard_map/ppermute | solution.py:306
  48.4 2.9 %collective-permute-done.11.up2 = f32[2,16,8,128]{3,2,1,0:T(8,128)S(1)} collective-permute-done((f32[2,16,8,128]{3,2,1,0:T(8,128)S(1)}, f32[2,16,8,128]{3,2,1,0:T(8,128)S(1)}, u32[]{:S(2)}, u32[]{:S(2)}) %collective-permute-start.11) | collective-permute-done | bytes 131104 | tf_op jit(solution)/shard_map/ppermute | solution.py:306
  51.4 5.1 %collective-permute-done.13.down2 = f32[2,16,8,128]{3,2,1,0:T(8,128)S(1)} collective-permute-done((f32[2,16,8,128]{3,2,1,0:T(8,128)S(1)}, f32[2,16,8,128]{3,2,1,0:T(8,128)S(1)}, u32[]{:S(2)}, u32[]{:S(2)}) %collective-permute-start.13) | collective-permute-done | bytes 131104 | tf_op jit(solution)/shard_map/ppermute | solution.py:306
  56.5 0.0 collective-permute-done.10.up1
  56.5 0.0 collective-permute-done.12.down1
  56.5 2.3 %stream.3 = (f32[4,16,8,128]{3,2,1,0:T(8,128)S(1)}, f32[4,16,8,128]{3,2,1,0:T(8,128)S(1)}, f32[5,8,128]{2,1,0:T(8,128)S(1)}) custom-call(s32[1]{0:T(128)} %bitcast.vel_ref.refs_0_, f32[4,16,8,128]{3,2,1,0:T(8,128)S(1)} %get-tuple-element.22.up0, f32[4,16,8,128]{3,2,1,0:T(8,128)S(1)} %collective-permute-done.10.up1, ...), custom_call_target="tpu_custom_call" | custom-call | tf_op jit(solution)/shard_map/stream/pallas_call | solution.py:260
  58.8 0.0 collective-permute-start.16
  58.9 0.8 %collective-permute-start.15 = (f32[5,8,128]{2,1,0:T(8,128)S(1)}, f32[5,8,128]{2,1,0:T(8,128)S(1)}, u32[]{:S(2)}, u32[]{:S(2)}) collective-permute-start(f32[5,8,128]{2,1,0:T(8,128)S(1)} %get-tuple-element.26), channel_id=1, source_target_pairs={{0,16},{8,24},{16,0},{24,8},{32,48},{40,56},{48,32},{56,40},{64,80... | collective-permute-start | bytes 61448 | tf_op jit(solution)/shard_map/ppermute | solution.py:311
  59.7 1.0 %collective-permute-start.14 = (f32[5,8,128]{2,1,0:T(8,128)S(1)}, f32[5,8,128]{2,1,0:T(8,128)S(1)}, u32[]{:S(2)}, u32[]{:S(2)}) collective-permute-start(f32[5,8,128]{2,1,0:T(8,128)S(1)} %get-tuple-element.26), channel_id=1, source_target_pairs={{0,8},{8,0},{16,24},{24,16},{32,40},{40,32},{48,56},{56,48},{64,72... | collective-permute-start | bytes 61448 | tf_op jit(solution)/shard_map/ppermute | solution.py:311
  60.7 1.3 %collective-permute-done.16 = f32[5,8,128]{2,1,0:T(8,128)S(1)} collective-permute-done((f32[5,8,128]{2,1,0:T(8,128)S(1)}, f32[5,8,128]{2,1,0:T(8,128)S(1)}, u32[]{:S(2)}, u32[]{:S(2)}) %collective-permute-start.16) | collective-permute-done | bytes 20512 | tf_op jit(solution)/shard_map/ppermute | solution.py:311
  62.1 0.7 collective-permute-done.15
  62.8 0.0 collective-permute-done.14
  62.8 0.1 collective-permute-start.17
  62.9 3.8 %collective-permute-done.17 = f32[5,8,128]{2,1,0:T(8,128)S(1)} collective-permute-done((f32[5,8,128]{2,1,0:T(8,128)S(1)}, f32[5,8,128]{2,1,0:T(8,128)S(1)}, u32[]{:S(2)}, u32[]{:S(2)}) %collective-permute-start.17) | collective-permute-done | bytes 20512 | tf_op jit(solution)/shard_map/ppermute | solution.py:311
  66.6 3.0 %collective-permute-start.18 = (f32[5,8,128]{2,1,0:T(8,128)S(1)}, f32[5,8,128]{2,1,0:T(8,128)S(1)}, u32[]{:S(2)}, u32[]{:S(2)}) collective-permute-start(f32[5,8,128]{2,1,0:T(8,128)S(1)} %add.45), channel_id=1, source_target_pairs={{0,224},{8,232},{16,240},{24,248},{32,64},{40,72},{48,80},{56,88},... | collective-permute-start | bytes 61448 | tf_op jit(solution)/shard_map/ppermute | solution.py:311
  69.7 2.0 %collective-permute-done.18 = f32[5,8,128]{2,1,0:T(8,128)S(1)} collective-permute-done((f32[5,8,128]{2,1,0:T(8,128)S(1)}, f32[5,8,128]{2,1,0:T(8,128)S(1)}, u32[]{:S(2)}, u32[]{:S(2)}) %collective-permute-start.18) | collective-permute-done | bytes 20512 | tf_op jit(solution)/shard_map/ppermute | solution.py:311
  71.6 2.0 %collective-permute-start.19 = (f32[5,8,128]{2,1,0:T(8,128)S(1)}, f32[5,8,128]{2,1,0:T(8,128)S(1)}, u32[]{:S(2)}, u32[]{:S(2)}) collective-permute-start(f32[5,8,128]{2,1,0:T(8,128)S(1)} %add.46), channel_id=1, source_target_pairs={{0,96},{8,104},{16,112},{24,120},{32,192},{40,200},{48,208},{56,21... | collective-permute-start | bytes 61448 | tf_op jit(solution)/shard_map/ppermute | solution.py:311
  73.7 3.8 %collective-permute-done.19 = f32[5,8,128]{2,1,0:T(8,128)S(1)} collective-permute-done((f32[5,8,128]{2,1,0:T(8,128)S(1)}, f32[5,8,128]{2,1,0:T(8,128)S(1)}, u32[]{:S(2)}, u32[]{:S(2)}) %collective-permute-start.19) | collective-permute-done | bytes 20512 | tf_op jit(solution)/shard_map/ppermute | solution.py:311
  77.5 1.3 %relax_last.1 = f32[4,128,256]{2,1,0:T(8,128)S(1)} custom-call(s32[1]{0:T(128)} %bitcast.vel_ref.refs_0_, f32[5,8,128]{2,1,0:T(8,128)S(1)} %add.47.refs_1_, f32[4,16,8,128]{3,2,1,0:T(8,128)S(1)} %get-tuple-element.27.refs_2_, f32[4,16,8,128]{3,2,1,0:T(8,128)S(1)} %get-tuple-element.28.refs_3_), custom_call_target="tpu_custom_call" | custom-call | tf_op jit(solution)/shard_map/relax_last/pallas_call | solution.py:260
  78.8 1.1 %copy.3 = f32[128,4,256]{2,1,0:T(4,128)} copy(f32[128,4,256]{2,0,1:T(8,128)S(1)} %bitcast.5) | data formatting | bytes 1048576 | tf_op jit(solution)/shard_map/transpose | solution.py:338
  (10 shorter events, 0.1 us)
Async XLA Ops:
  3.2 15.3 %collective-permute-start = (f32[4,16,8,128]{3,2,1,0:T(8,128)S(1)}, f32[4,16,8,128]{3,2,1,0:T(8,128)S(1)}, u32[]{:S(2)}, u32[]{:S(2)}) collective-permute-start(f32[4,16,8,128]{3,2,1,0:T(8,128)S(1)} %get-tuple-element.17.up0), channel_id=1, source_target_pairs={{0,1},{1,2},{2,3},{3,4},{4,5},{5,6},{6,7},{7,0},{8,9},{9,10},{10,1... | collective-permute-start | bytes 786440 | tf_op jit(solution)/shard_map/ppermute | solution.py:306
  4.4 14.2 %collective-permute-start.2 = (f32[4,16,8,128]{3,2,1,0:T(8,128)S(1)}, f32[4,16,8,128]{3,2,1,0:T(8,128)S(1)}, u32[]{:S(2)}, u32[]{:S(2)}) collective-permute-start(f32[4,16,8,128]{3,2,1,0:T(8,128)S(1)} %get-tuple-element.18.down0), channel_id=1, source_target_pairs={{0,7},{1,0},{2,1},{3,2},{4,3},{5,4},{6,5},{7,6},{8,15},{9,8},{10,9... | collective-permute-start | bytes 786440 | tf_op jit(solution)/shard_map/ppermute | solution.py:306
  6.9 11.7 %collective-permute-start.3 = (f32[2,16,8,128]{3,2,1,0:T(8,128)S(1)}, f32[2,16,8,128]{3,2,1,0:T(8,128)S(1)}, u32[]{:S(2)}, u32[]{:S(2)}) collective-permute-start(f32[2,16,8,128]{3,2,1,0:T(8,128)S(1)} %slice.7), channel_id=1, source_target_pairs={{0,6},{1,7},{2,0},{3,1},{4,2},{5,3},{6,4},{7,5},{8,14},{9,15},{10,... | collective-permute-start | bytes 393224 | tf_op jit(solution)/shard_map/ppermute | solution.py:306
  7.7 10.9 %collective-permute-start.1 = (f32[2,16,8,128]{3,2,1,0:T(8,128)S(1)}, f32[2,16,8,128]{3,2,1,0:T(8,128)S(1)}, u32[]{:S(2)}, u32[]{:S(2)}) collective-permute-start(f32[2,16,8,128]{3,2,1,0:T(8,128)S(1)} %slice.6), channel_id=1, source_target_pairs={{0,2},{1,3},{2,4},{3,5},{4,6},{5,7},{6,0},{7,1},{8,10},{9,11},{10,... | collective-permute-start | bytes 393224 | tf_op jit(solution)/shard_map/ppermute | solution.py:306
  20.9 3.2 %collective-permute-start.6 = (f32[5,8,128]{2,1,0:T(8,128)S(1)}, f32[5,8,128]{2,1,0:T(8,128)S(1)}, u32[]{:S(2)}, u32[]{:S(2)}) collective-permute-start(f32[5,8,128]{2,1,0:T(8,128)S(1)} %get-tuple-element.19), channel_id=1, source_target_pairs={{0,24},{8,16},{16,8},{24,0},{32,56},{40,48},{48,40},{56,32},{64,88... | collective-permute-start | bytes 61448 | tf_op jit(solution)/shard_map/ppermute | solution.py:311
  20.9 4.0 %collective-permute-start.5 = (f32[5,8,128]{2,1,0:T(8,128)S(1)}, f32[5,8,128]{2,1,0:T(8,128)S(1)}, u32[]{:S(2)}, u32[]{:S(2)}) collective-permute-start(f32[5,8,128]{2,1,0:T(8,128)S(1)} %get-tuple-element.19), channel_id=1, source_target_pairs={{0,16},{8,24},{16,0},{24,8},{32,48},{40,56},{48,32},{56,40},{64,80... | collective-permute-start | bytes 61448 | tf_op jit(solution)/shard_map/ppermute | solution.py:311
  21.8 3.0 %collective-permute-start.4 = (f32[5,8,128]{2,1,0:T(8,128)S(1)}, f32[5,8,128]{2,1,0:T(8,128)S(1)}, u32[]{:S(2)}, u32[]{:S(2)}) collective-permute-start(f32[5,8,128]{2,1,0:T(8,128)S(1)} %get-tuple-element.19), channel_id=1, source_target_pairs={{0,8},{8,0},{16,24},{24,16},{32,40},{40,32},{48,56},{56,48},{64,72... | collective-permute-start | bytes 61448 | tf_op jit(solution)/shard_map/ppermute | solution.py:311
  24.9 3.9 %collective-permute-start.7 = (f32[5,8,128]{2,1,0:T(8,128)S(1)}, f32[5,8,128]{2,1,0:T(8,128)S(1)}, u32[]{:S(2)}, u32[]{:S(2)}) collective-permute-start(f32[5,8,128]{2,1,0:T(8,128)S(1)} %add_add_fusion.1), channel_id=1, source_target_pairs={{0,32},{8,40},{16,48},{24,56},{32,0},{40,8},{48,16},{56,24},{64,96... | collective-permute-start | bytes 61448 | tf_op jit(solution)/shard_map/ppermute | solution.py:311
  28.8 7.6 %collective-permute-start.8 = (f32[5,8,128]{2,1,0:T(8,128)S(1)}, f32[5,8,128]{2,1,0:T(8,128)S(1)}, u32[]{:S(2)}, u32[]{:S(2)}) collective-permute-start(f32[5,8,128]{2,1,0:T(8,128)S(1)} %add.39), channel_id=1, source_target_pairs={{0,224},{8,232},{16,240},{24,248},{32,64},{40,72},{48,80},{56,88},... | collective-permute-start | bytes 61448 | tf_op jit(solution)/shard_map/ppermute | solution.py:311
  36.4 5.8 %collective-permute-start.9 = (f32[5,8,128]{2,1,0:T(8,128)S(1)}, f32[5,8,128]{2,1,0:T(8,128)S(1)}, u32[]{:S(2)}, u32[]{:S(2)}) collective-permute-start(f32[5,8,128]{2,1,0:T(8,128)S(1)} %add.40), channel_id=1, source_target_pairs={{0,96},{8,104},{16,112},{24,120},{32,192},{40,200},{48,208},{56,21... | collective-permute-start | bytes 61448 | tf_op jit(solution)/shard_map/ppermute | solution.py:311
  42.8 13.7 %collective-permute-start.10 = (f32[4,16,8,128]{3,2,1,0:T(8,128)S(1)}, f32[4,16,8,128]{3,2,1,0:T(8,128)S(1)}, u32[]{:S(2)}, u32[]{:S(2)}) collective-permute-start(f32[4,16,8,128]{3,2,1,0:T(8,128)S(1)} %get-tuple-element.22.up0), channel_id=1, source_target_pairs={{0,1},{1,2},{2,3},{3,4},{4,5},{5,6},{6,7},{7,0},{8,9},{9,10},{10,1... | collective-permute-start | bytes 786440 | tf_op jit(solution)/shard_map/ppermute | solution.py:306
  44.7 11.8 %collective-permute-start.12 = (f32[4,16,8,128]{3,2,1,0:T(8,128)S(1)}, f32[4,16,8,128]{3,2,1,0:T(8,128)S(1)}, u32[]{:S(2)}, u32[]{:S(2)}) collective-permute-start(f32[4,16,8,128]{3,2,1,0:T(8,128)S(1)} %get-tuple-element.24.down0), channel_id=1, source_target_pairs={{0,7},{1,0},{2,1},{3,2},{4,3},{5,4},{6,5},{7,6},{8,15},{9,8},{10,9... | collective-permute-start | bytes 786440 | tf_op jit(solution)/shard_map/ppermute | solution.py:306
  46.4 5.0 %collective-permute-start.11 = (f32[2,16,8,128]{3,2,1,0:T(8,128)S(1)}, f32[2,16,8,128]{3,2,1,0:T(8,128)S(1)}, u32[]{:S(2)}, u32[]{:S(2)}) collective-permute-start(f32[2,16,8,128]{3,2,1,0:T(8,128)S(1)} %get-tuple-element.23), channel_id=1, source_target_pairs={{0,2},{1,3},{2,4},{3,5},{4,6},{5,7},{6,0},{7,1},{8,10},{9,11},{10,... | collective-permute-start | bytes 393224 | tf_op jit(solution)/shard_map/ppermute | solution.py:306
  47.5 9.0 %collective-permute-start.13 = (f32[2,16,8,128]{3,2,1,0:T(8,128)S(1)}, f32[2,16,8,128]{3,2,1,0:T(8,128)S(1)}, u32[]{:S(2)}, u32[]{:S(2)}) collective-permute-start(f32[2,16,8,128]{3,2,1,0:T(8,128)S(1)} %get-tuple-element.25), channel_id=1, source_target_pairs={{0,6},{1,7},{2,0},{3,1},{4,2},{5,3},{6,4},{7,5},{8,14},{9,15},{10,... | collective-permute-start | bytes 393224 | tf_op jit(solution)/shard_map/ppermute | solution.py:306
  58.8 3.2 %collective-permute-start.16 = (f32[5,8,128]{2,1,0:T(8,128)S(1)}, f32[5,8,128]{2,1,0:T(8,128)S(1)}, u32[]{:S(2)}, u32[]{:S(2)}) collective-permute-start(f32[5,8,128]{2,1,0:T(8,128)S(1)} %get-tuple-element.26), channel_id=1, source_target_pairs={{0,24},{8,16},{16,8},{24,0},{32,56},{40,48},{48,40},{56,32},{64,88... | collective-permute-start | bytes 61448 | tf_op jit(solution)/shard_map/ppermute | solution.py:311
  58.9 3.9 %collective-permute-start.15 = (f32[5,8,128]{2,1,0:T(8,128)S(1)}, f32[5,8,128]{2,1,0:T(8,128)S(1)}, u32[]{:S(2)}, u32[]{:S(2)}) collective-permute-start(f32[5,8,128]{2,1,0:T(8,128)S(1)} %get-tuple-element.26), channel_id=1, source_target_pairs={{0,16},{8,24},{16,0},{24,8},{32,48},{40,56},{48,32},{56,40},{64,80... | collective-permute-start | bytes 61448 | tf_op jit(solution)/shard_map/ppermute | solution.py:311
  59.7 3.1 %collective-permute-start.14 = (f32[5,8,128]{2,1,0:T(8,128)S(1)}, f32[5,8,128]{2,1,0:T(8,128)S(1)}, u32[]{:S(2)}, u32[]{:S(2)}) collective-permute-start(f32[5,8,128]{2,1,0:T(8,128)S(1)} %get-tuple-element.26), channel_id=1, source_target_pairs={{0,8},{8,0},{16,24},{24,16},{32,40},{40,32},{48,56},{56,48},{64,72... | collective-permute-start | bytes 61448 | tf_op jit(solution)/shard_map/ppermute | solution.py:311
  62.8 3.9 %collective-permute-start.17 = (f32[5,8,128]{2,1,0:T(8,128)S(1)}, f32[5,8,128]{2,1,0:T(8,128)S(1)}, u32[]{:S(2)}, u32[]{:S(2)}) collective-permute-start(f32[5,8,128]{2,1,0:T(8,128)S(1)} %add_add_fusion), channel_id=1, source_target_pairs={{0,32},{8,40},{16,48},{24,56},{32,0},{40,8},{48,16},{56,24},{64,96... | collective-permute-start | bytes 61448 | tf_op jit(solution)/shard_map/ppermute | solution.py:311
  66.6 5.0 %collective-permute-start.18 = (f32[5,8,128]{2,1,0:T(8,128)S(1)}, f32[5,8,128]{2,1,0:T(8,128)S(1)}, u32[]{:S(2)}, u32[]{:S(2)}) collective-permute-start(f32[5,8,128]{2,1,0:T(8,128)S(1)} %add.45), channel_id=1, source_target_pairs={{0,224},{8,232},{16,240},{24,248},{32,64},{40,72},{48,80},{56,88},... | collective-permute-start | bytes 61448 | tf_op jit(solution)/shard_map/ppermute | solution.py:311
  71.6 5.8 %collective-permute-start.19 = (f32[5,8,128]{2,1,0:T(8,128)S(1)}, f32[5,8,128]{2,1,0:T(8,128)S(1)}, u32[]{:S(2)}, u32[]{:S(2)}) collective-permute-start(f32[5,8,128]{2,1,0:T(8,128)S(1)} %add.46), channel_id=1, source_target_pairs={{0,96},{8,104},{16,112},{24,120},{32,192},{40,200},{48,208},{56,21... | collective-permute-start | bytes 61448 | tf_op jit(solution)/shard_map/ppermute | solution.py:311

commit v3 on v2

--- a/solution.py
+++ b/solution.py
@@ -312,15 +312,9 @@
 
 
 def summed_over_velocities(value):
-    value = value + sum(swapped_over(value, lambda i, k=k: i ^ k) for k in (1, 2, 3))
-    rounds = (
-        lambda c: c ^ 1,
-        lambda c: (c + 1) % 8 if c % 2 else (c - 1) % 8,
-        lambda c: (3, 6, 5, 0, 7, 2, 1, 4)[c],
-    )
-    for chip in rounds:
-        value = value + swapped_over(value, lambda i: 4 * chip(i // 4) + i % 4)
-    return value
+    for step in (1, 4):
+        value = value + sum(swapped_over(value, lambda i, k=k: i ^ (step * k)) for k in (1, 2, 3))
+    return value + swapped_over(value, lambda i: 4 * (7 - i // 4) + i % 4)
 
 
 def on_device(distribution):

time: 80.5 us -> 77.9 us (0.968); the launches traced: 79.9 us -> 76.3 us
  waiting for transfers between devices: 37.5 us -> 32 us
  starting transfers between devices: 31.4 us -> 33.4 us
    ppermute x12 -> x14, waiting for transfers between devices: 21.1 us -> 14.9 us  [swapped_over(): return lax.ppermute(value, 'vel', [(i, partner(i)) for i in range(size)])]
    ppermute x12 -> x14, starting transfers between devices: 18.8 us -> 20.8 us  [swapped_over(): return lax.ppermute(value, 'vel', [(i, partner(i)) for i in range(size)])]
  transfers between devices with their start and end apart: 20 -> 22, of which waited for: 13 -> 14; matrix products, arithmetic and copies ran while one was open for 0% -> 0% of each run, Pallas kernels for 0% -> 0%
where the time goes in v3:
time: 77.9 us; the launch traced here: 76.3 us
  starting transfers between devices  33.4 us (43%)
  waiting for transfers between devices  32 us (41%)
  Pallas kernels  8.54 us (11%)
  local copies, waits for them, and re-layouts  2.3 us (3%)
    ppermute x14, starting transfers between devices, swapped_over(): return lax.ppermute(value, 'vel', [(i, partner(i)) for i in range(size)])  20.8 us
    ppermute x8, waiting for transfers between devices, passed_along(): lax.ppermute(value, 'gx', [(i, (i + by) % size) for i in range(size)])  17 us
    ppermute x14, waiting for transfers between devices, swapped_over(): return lax.ppermute(value, 'vel', [(i, partner(i)) for i in range(size)])  14.9 us
    ppermute x8, starting transfers between devices, passed_along(): lax.ppermute(value, 'gx', [(i, (i + by) % size) for i in range(size)])  12.6 us
    pallas_call x5, Pallas kernels, call(): pl.pallas_call(body, in_specs=[smem()] + [vmem()] * len(operands), out_sp...  8.54 us
  transfers between devices with their start and end apart: 22, of which 14 were waited for; matrix products, arithmetic and copies ran while one was open for 0% of the time, Pallas kernels for 0%

profile of v3, /device:TPU:30, one launch (start us, length us, event | category | flops | bytes accessed | tf_op | source)
XLA Modules:
  0.0 76.3 jit_solution(13342605522351531903)
XLA Ops:
  0.0 1.1 %copy.5 = f32[128,4,256]{2,0,1:T(8,128)S(1)} copy(f32[128,4,256]{2,1,0:T(4,128)} %param.1) | data formatting | bytes 1048576 | tf_op args[0]
  1.1 2.1 %pack.1 = (f32[4,16,8,128]{3,2,1,0:T(8,128)S(1)}, f32[4,16,8,128]{3,2,1,0:T(8,128)S(1)}) custom-call(s32[1]{0:T(128)} %bitcast.vel_ref.refs_0_, f32[4,128,256]{2,1,0:T(8,128)S(1)} %bitcast.6), custom_call_target="tpu_custom_call" | custom-call | tf_op jit(solution)/shard_map/pack/pallas_call | solution.py:260
  3.2 1.1 %collective-permute-start = (f32[4,16,8,128]{3,2,1,0:T(8,128)S(1)}, f32[4,16,8,128]{3,2,1,0:T(8,128)S(1)}, u32[]{:S(2)}, u32[]{:S(2)}) collective-permute-start(f32[4,16,8,128]{3,2,1,0:T(8,128)S(1)} %get-tuple-element.17.up0), channel_id=1, source_target_pairs={{0,1},{1,2},{2,3},{3,4},{4,5},{5,6},{6,7},{7,0},{8,9},{9,10},{10,1... | collective-permute-start | bytes 786440 | tf_op jit(solution)/shard_map/ppermute | solution.py:306
  4.4 2.5 %collective-permute-start.2 = (f32[4,16,8,128]{3,2,1,0:T(8,128)S(1)}, f32[4,16,8,128]{3,2,1,0:T(8,128)S(1)}, u32[]{:S(2)}, u32[]{:S(2)}) collective-permute-start(f32[4,16,8,128]{3,2,1,0:T(8,128)S(1)} %get-tuple-element.18.down0), channel_id=1, source_target_pairs={{0,7},{1,0},{2,1},{3,2},{4,3},{5,4},{6,5},{7,6},{8,15},{9,8},{10,9... | collective-permute-start | bytes 786440 | tf_op jit(solution)/shard_map/ppermute | solution.py:306
  6.9 0.8 %collective-permute-start.3 = (f32[2,16,8,128]{3,2,1,0:T(8,128)S(1)}, f32[2,16,8,128]{3,2,1,0:T(8,128)S(1)}, u32[]{:S(2)}, u32[]{:S(2)}) collective-permute-start(f32[2,16,8,128]{3,2,1,0:T(8,128)S(1)} %slice.7), channel_id=1, source_target_pairs={{0,6},{1,7},{2,0},{3,1},{4,2},{5,3},{6,4},{7,5},{8,14},{9,15},{10,... | collective-permute-start | bytes 393224 | tf_op jit(solution)/shard_map/ppermute | solution.py:306
  7.7 2.6 %collective-permute-start.1 = (f32[2,16,8,128]{3,2,1,0:T(8,128)S(1)}, f32[2,16,8,128]{3,2,1,0:T(8,128)S(1)}, u32[]{:S(2)}, u32[]{:S(2)}) collective-permute-start(f32[2,16,8,128]{3,2,1,0:T(8,128)S(1)} %slice.6), channel_id=1, source_target_pairs={{0,2},{1,3},{2,4},{3,5},{4,6},{5,7},{6,0},{7,1},{8,10},{9,11},{10,... | collective-permute-start | bytes 393224 | tf_op jit(solution)/shard_map/ppermute | solution.py:306
  10.3 8.3 %collective-permute-done.3.down2 = f32[2,16,8,128]{3,2,1,0:T(8,128)S(1)} collective-permute-done((f32[2,16,8,128]{3,2,1,0:T(8,128)S(1)}, f32[2,16,8,128]{3,2,1,0:T(8,128)S(1)}, u32[]{:S(2)}, u32[]{:S(2)}) %collective-permute-start.3) | collective-permute-done | bytes 131104 | tf_op jit(solution)/shard_map/ppermute | solution.py:306
  18.6 0.0 collective-permute-done.1.up2
  18.6 0.0 collective-permute-done.up1
  18.6 2.3 %stream.2 = (f32[4,16,8,128]{3,2,1,0:T(8,128)S(1)}, f32[4,16,8,128]{3,2,1,0:T(8,128)S(1)}, f32[5,8,128]{2,1,0:T(8,128)S(1)}) custom-call(s32[1]{0:T(128)} %bitcast.vel_ref.refs_0_, f32[4,16,8,128]{3,2,1,0:T(8,128)S(1)} %get-tuple-element.17.up0, f32[4,16,8,128]{3,2,1,0:T(8,128)S(1)} %collective-permute-done.up1, ...), custom_call_target="tpu_custom_call" | custom-call | tf_op jit(solution)/shard_map/stream/pallas_call | solution.py:260
  20.9 0.0 collective-permute-start.6
  20.9 0.9 %collective-permute-start.5 = (f32[5,8,128]{2,1,0:T(8,128)S(1)}, f32[5,8,128]{2,1,0:T(8,128)S(1)}, u32[]{:S(2)}, u32[]{:S(2)}) collective-permute-start(f32[5,8,128]{2,1,0:T(8,128)S(1)} %get-tuple-element.19), channel_id=1, source_target_pairs={{0,16},{8,24},{16,0},{24,8},{32,48},{40,56},{48,32},{56,40},{64,80... | collective-permute-start | bytes 61448 | tf_op jit(solution)/shard_map/ppermute | solution.py:311
  21.8 0.9 %collective-permute-start.4 = (f32[5,8,128]{2,1,0:T(8,128)S(1)}, f32[5,8,128]{2,1,0:T(8,128)S(1)}, u32[]{:S(2)}, u32[]{:S(2)}) collective-permute-start(f32[5,8,128]{2,1,0:T(8,128)S(1)} %get-tuple-element.19), channel_id=1, source_target_pairs={{0,8},{8,0},{16,24},{24,16},{32,40},{40,32},{48,56},{56,48},{64,72... | collective-permute-start | bytes 61448 | tf_op jit(solution)/shard_map/ppermute | solution.py:311
  22.8 1.3 %collective-permute-done.6 = f32[5,8,128]{2,1,0:T(8,128)S(1)} collective-permute-done((f32[5,8,128]{2,1,0:T(8,128)S(1)}, f32[5,8,128]{2,1,0:T(8,128)S(1)}, u32[]{:S(2)}, u32[]{:S(2)}) %collective-permute-start.6) | collective-permute-done | bytes 20512 | tf_op jit(solution)/shard_map/ppermute | solution.py:311
  24.1 0.8 %collective-permute-done.5 = f32[5,8,128]{2,1,0:T(8,128)S(1)} collective-permute-done((f32[5,8,128]{2,1,0:T(8,128)S(1)}, f32[5,8,128]{2,1,0:T(8,128)S(1)}, u32[]{:S(2)}, u32[]{:S(2)}) %collective-permute-start.5) | collective-permute-done | bytes 20512 | tf_op jit(solution)/shard_map/ppermute | solution.py:311
  24.9 0.0 collective-permute-done.4
  24.9 4.7 %collective-permute-start.9 = (f32[5,8,128]{2,1,0:T(8,128)S(1)}, f32[5,8,128]{2,1,0:T(8,128)S(1)}, u32[]{:S(2)}, u32[]{:S(2)}) collective-permute-start(f32[5,8,128]{2,1,0:T(8,128)S(1)} %add_add_fusion.3), channel_id=1, source_target_pairs={{0,96},{8,104},{16,112},{24,120},{32,64},{40,72},{48,80},{56,88},{... | collective-permute-start | bytes 61448 | tf_op jit(solution)/shard_map/ppermute | solution.py:311
  29.6 0.0 collective-permute-start.8
  29.6 0.7 collective-permute-start.7
  30.3 1.1 %collective-permute-done.9 = f32[5,8,128]{2,1,0:T(8,128)S(1)} collective-permute-done((f32[5,8,128]{2,1,0:T(8,128)S(1)}, f32[5,8,128]{2,1,0:T(8,128)S(1)}, u32[]{:S(2)}, u32[]{:S(2)}) %collective-permute-start.9) | collective-permute-done | bytes 20512 | tf_op jit(solution)/shard_map/ppermute | solution.py:311
  31.4 2.9 %collective-permute-done.8 = f32[5,8,128]{2,1,0:T(8,128)S(1)} collective-permute-done((f32[5,8,128]{2,1,0:T(8,128)S(1)}, f32[5,8,128]{2,1,0:T(8,128)S(1)}, u32[]{:S(2)}, u32[]{:S(2)}) %collective-permute-start.8) | collective-permute-done | bytes 20512 | tf_op jit(solution)/shard_map/ppermute | solution.py:311
  34.3 3.2 %collective-permute-start.10 = (f32[5,8,128]{2,1,0:T(8,128)S(1)}, f32[5,8,128]{2,1,0:T(8,128)S(1)}, u32[]{:S(2)}, u32[]{:S(2)}) collective-permute-start(f32[5,8,128]{2,1,0:T(8,128)S(1)} %add_add_fusion.2), channel_id=1, source_target_pairs={{0,224},{8,232},{16,240},{24,248},{32,192},{40,200},{48,208},{56,2... | collective-permute-start | bytes 61448 | tf_op jit(solution)/shard_map/ppermute | solution.py:311
  37.5 1.9 %collective-permute-done.10 = f32[5,8,128]{2,1,0:T(8,128)S(1)} collective-permute-done((f32[5,8,128]{2,1,0:T(8,128)S(1)}, f32[5,8,128]{2,1,0:T(8,128)S(1)}, u32[]{:S(2)}, u32[]{:S(2)}) %collective-permute-start.10) | collective-permute-done | bytes 20512 | tf_op jit(solution)/shard_map/ppermute | solution.py:311
  39.4 0.6 relax.1
  40.0 2.0 %collective-permute-start.11 = (f32[4,16,8,128]{3,2,1,0:T(8,128)S(1)}, f32[4,16,8,128]{3,2,1,0:T(8,128)S(1)}, u32[]{:S(2)}, u32[]{:S(2)}) collective-permute-start(f32[4,16,8,128]{3,2,1,0:T(8,128)S(1)} %get-tuple-element.22.up0), channel_id=1, source_target_pairs={{0,1},{1,2},{2,3},{3,4},{4,5},{5,6},{6,7},{7,0},{8,9},{9,10},{10,1... | collective-permute-start | bytes 786440 | tf_op jit(solution)/shard_map/ppermute | solution.py:306
  41.9 1.7 %collective-permute-start.13 = (f32[4,16,8,128]{3,2,1,0:T(8,128)S(1)}, f32[4,16,8,128]{3,2,1,0:T(8,128)S(1)}, u32[]{:S(2)}, u32[]{:S(2)}) collective-permute-start(f32[4,16,8,128]{3,2,1,0:T(8,128)S(1)} %get-tuple-element.24.down0), channel_id=1, source_target_pairs={{0,7},{1,0},{2,1},{3,2},{4,3},{5,4},{6,5},{7,6},{8,15},{9,8},{10,9... | collective-permute-start | bytes 786440 | tf_op jit(solution)/shard_map/ppermute | solution.py:306
  43.6 1.1 %collective-permute-start.12 = (f32[2,16,8,128]{3,2,1,0:T(8,128)S(1)}, f32[2,16,8,128]{3,2,1,0:T(8,128)S(1)}, u32[]{:S(2)}, u32[]{:S(2)}) collective-permute-start(f32[2,16,8,128]{3,2,1,0:T(8,128)S(1)} %get-tuple-element.23), channel_id=1, source_target_pairs={{0,2},{1,3},{2,4},{3,5},{4,6},{5,7},{6,0},{7,1},{8,10},{9,11},{10,... | collective-permute-start | bytes 393224 | tf_op jit(solution)/shard_map/ppermute | solution.py:306
  44.7 0.9 %collective-permute-start.14 = (f32[2,16,8,128]{3,2,1,0:T(8,128)S(1)}, f32[2,16,8,128]{3,2,1,0:T(8,128)S(1)}, u32[]{:S(2)}, u32[]{:S(2)}) collective-permute-start(f32[2,16,8,128]{3,2,1,0:T(8,128)S(1)} %get-tuple-element.25), channel_id=1, source_target_pairs={{0,6},{1,7},{2,0},{3,1},{4,2},{5,3},{6,4},{7,5},{8,14},{9,15},{10,... | collective-permute-start | bytes 393224 | tf_op jit(solution)/shard_map/ppermute | solution.py:306
  45.6 2.9 %collective-permute-done.12.up2 = f32[2,16,8,128]{3,2,1,0:T(8,128)S(1)} collective-permute-done((f32[2,16,8,128]{3,2,1,0:T(8,128)S(1)}, f32[2,16,8,128]{3,2,1,0:T(8,128)S(1)}, u32[]{:S(2)}, u32[]{:S(2)}) %collective-permute-start.12) | collective-permute-done | bytes 131104 | tf_op jit(solution)/shard_map/ppermute | solution.py:306
  48.6 5.8 %collective-permute-done.14.down2 = f32[2,16,8,128]{3,2,1,0:T(8,128)S(1)} collective-permute-done((f32[2,16,8,128]{3,2,1,0:T(8,128)S(1)}, f32[2,16,8,128]{3,2,1,0:T(8,128)S(1)}, u32[]{:S(2)}, u32[]{:S(2)}) %collective-permute-start.14) | collective-permute-done | bytes 131104 | tf_op jit(solution)/shard_map/ppermute | solution.py:306
  54.3 0.0 collective-permute-done.13.down1
  54.3 2.3 %stream.3 = (f32[4,16,8,128]{3,2,1,0:T(8,128)S(1)}, f32[4,16,8,128]{3,2,1,0:T(8,128)S(1)}, f32[5,8,128]{2,1,0:T(8,128)S(1)}) custom-call(s32[1]{0:T(128)} %bitcast.vel_ref.refs_0_, f32[4,16,8,128]{3,2,1,0:T(8,128)S(1)} %get-tuple-element.22.up0, f32[4,16,8,128]{3,2,1,0:T(8,128)S(1)} %collective-permute-done.11.up1, ...), custom_call_target="tpu_custom_call" | custom-call | tf_op jit(solution)/shard_map/stream/pallas_call | solution.py:260
  56.7 0.0 collective-permute-start.17
  56.7 1.0 %collective-permute-start.16 = (f32[5,8,128]{2,1,0:T(8,128)S(1)}, f32[5,8,128]{2,1,0:T(8,128)S(1)}, u32[]{:S(2)}, u32[]{:S(2)}) collective-permute-start(f32[5,8,128]{2,1,0:T(8,128)S(1)} %get-tuple-element.26), channel_id=1, source_target_pairs={{0,16},{8,24},{16,0},{24,8},{32,48},{40,56},{48,32},{56,40},{64,80... | collective-permute-start | bytes 61448 | tf_op jit(solution)/shard_map/ppermute | solution.py:311
  57.7 0.9 %collective-permute-start.15 = (f32[5,8,128]{2,1,0:T(8,128)S(1)}, f32[5,8,128]{2,1,0:T(8,128)S(1)}, u32[]{:S(2)}, u32[]{:S(2)}) collective-permute-start(f32[5,8,128]{2,1,0:T(8,128)S(1)} %get-tuple-element.26), channel_id=1, source_target_pairs={{0,8},{8,0},{16,24},{24,16},{32,40},{40,32},{48,56},{56,48},{64,72... | collective-permute-start | bytes 61448 | tf_op jit(solution)/shard_map/ppermute | solution.py:311
  58.6 1.3 %collective-permute-done.17 = f32[5,8,128]{2,1,0:T(8,128)S(1)} collective-permute-done((f32[5,8,128]{2,1,0:T(8,128)S(1)}, f32[5,8,128]{2,1,0:T(8,128)S(1)}, u32[]{:S(2)}, u32[]{:S(2)}) %collective-permute-start.17) | collective-permute-done | bytes 20512 | tf_op jit(solution)/shard_map/ppermute | solution.py:311
  59.9 0.8 %collective-permute-done.16 = f32[5,8,128]{2,1,0:T(8,128)S(1)} collective-permute-done((f32[5,8,128]{2,1,0:T(8,128)S(1)}, f32[5,8,128]{2,1,0:T(8,128)S(1)}, u32[]{:S(2)}, u32[]{:S(2)}) %collective-permute-start.16) | collective-permute-done | bytes 20512 | tf_op jit(solution)/shard_map/ppermute | solution.py:311
  60.7 0.0 collective-permute-done.15
  60.7 2.1 %collective-permute-start.20 = (f32[5,8,128]{2,1,0:T(8,128)S(1)}, f32[5,8,128]{2,1,0:T(8,128)S(1)}, u32[]{:S(2)}, u32[]{:S(2)}) collective-permute-start(f32[5,8,128]{2,1,0:T(8,128)S(1)} %add_add_fusion.1), channel_id=1, source_target_pairs={{0,96},{8,104},{16,112},{24,120},{32,64},{40,72},{48,80},{56,88},{... | collective-permute-start | bytes 61448 | tf_op jit(solution)/shard_map/ppermute | solution.py:311
  62.8 1.6 %collective-permute-start.19 = (f32[5,8,128]{2,1,0:T(8,128)S(1)}, f32[5,8,128]{2,1,0:T(8,128)S(1)}, u32[]{:S(2)}, u32[]{:S(2)}) collective-permute-start(f32[5,8,128]{2,1,0:T(8,128)S(1)} %add_add_fusion.1), channel_id=1, source_target_pairs={{0,64},{8,72},{16,80},{24,88},{32,96},{40,104},{48,112},{56,120},{... | collective-permute-start | bytes 61448 | tf_op jit(solution)/shard_map/ppermute | solution.py:311
  64.4 0.8 %collective-permute-start.18 = (f32[5,8,128]{2,1,0:T(8,128)S(1)}, f32[5,8,128]{2,1,0:T(8,128)S(1)}, u32[]{:S(2)}, u32[]{:S(2)}) collective-permute-start(f32[5,8,128]{2,1,0:T(8,128)S(1)} %add_add_fusion.1), channel_id=1, source_target_pairs={{0,32},{8,40},{16,48},{24,56},{32,0},{40,8},{48,16},{56,24},{64,96... | collective-permute-start | bytes 61448 | tf_op jit(solution)/shard_map/ppermute | solution.py:311
  65.2 1.3 %collective-permute-done.20 = f32[5,8,128]{2,1,0:T(8,128)S(1)} collective-permute-done((f32[5,8,128]{2,1,0:T(8,128)S(1)}, f32[5,8,128]{2,1,0:T(8,128)S(1)}, u32[]{:S(2)}, u32[]{:S(2)}) %collective-permute-start.20) | collective-permute-done | bytes 20512 | tf_op jit(solution)/shard_map/ppermute | solution.py:311
  66.5 1.0 %collective-permute-done.19 = f32[5,8,128]{2,1,0:T(8,128)S(1)} collective-permute-done((f32[5,8,128]{2,1,0:T(8,128)S(1)}, f32[5,8,128]{2,1,0:T(8,128)S(1)}, u32[]{:S(2)}, u32[]{:S(2)}) %collective-permute-start.19) | collective-permute-done | bytes 20512 | tf_op jit(solution)/shard_map/ppermute | solution.py:311
  67.5 0.7 collective-permute-done.18
  68.2 3.9 %collective-permute-start.21 = (f32[5,8,128]{2,1,0:T(8,128)S(1)}, f32[5,8,128]{2,1,0:T(8,128)S(1)}, u32[]{:S(2)}, u32[]{:S(2)}) collective-permute-start(f32[5,8,128]{2,1,0:T(8,128)S(1)} %add_add_fusion), channel_id=1, source_target_pairs={{0,224},{8,232},{16,240},{24,248},{32,192},{40,200},{48,208},{56,2... | collective-permute-start | bytes 61448 | tf_op jit(solution)/shard_map/ppermute | solution.py:311
  72.2 1.8 %collective-permute-done.21 = f32[5,8,128]{2,1,0:T(8,128)S(1)} collective-permute-done((f32[5,8,128]{2,1,0:T(8,128)S(1)}, f32[5,8,128]{2,1,0:T(8,128)S(1)}, u32[]{:S(2)}, u32[]{:S(2)}) %collective-permute-start.21) | collective-permute-done | bytes 20512 | tf_op jit(solution)/shard_map/ppermute | solution.py:311
  73.9 1.3 %relax_last.1 = f32[4,128,256]{2,1,0:T(8,128)S(1)} custom-call(s32[1]{0:T(128)} %bitcast.vel_ref.refs_0_, f32[5,8,128]{2,1,0:T(8,128)S(1)} %add.55.refs_1_, f32[4,16,8,128]{3,2,1,0:T(8,128)S(1)} %get-tuple-element.27.refs_2_, f32[4,16,8,128]{3,2,1,0:T(8,128)S(1)} %get-tuple-element.28.refs_3_), custom_call_target="tpu_custom_call" | custom-call | tf_op jit(solution)/shard_map/relax_last/pallas_call | solution.py:260
  75.2 1.1 %copy.3 = f32[128,4,256]{2,1,0:T(4,128)} copy(f32[128,4,256]{2,0,1:T(8,128)S(1)} %bitcast.5) | data formatting | bytes 1048576 | tf_op jit(solution)/shard_map/transpose | solution.py:332
  (11 shorter events, 0.1 us)
Async XLA Ops:
  3.2 15.3 %collective-permute-start = (f32[4,16,8,128]{3,2,1,0:T(8,128)S(1)}, f32[4,16,8,128]{3,2,1,0:T(8,128)S(1)}, u32[]{:S(2)}, u32[]{:S(2)}) collective-permute-start(f32[4,16,8,128]{3,2,1,0:T(8,128)S(1)} %get-tuple-element.17.up0), channel_id=1, source_target_pairs={{0,1},{1,2},{2,3},{3,4},{4,5},{5,6},{6,7},{7,0},{8,9},{9,10},{10,1... | collective-permute-start | bytes 786440 | tf_op jit(solution)/shard_map/ppermute | solution.py:306
  4.4 14.2 %collective-permute-start.2 = (f32[4,16,8,128]{3,2,1,0:T(8,128)S(1)}, f32[4,16,8,128]{3,2,1,0:T(8,128)S(1)}, u32[]{:S(2)}, u32[]{:S(2)}) collective-permute-start(f32[4,16,8,128]{3,2,1,0:T(8,128)S(1)} %get-tuple-element.18.down0), channel_id=1, source_target_pairs={{0,7},{1,0},{2,1},{3,2},{4,3},{5,4},{6,5},{7,6},{8,15},{9,8},{10,9... | collective-permute-start | bytes 786440 | tf_op jit(solution)/shard_map/ppermute | solution.py:306
  6.9 11.7 %collective-permute-start.3 = (f32[2,16,8,128]{3,2,1,0:T(8,128)S(1)}, f32[2,16,8,128]{3,2,1,0:T(8,128)S(1)}, u32[]{:S(2)}, u32[]{:S(2)}) collective-permute-start(f32[2,16,8,128]{3,2,1,0:T(8,128)S(1)} %slice.7), channel_id=1, source_target_pairs={{0,6},{1,7},{2,0},{3,1},{4,2},{5,3},{6,4},{7,5},{8,14},{9,15},{10,... | collective-permute-start | bytes 393224 | tf_op jit(solution)/shard_map/ppermute | solution.py:306
  7.7 10.9 %collective-permute-start.1 = (f32[2,16,8,128]{3,2,1,0:T(8,128)S(1)}, f32[2,16,8,128]{3,2,1,0:T(8,128)S(1)}, u32[]{:S(2)}, u32[]{:S(2)}) collective-permute-start(f32[2,16,8,128]{3,2,1,0:T(8,128)S(1)} %slice.6), channel_id=1, source_target_pairs={{0,2},{1,3},{2,4},{3,5},{4,6},{5,7},{6,0},{7,1},{8,10},{9,11},{10,... | collective-permute-start | bytes 393224 | tf_op jit(solution)/shard_map/ppermute | solution.py:306
  20.9 3.2 %collective-permute-start.6 = (f32[5,8,128]{2,1,0:T(8,128)S(1)}, f32[5,8,128]{2,1,0:T(8,128)S(1)}, u32[]{:S(2)}, u32[]{:S(2)}) collective-permute-start(f32[5,8,128]{2,1,0:T(8,128)S(1)} %get-tuple-element.19), channel_id=1, source_target_pairs={{0,24},{8,16},{16,8},{24,0},{32,56},{40,48},{48,40},{56,32},{64,88... | collective-permute-start | bytes 61448 | tf_op jit(solution)/shard_map/ppermute | solution.py:311
  20.9 4.0 %collective-permute-start.5 = (f32[5,8,128]{2,1,0:T(8,128)S(1)}, f32[5,8,128]{2,1,0:T(8,128)S(1)}, u32[]{:S(2)}, u32[]{:S(2)}) collective-permute-start(f32[5,8,128]{2,1,0:T(8,128)S(1)} %get-tuple-element.19), channel_id=1, source_target_pairs={{0,16},{8,24},{16,0},{24,8},{32,48},{40,56},{48,32},{56,40},{64,80... | collective-permute-start | bytes 61448 | tf_op jit(solution)/shard_map/ppermute | solution.py:311
  21.8 3.0 %collective-permute-start.4 = (f32[5,8,128]{2,1,0:T(8,128)S(1)}, f32[5,8,128]{2,1,0:T(8,128)S(1)}, u32[]{:S(2)}, u32[]{:S(2)}) collective-permute-start(f32[5,8,128]{2,1,0:T(8,128)S(1)} %get-tuple-element.19), channel_id=1, source_target_pairs={{0,8},{8,0},{16,24},{24,16},{32,40},{40,32},{48,56},{56,48},{64,72... | collective-permute-start | bytes 61448 | tf_op jit(solution)/shard_map/ppermute | solution.py:311
  24.9 6.5 %collective-permute-start.9 = (f32[5,8,128]{2,1,0:T(8,128)S(1)}, f32[5,8,128]{2,1,0:T(8,128)S(1)}, u32[]{:S(2)}, u32[]{:S(2)}) collective-permute-start(f32[5,8,128]{2,1,0:T(8,128)S(1)} %add_add_fusion.3), channel_id=1, source_target_pairs={{0,96},{8,104},{16,112},{24,120},{32,64},{40,72},{48,80},{56,88},{... | collective-permute-start | bytes 61448 | tf_op jit(solution)/shard_map/ppermute | solution.py:311
  29.6 4.7 %collective-permute-start.8 = (f32[5,8,128]{2,1,0:T(8,128)S(1)}, f32[5,8,128]{2,1,0:T(8,128)S(1)}, u32[]{:S(2)}, u32[]{:S(2)}) collective-permute-start(f32[5,8,128]{2,1,0:T(8,128)S(1)} %add_add_fusion.3), channel_id=1, source_target_pairs={{0,64},{8,72},{16,80},{24,88},{32,96},{40,104},{48,112},{56,120},{... | collective-permute-start | bytes 61448 | tf_op jit(solution)/shard_map/ppermute | solution.py:311
  29.6 4.7 %collective-permute-start.7 = (f32[5,8,128]{2,1,0:T(8,128)S(1)}, f32[5,8,128]{2,1,0:T(8,128)S(1)}, u32[]{:S(2)}, u32[]{:S(2)}) collective-permute-start(f32[5,8,128]{2,1,0:T(8,128)S(1)} %add_add_fusion.3), channel_id=1, source_target_pairs={{0,32},{8,40},{16,48},{24,56},{32,0},{40,8},{48,16},{56,24},{64,96... | collective-permute-start | bytes 61448 | tf_op jit(solution)/shard_map/ppermute | solution.py:311
  34.3 5.1 %collective-permute-start.10 = (f32[5,8,128]{2,1,0:T(8,128)S(1)}, f32[5,8,128]{2,1,0:T(8,128)S(1)}, u32[]{:S(2)}, u32[]{:S(2)}) collective-permute-start(f32[5,8,128]{2,1,0:T(8,128)S(1)} %add_add_fusion.2), channel_id=1, source_target_pairs={{0,224},{8,232},{16,240},{24,248},{32,192},{40,200},{48,208},{56,2... | collective-permute-start | bytes 61448 | tf_op jit(solution)/shard_map/ppermute | solution.py:311
  40.0 14.4 %collective-permute-start.11 = (f32[4,16,8,128]{3,2,1,0:T(8,128)S(1)}, f32[4,16,8,128]{3,2,1,0:T(8,128)S(1)}, u32[]{:S(2)}, u32[]{:S(2)}) collective-permute-start(f32[4,16,8,128]{3,2,1,0:T(8,128)S(1)} %get-tuple-element.22.up0), channel_id=1, source_target_pairs={{0,1},{1,2},{2,3},{3,4},{4,5},{5,6},{6,7},{7,0},{8,9},{9,10},{10,1... | collective-permute-start | bytes 786440 | tf_op jit(solution)/shard_map/ppermute | solution.py:306
  41.9 12.4 %collective-permute-start.13 = (f32[4,16,8,128]{3,2,1,0:T(8,128)S(1)}, f32[4,16,8,128]{3,2,1,0:T(8,128)S(1)}, u32[]{:S(2)}, u32[]{:S(2)}) collective-permute-start(f32[4,16,8,128]{3,2,1,0:T(8,128)S(1)} %get-tuple-element.24.down0), channel_id=1, source_target_pairs={{0,7},{1,0},{2,1},{3,2},{4,3},{5,4},{6,5},{7,6},{8,15},{9,8},{10,9... | collective-permute-start | bytes 786440 | tf_op jit(solution)/shard_map/ppermute | solution.py:306
  43.6 5.0 %collective-permute-start.12 = (f32[2,16,8,128]{3,2,1,0:T(8,128)S(1)}, f32[2,16,8,128]{3,2,1,0:T(8,128)S(1)}, u32[]{:S(2)}, u32[]{:S(2)}) collective-permute-start(f32[2,16,8,128]{3,2,1,0:T(8,128)S(1)} %get-tuple-element.23), channel_id=1, source_target_pairs={{0,2},{1,3},{2,4},{3,5},{4,6},{5,7},{6,0},{7,1},{8,10},{9,11},{10,... | collective-permute-start | bytes 393224 | tf_op jit(solution)/shard_map/ppermute | solution.py:306
  44.7 9.6 %collective-permute-start.14 = (f32[2,16,8,128]{3,2,1,0:T(8,128)S(1)}, f32[2,16,8,128]{3,2,1,0:T(8,128)S(1)}, u32[]{:S(2)}, u32[]{:S(2)}) collective-permute-start(f32[2,16,8,128]{3,2,1,0:T(8,128)S(1)} %get-tuple-element.25), channel_id=1, source_target_pairs={{0,6},{1,7},{2,0},{3,1},{4,2},{5,3},{6,4},{7,5},{8,14},{9,15},{10,... | collective-permute-start | bytes 393224 | tf_op jit(solution)/shard_map/ppermute | solution.py:306
  56.7 3.2 %collective-permute-start.17 = (f32[5,8,128]{2,1,0:T(8,128)S(1)}, f32[5,8,128]{2,1,0:T(8,128)S(1)}, u32[]{:S(2)}, u32[]{:S(2)}) collective-permute-start(f32[5,8,128]{2,1,0:T(8,128)S(1)} %get-tuple-element.26), channel_id=1, source_target_pairs={{0,24},{8,16},{16,8},{24,0},{32,56},{40,48},{48,40},{56,32},{64,88... | collective-permute-start | bytes 61448 | tf_op jit(solution)/shard_map/ppermute | solution.py:311
  56.7 4.0 %collective-permute-start.16 = (f32[5,8,128]{2,1,0:T(8,128)S(1)}, f32[5,8,128]{2,1,0:T(8,128)S(1)}, u32[]{:S(2)}, u32[]{:S(2)}) collective-permute-start(f32[5,8,128]{2,1,0:T(8,128)S(1)} %get-tuple-element.26), channel_id=1, source_target_pairs={{0,16},{8,24},{16,0},{24,8},{32,48},{40,56},{48,32},{56,40},{64,80... | collective-permute-start | bytes 61448 | tf_op jit(solution)/shard_map/ppermute | solution.py:311
  57.7 3.0 %collective-permute-start.15 = (f32[5,8,128]{2,1,0:T(8,128)S(1)}, f32[5,8,128]{2,1,0:T(8,128)S(1)}, u32[]{:S(2)}, u32[]{:S(2)}) collective-permute-start(f32[5,8,128]{2,1,0:T(8,128)S(1)} %get-tuple-element.26), channel_id=1, source_target_pairs={{0,8},{8,0},{16,24},{24,16},{32,40},{40,32},{48,56},{56,48},{64,72... | collective-permute-start | bytes 61448 | tf_op jit(solution)/shard_map/ppermute | solution.py:311
  60.7 5.8 %collective-permute-start.20 = (f32[5,8,128]{2,1,0:T(8,128)S(1)}, f32[5,8,128]{2,1,0:T(8,128)S(1)}, u32[]{:S(2)}, u32[]{:S(2)}) collective-permute-start(f32[5,8,128]{2,1,0:T(8,128)S(1)} %add_add_fusion.1), channel_id=1, source_target_pairs={{0,96},{8,104},{16,112},{24,120},{32,64},{40,72},{48,80},{56,88},{... | collective-permute-start | bytes 61448 | tf_op jit(solution)/shard_map/ppermute | solution.py:311
  62.8 4.7 %collective-permute-start.19 = (f32[5,8,128]{2,1,0:T(8,128)S(1)}, f32[5,8,128]{2,1,0:T(8,128)S(1)}, u32[]{:S(2)}, u32[]{:S(2)}) collective-permute-start(f32[5,8,128]{2,1,0:T(8,128)S(1)} %add_add_fusion.1), channel_id=1, source_target_pairs={{0,64},{8,72},{16,80},{24,88},{32,96},{40,104},{48,112},{56,120},{... | collective-permute-start | bytes 61448 | tf_op jit(solution)/shard_map/ppermute | solution.py:311
  64.4 3.8 %collective-permute-start.18 = (f32[5,8,128]{2,1,0:T(8,128)S(1)}, f32[5,8,128]{2,1,0:T(8,128)S(1)}, u32[]{:S(2)}, u32[]{:S(2)}) collective-permute-start(f32[5,8,128]{2,1,0:T(8,128)S(1)} %add_add_fusion.1), channel_id=1, source_target_pairs={{0,32},{8,40},{16,48},{24,56},{32,0},{40,8},{48,16},{56,24},{64,96... | collective-permute-start | bytes 61448 | tf_op jit(solution)/shard_map/ppermute | solution.py:311
  68.2 5.7 %collective-permute-start.21 = (f32[5,8,128]{2,1,0:T(8,128)S(1)}, f32[5,8,128]{2,1,0:T(8,128)S(1)}, u32[]{:S(2)}, u32[]{:S(2)}) collective-permute-start(f32[5,8,128]{2,1,0:T(8,128)S(1)} %add_add_fusion), channel_id=1, source_target_pairs={{0,224},{8,232},{16,240},{24,248},{32,192},{40,200},{48,208},{56,2... | collective-permute-start | bytes 61448 | tf_op jit(solution)/shard_map/ppermute | solution.py:311

commit v4 on v3

--- a/solution.py
+++ b/solution.py
@@ -24,7 +24,6 @@
 LANES = 128
 TILE = (8, LANES)
 ROWS = PLANES * NY
-SPLIT = (PLANES, 2, COUNT, LANES)
 
 
 def point(index):
@@ -76,24 +75,24 @@
     return tiles
 
 
-def pack_kernel(vel_ref, in_ref, up_out, down_out, split):
+def native_rows(half, ix, plane, yhalf):
+    return pl.ds((half * CX + ix) * 8 + yhalf * 4 + plane, CZ, stride=2 * CX * 8)
+
+
+def pack_kernel(half, vel_ref, in_ref, out):
     device = Device(vel_ref[0])
     lane = iota(1)
     y, z = lane % 8, lane // 8
     source = jnp.where(device.ypos, y, 7 - y) * 16 + jnp.where(device.zpos, z, 15 - z)
     for plane in range(PLANES):
         for yhalf in (0, 1):
-            split[plane, yhalf] = in_ref[plane, :, yhalf * LANES : (yhalf + 1) * LANES]
-    for plane in range(PLANES):
-        for yhalf in (0, 1):
             base = device.base(yhalf)
-            for half, out in ((0, down_out), (1, up_out)):
-                tiles = []
-                for ix in range(CX):
-                    rows = pl.ds(half * CX + ix, CZ, stride=2 * CX)
-                    tiles.append(permuted(split[plane, yhalf, rows, :], source))
-                for j, tile in enumerate(swapped(tiles)):
-                    out[plane, base + j] = tile
+            tiles = [
+                permuted(in_ref[native_rows(half, ix, plane, yhalf), :], source)
+                for ix in range(CX)
+            ]
+            for j, tile in enumerate(swapped(tiles)):
+                out[plane, base + j] = tile
 
 
 def stream_kernel(vel_ref, up0, up1, up2, down0, down1, down2, up_out, down_out, mom_out, *scratch):
@@ -167,7 +166,7 @@
 
 
 def relax_kernel(last, vel_ref, mom_ref, up_in, down_in, *outs_and_scratch):
-    *outs, rows, split = outs_and_scratch
+    *outs, rows = outs_and_scratch
     device = Device(vel_ref[0])
     rho = mom_ref[0]
     ux = mom_ref[1] / rho
@@ -236,12 +235,7 @@
             if last:
                 for half in (0, 1):
                     for ix, tile in enumerate(swapped(values[half])):
-                        where = pl.ds(half * CX + ix, CZ, stride=2 * CX)
-                        split[plane, yhalf, where, :] = permuted(tile, back)
-    if last:
-        for plane in range(PLANES):
-            for yhalf in (0, 1):
-                outs[0][plane, :, yhalf * LANES : (yhalf + 1) * LANES] = split[plane, yhalf]
+                        outs[0][native_rows(half, ix, plane, yhalf), :] = permuted(tile, back)
 
 
 def vmem():
@@ -272,8 +266,12 @@
     return (count, NY, CZ, LANES)
 
 
-def pack(vel, field):
-    return call(pack_kernel, "pack", [shape(*planes(PLANES))] * 2, [SPLIT], vel, field)
+def pack(vel, field, half):
+    def body(*refs):
+        pack_kernel(half, *refs)
+
+    name = "pack_up" if half else "pack_down"
+    return call(body, name, [shape(*planes(PLANES))], [], vel, field)[0]
 
 
 def stream(vel, up, down):
@@ -290,7 +288,7 @@
 
 def relax(vel, moments, up, down, last):
     if last:
-        out_shape = [shape(PLANES, COUNT, 2 * LANES)]
+        out_shape = [shape(8 * COUNT, LANES)]
     else:
         out_shape = [shape(*planes(PLANES))] * 2 + [shape(*planes(2))] * 2
 
@@ -298,7 +296,7 @@
         relax_kernel(last, *refs)
 
     name = "relax_last" if last else "relax"
-    return call(body, name, out_shape, [(5, ROWS, LANES), SPLIT], vel, moments, up, down)
+    return call(body, name, out_shape, [(5, ROWS, LANES)], vel, moments, up, down)
 
 
 def passed_along(value, by):
@@ -319,7 +317,9 @@
 
 def on_device(distribution):
     vel = lax.axis_index("vel").astype(jnp.int32).reshape(1)
-    up, down = pack(vel, distribution.transpose(1, 0, 2))
+    field = distribution.reshape(COUNT, PLANES, 2, LANES).transpose(0, 2, 1, 3)
+    field = field.reshape(8 * COUNT, LANES)
+    up, down = pack(vel, field, 1), pack(vel, field, 0)
     up_far, down_far = up[2:], down[:2]
     for step in range(COLLISIONS):
         ups = (up, passed_along(up, 1), passed_along(up_far, 2))
@@ -329,7 +329,8 @@
         outs = relax(vel, moments, up_read, down_read, step == COLLISIONS - 1)
         if step < COLLISIONS - 1:
             down, up, down_far, up_far = outs
-    return outs[0].transpose(1, 0, 2)
+    field = outs[0].reshape(COUNT, 2, PLANES, LANES).transpose(0, 2, 1, 3)
+    return field.reshape(distribution.shape)
 
 
 def solution(mesh):

time: 77.9 us -> 75.9 us (0.974)
  local copies, waits for them, and re-layouts: 2.3 us -> 1.06 us
    transpose x1 -> x0, local copies, waits for them, and re-layouts: 1.13 us -> none  [on_device(): return outs[0].transpose(1, 0, 2)]
    pallas_call x5 -> x6, Pallas kernels: 8.54 us -> 8.39 us  [call(): pl.pallas_call(body, in_specs=[smem()] + [vmem()] * len(operands), out_sp...]
  transfers between devices with their start and end apart: 22 -> 22, of which waited for: 14 -> 14; matrix products, arithmetic and copies ran while one was open for 0% -> 0% of each run, Pallas kernels for 0% -> 1%
where the time goes in v4:
time: 75.9 us; the launch traced here: 74.4 us
  starting transfers between devices  33.5 us (44%)
  waiting for transfers between devices  31.3 us (41%)
  Pallas kernels  8.39 us (11%)
  local copies, waits for them, and re-layouts  1.06 us (1%)
    ppermute x14, starting transfers between devices, swapped_over(): return lax.ppermute(value, 'vel', [(i, partner(i)) for i in range(size)])  20.8 us
    ppermute x8, waiting for transfers between devices, passed_along(): lax.ppermute(value, 'gx', [(i, (i + by) % size) for i in range(size)])  16.4 us
    ppermute x14, waiting for transfers between devices, swapped_over(): return lax.ppermute(value, 'vel', [(i, partner(i)) for i in range(size)])  14.9 us
    ppermute x8, starting transfers between devices, passed_along(): lax.ppermute(value, 'gx', [(i, (i + by) % size) for i in range(size)])  12.7 us
    pallas_call x6, Pallas kernels, call(): pl.pallas_call(body, in_specs=[smem()] + [vmem()] * len(operands), out_sp...  8.39 us
  transfers between devices with their start and end apart: 22, of which 14 were waited for; matrix products, arithmetic and copies ran while one was open for 0% of the time, Pallas kernels for 1%

profile of v4, /device:TPU:30, one launch (start us, length us, event | category | flops | bytes accessed | tf_op | source)
XLA Modules:
  0.0 74.4 jit_solution(6277782396715669463)
XLA Ops:
  0.0 1.0 %copy-done = f32[128,4,256]{2,1,0:T(4,128)S(1)} copy-done((f32[128,4,256]{2,1,0:T(4,128)S(1)}, f32[128,4,256]{2,1,0:T(4,128)}, u32[]{:S(2)}) %copy-start) | copy-done | bytes 524312
  1.0 0.5 pack_up.1.up0
  1.6 1.1 %collective-permute-start = (f32[4,16,8,128]{3,2,1,0:T(8,128)S(1)}, f32[4,16,8,128]{3,2,1,0:T(8,128)S(1)}, u32[]{:S(2)}, u32[]{:S(2)}) collective-permute-start(f32[4,16,8,128]{3,2,1,0:T(8,128)S(1)} %pack_up.1.up0), channel_id=1, source_target_pairs={{0,1},{1,2},{2,3},{3,4},{4,5},{5,6},{6,7},{7,0},{8,9},{9,10},{10,1... | collective-permute-start | bytes 786440 | tf_op jit(solution)/shard_map/ppermute | solution.py:304
  2.7 0.5 pack_down.1.down0
  3.3 2.5 %collective-permute-start.2 = (f32[4,16,8,128]{3,2,1,0:T(8,128)S(1)}, f32[4,16,8,128]{3,2,1,0:T(8,128)S(1)}, u32[]{:S(2)}, u32[]{:S(2)}) collective-permute-start(f32[4,16,8,128]{3,2,1,0:T(8,128)S(1)} %pack_down.1.down0), channel_id=1, source_target_pairs={{0,7},{1,0},{2,1},{3,2},{4,3},{5,4},{6,5},{7,6},{8,15},{9,8},{10,9... | collective-permute-start | bytes 786440 | tf_op jit(solution)/shard_map/ppermute | solution.py:304
  5.8 0.8 %collective-permute-start.3 = (f32[2,16,8,128]{3,2,1,0:T(8,128)S(1)}, f32[2,16,8,128]{3,2,1,0:T(8,128)S(1)}, u32[]{:S(2)}, u32[]{:S(2)}) collective-permute-start(f32[2,16,8,128]{3,2,1,0:T(8,128)S(1)} %slice.9), channel_id=1, source_target_pairs={{0,6},{1,7},{2,0},{3,1},{4,2},{5,3},{6,4},{7,5},{8,14},{9,15},{10,... | collective-permute-start | bytes 393224 | tf_op jit(solution)/shard_map/ppermute | solution.py:304
  6.7 2.6 %collective-permute-start.1 = (f32[2,16,8,128]{3,2,1,0:T(8,128)S(1)}, f32[2,16,8,128]{3,2,1,0:T(8,128)S(1)}, u32[]{:S(2)}, u32[]{:S(2)}) collective-permute-start(f32[2,16,8,128]{3,2,1,0:T(8,128)S(1)} %slice.8), channel_id=1, source_target_pairs={{0,2},{1,3},{2,4},{3,5},{4,6},{5,7},{6,0},{7,1},{8,10},{9,11},{10,... | collective-permute-start | bytes 393224 | tf_op jit(solution)/shard_map/ppermute | solution.py:304
  9.2 8.2 %collective-permute-done.3.down2 = f32[2,16,8,128]{3,2,1,0:T(8,128)S(1)} collective-permute-done((f32[2,16,8,128]{3,2,1,0:T(8,128)S(1)}, f32[2,16,8,128]{3,2,1,0:T(8,128)S(1)}, u32[]{:S(2)}, u32[]{:S(2)}) %collective-permute-start.3) | collective-permute-done | bytes 131104 | tf_op jit(solution)/shard_map/ppermute | solution.py:304
  17.4 0.0 collective-permute-done.1.up2
  17.4 0.0 collective-permute-done.up1
  17.4 0.0 collective-permute-done.2.down1
  17.4 2.3 %stream.2 = (f32[4,16,8,128]{3,2,1,0:T(8,128)S(1)}, f32[4,16,8,128]{3,2,1,0:T(8,128)S(1)}, f32[5,8,128]{2,1,0:T(8,128)S(1)}) custom-call(s32[1]{0:T(128)} %bitcast.refs_0_.vel_ref, f32[4,16,8,128]{3,2,1,0:T(8,128)S(1)} %pack_up.1.up0, f32[4,16,8,128]{3,2,1,0:T(8,128)S(1)} %collective-permute-done.up1, f32[2,16,8,128]{3,2,1,0:T(8,128)S(1)} %collective-permute-done.1.up2, ...), custom_call_target="tpu_custom_call" | custom-call | tf_op jit(solution)/shard_map/stream/pallas_call | solution.py:254
  19.7 0.0 collective-permute-start.6
  19.7 0.9 %collective-permute-start.5 = (f32[5,8,128]{2,1,0:T(8,128)S(1)}, f32[5,8,128]{2,1,0:T(8,128)S(1)}, u32[]{:S(2)}, u32[]{:S(2)}) collective-permute-start(f32[5,8,128]{2,1,0:T(8,128)S(1)} %get-tuple-element.15), channel_id=1, source_target_pairs={{0,16},{8,24},{16,0},{24,8},{32,48},{40,56},{48,32},{56,40},{64,80... | collective-permute-start | bytes 61448 | tf_op jit(solution)/shard_map/ppermute | solution.py:309
  20.7 0.9 %collective-permute-start.4 = (f32[5,8,128]{2,1,0:T(8,128)S(1)}, f32[5,8,128]{2,1,0:T(8,128)S(1)}, u32[]{:S(2)}, u32[]{:S(2)}) collective-permute-start(f32[5,8,128]{2,1,0:T(8,128)S(1)} %get-tuple-element.15), channel_id=1, source_target_pairs={{0,8},{8,0},{16,24},{24,16},{32,40},{40,32},{48,56},{56,48},{64,72... | collective-permute-start | bytes 61448 | tf_op jit(solution)/shard_map/ppermute | solution.py:309
  21.6 1.3 %collective-permute-done.6 = f32[5,8,128]{2,1,0:T(8,128)S(1)} collective-permute-done((f32[5,8,128]{2,1,0:T(8,128)S(1)}, f32[5,8,128]{2,1,0:T(8,128)S(1)}, u32[]{:S(2)}, u32[]{:S(2)}) %collective-permute-start.6) | collective-permute-done | bytes 20512 | tf_op jit(solution)/shard_map/ppermute | solution.py:309
  22.9 0.8 %collective-permute-done.5 = f32[5,8,128]{2,1,0:T(8,128)S(1)} collective-permute-done((f32[5,8,128]{2,1,0:T(8,128)S(1)}, f32[5,8,128]{2,1,0:T(8,128)S(1)}, u32[]{:S(2)}, u32[]{:S(2)}) %collective-permute-start.5) | collective-permute-done | bytes 20512 | tf_op jit(solution)/shard_map/ppermute | solution.py:309
  23.7 4.7 %collective-permute-start.9 = (f32[5,8,128]{2,1,0:T(8,128)S(1)}, f32[5,8,128]{2,1,0:T(8,128)S(1)}, u32[]{:S(2)}, u32[]{:S(2)}) collective-permute-start(f32[5,8,128]{2,1,0:T(8,128)S(1)} %add_add_fusion.3), channel_id=1, source_target_pairs={{0,96},{8,104},{16,112},{24,120},{32,64},{40,72},{48,80},{56,88},{... | collective-permute-start | bytes 61448 | tf_op jit(solution)/shard_map/ppermute | solution.py:309
  28.4 0.0 collective-permute-start.8
  28.4 0.7 collective-permute-start.7
  29.1 1.1 %collective-permute-done.9 = f32[5,8,128]{2,1,0:T(8,128)S(1)} collective-permute-done((f32[5,8,128]{2,1,0:T(8,128)S(1)}, f32[5,8,128]{2,1,0:T(8,128)S(1)}, u32[]{:S(2)}, u32[]{:S(2)}) %collective-permute-start.9) | collective-permute-done | bytes 20512 | tf_op jit(solution)/shard_map/ppermute | solution.py:309
  30.2 2.9 %collective-permute-done.8 = f32[5,8,128]{2,1,0:T(8,128)S(1)} collective-permute-done((f32[5,8,128]{2,1,0:T(8,128)S(1)}, f32[5,8,128]{2,1,0:T(8,128)S(1)}, u32[]{:S(2)}, u32[]{:S(2)}) %collective-permute-start.8) | collective-permute-done | bytes 20512 | tf_op jit(solution)/shard_map/ppermute | solution.py:309
  33.1 3.2 %collective-permute-start.10 = (f32[5,8,128]{2,1,0:T(8,128)S(1)}, f32[5,8,128]{2,1,0:T(8,128)S(1)}, u32[]{:S(2)}, u32[]{:S(2)}) collective-permute-start(f32[5,8,128]{2,1,0:T(8,128)S(1)} %add_add_fusion.2), channel_id=1, source_target_pairs={{0,224},{8,232},{16,240},{24,248},{32,192},{40,200},{48,208},{56,2... | collective-permute-start | bytes 61448 | tf_op jit(solution)/shard_map/ppermute | solution.py:309
  36.3 1.9 %collective-permute-done.10 = f32[5,8,128]{2,1,0:T(8,128)S(1)} collective-permute-done((f32[5,8,128]{2,1,0:T(8,128)S(1)}, f32[5,8,128]{2,1,0:T(8,128)S(1)}, u32[]{:S(2)}, u32[]{:S(2)}) %collective-permute-start.10) | collective-permute-done | bytes 20512 | tf_op jit(solution)/shard_map/ppermute | solution.py:309
  38.2 0.6 relax.1
  38.8 1.5 %collective-permute-start.11 = (f32[4,16,8,128]{3,2,1,0:T(8,128)S(1)}, f32[4,16,8,128]{3,2,1,0:T(8,128)S(1)}, u32[]{:S(2)}, u32[]{:S(2)}) collective-permute-start(f32[4,16,8,128]{3,2,1,0:T(8,128)S(1)} %get-tuple-element.18.up0), channel_id=1, source_target_pairs={{0,1},{1,2},{2,3},{3,4},{4,5},{5,6},{6,7},{7,0},{8,9},{9,10},{10,1... | collective-permute-start | bytes 786440 | tf_op jit(solution)/shard_map/ppermute | solution.py:304
  40.3 2.1 %collective-permute-start.13 = (f32[4,16,8,128]{3,2,1,0:T(8,128)S(1)}, f32[4,16,8,128]{3,2,1,0:T(8,128)S(1)}, u32[]{:S(2)}, u32[]{:S(2)}) collective-permute-start(f32[4,16,8,128]{3,2,1,0:T(8,128)S(1)} %get-tuple-element.20.down0), channel_id=1, source_target_pairs={{0,7},{1,0},{2,1},{3,2},{4,3},{5,4},{6,5},{7,6},{8,15},{9,8},{10,9... | collective-permute-start | bytes 786440 | tf_op jit(solution)/shard_map/ppermute | solution.py:304
  42.4 0.6 collective-permute-start.12
  43.1 1.4 %collective-permute-start.14 = (f32[2,16,8,128]{3,2,1,0:T(8,128)S(1)}, f32[2,16,8,128]{3,2,1,0:T(8,128)S(1)}, u32[]{:S(2)}, u32[]{:S(2)}) collective-permute-start(f32[2,16,8,128]{3,2,1,0:T(8,128)S(1)} %get-tuple-element.21), channel_id=1, source_target_pairs={{0,6},{1,7},{2,0},{3,1},{4,2},{5,3},{6,4},{7,5},{8,14},{9,15},{10,... | collective-permute-start | bytes 393224 | tf_op jit(solution)/shard_map/ppermute | solution.py:304
  44.4 2.9 %collective-permute-done.12.up2 = f32[2,16,8,128]{3,2,1,0:T(8,128)S(1)} collective-permute-done((f32[2,16,8,128]{3,2,1,0:T(8,128)S(1)}, f32[2,16,8,128]{3,2,1,0:T(8,128)S(1)}, u32[]{:S(2)}, u32[]{:S(2)}) %collective-permute-start.12) | collective-permute-done | bytes 131104 | tf_op jit(solution)/shard_map/ppermute | solution.py:304
  47.4 5.3 %collective-permute-done.14.down2 = f32[2,16,8,128]{3,2,1,0:T(8,128)S(1)} collective-permute-done((f32[2,16,8,128]{3,2,1,0:T(8,128)S(1)}, f32[2,16,8,128]{3,2,1,0:T(8,128)S(1)}, u32[]{:S(2)}, u32[]{:S(2)}) %collective-permute-start.14) | collective-permute-done | bytes 131104 | tf_op jit(solution)/shard_map/ppermute | solution.py:304
  52.7 0.0 collective-permute-done.11.up1
  52.7 0.0 collective-permute-done.13.down1
  52.7 2.3 %stream.3 = (f32[4,16,8,128]{3,2,1,0:T(8,128)S(1)}, f32[4,16,8,128]{3,2,1,0:T(8,128)S(1)}, f32[5,8,128]{2,1,0:T(8,128)S(1)}) custom-call(s32[1]{0:T(128)} %bitcast.refs_0_.vel_ref, f32[4,16,8,128]{3,2,1,0:T(8,128)S(1)} %get-tuple-element.18.up0, f32[4,16,8,128]{3,2,1,0:T(8,128)S(1)} %collective-permute-done.11.up1, ...), custom_call_target="tpu_custom_call" | custom-call | tf_op jit(solution)/shard_map/stream/pallas_call | solution.py:254
  55.0 0.0 collective-permute-start.17
  55.0 1.0 %collective-permute-start.16 = (f32[5,8,128]{2,1,0:T(8,128)S(1)}, f32[5,8,128]{2,1,0:T(8,128)S(1)}, u32[]{:S(2)}, u32[]{:S(2)}) collective-permute-start(f32[5,8,128]{2,1,0:T(8,128)S(1)} %get-tuple-element.22), channel_id=1, source_target_pairs={{0,16},{8,24},{16,0},{24,8},{32,48},{40,56},{48,32},{56,40},{64,80... | collective-permute-start | bytes 61448 | tf_op jit(solution)/shard_map/ppermute | solution.py:309
  56.0 0.9 %collective-permute-start.15 = (f32[5,8,128]{2,1,0:T(8,128)S(1)}, f32[5,8,128]{2,1,0:T(8,128)S(1)}, u32[]{:S(2)}, u32[]{:S(2)}) collective-permute-start(f32[5,8,128]{2,1,0:T(8,128)S(1)} %get-tuple-element.22), channel_id=1, source_target_pairs={{0,8},{8,0},{16,24},{24,16},{32,40},{40,32},{48,56},{56,48},{64,72... | collective-permute-start | bytes 61448 | tf_op jit(solution)/shard_map/ppermute | solution.py:309
  56.9 1.3 %collective-permute-done.17 = f32[5,8,128]{2,1,0:T(8,128)S(1)} collective-permute-done((f32[5,8,128]{2,1,0:T(8,128)S(1)}, f32[5,8,128]{2,1,0:T(8,128)S(1)}, u32[]{:S(2)}, u32[]{:S(2)}) %collective-permute-start.17) | collective-permute-done | bytes 20512 | tf_op jit(solution)/shard_map/ppermute | solution.py:309
  58.2 0.8 %collective-permute-done.16 = f32[5,8,128]{2,1,0:T(8,128)S(1)} collective-permute-done((f32[5,8,128]{2,1,0:T(8,128)S(1)}, f32[5,8,128]{2,1,0:T(8,128)S(1)}, u32[]{:S(2)}, u32[]{:S(2)}) %collective-permute-start.16) | collective-permute-done | bytes 20512 | tf_op jit(solution)/shard_map/ppermute | solution.py:309
  59.1 2.1 %collective-permute-start.20 = (f32[5,8,128]{2,1,0:T(8,128)S(1)}, f32[5,8,128]{2,1,0:T(8,128)S(1)}, u32[]{:S(2)}, u32[]{:S(2)}) collective-permute-start(f32[5,8,128]{2,1,0:T(8,128)S(1)} %add_add_fusion.1), channel_id=1, source_target_pairs={{0,96},{8,104},{16,112},{24,120},{32,64},{40,72},{48,80},{56,88},{... | collective-permute-start | bytes 61448 | tf_op jit(solution)/shard_map/ppermute | solution.py:309
  61.2 1.6 %collective-permute-start.19 = (f32[5,8,128]{2,1,0:T(8,128)S(1)}, f32[5,8,128]{2,1,0:T(8,128)S(1)}, u32[]{:S(2)}, u32[]{:S(2)}) collective-permute-start(f32[5,8,128]{2,1,0:T(8,128)S(1)} %add_add_fusion.1), channel_id=1, source_target_pairs={{0,64},{8,72},{16,80},{24,88},{32,96},{40,104},{48,112},{56,120},{... | collective-permute-start | bytes 61448 | tf_op jit(solution)/shard_map/ppermute | solution.py:309
  62.8 0.8 %collective-permute-start.18 = (f32[5,8,128]{2,1,0:T(8,128)S(1)}, f32[5,8,128]{2,1,0:T(8,128)S(1)}, u32[]{:S(2)}, u32[]{:S(2)}) collective-permute-start(f32[5,8,128]{2,1,0:T(8,128)S(1)} %add_add_fusion.1), channel_id=1, source_target_pairs={{0,32},{8,40},{16,48},{24,56},{32,0},{40,8},{48,16},{56,24},{64,96... | collective-permute-start | bytes 61448 | tf_op jit(solution)/shard_map/ppermute | solution.py:309
  63.6 1.3 %collective-permute-done.20 = f32[5,8,128]{2,1,0:T(8,128)S(1)} collective-permute-done((f32[5,8,128]{2,1,0:T(8,128)S(1)}, f32[5,8,128]{2,1,0:T(8,128)S(1)}, u32[]{:S(2)}, u32[]{:S(2)}) %collective-permute-start.20) | collective-permute-done | bytes 20512 | tf_op jit(solution)/shard_map/ppermute | solution.py:309
  64.8 1.0 %collective-permute-done.19 = f32[5,8,128]{2,1,0:T(8,128)S(1)} collective-permute-done((f32[5,8,128]{2,1,0:T(8,128)S(1)}, f32[5,8,128]{2,1,0:T(8,128)S(1)}, u32[]{:S(2)}, u32[]{:S(2)}) %collective-permute-start.19) | collective-permute-done | bytes 20512 | tf_op jit(solution)/shard_map/ppermute | solution.py:309
  65.8 0.7 collective-permute-done.18
  66.6 3.9 %collective-permute-start.21 = (f32[5,8,128]{2,1,0:T(8,128)S(1)}, f32[5,8,128]{2,1,0:T(8,128)S(1)}, u32[]{:S(2)}, u32[]{:S(2)}) collective-permute-start(f32[5,8,128]{2,1,0:T(8,128)S(1)} %add_add_fusion), channel_id=1, source_target_pairs={{0,224},{8,232},{16,240},{24,248},{32,192},{40,200},{48,208},{56,2... | collective-permute-start | bytes 61448 | tf_op jit(solution)/shard_map/ppermute | solution.py:309
  70.5 1.8 %collective-permute-done.21 = f32[5,8,128]{2,1,0:T(8,128)S(1)} collective-permute-done((f32[5,8,128]{2,1,0:T(8,128)S(1)}, f32[5,8,128]{2,1,0:T(8,128)S(1)}, u32[]{:S(2)}, u32[]{:S(2)}) %collective-permute-start.21) | collective-permute-done | bytes 20512 | tf_op jit(solution)/shard_map/ppermute | solution.py:309
  72.3 2.1 %relax_last.1 = f32[1024,128]{1,0:T(8,128)} custom-call(s32[1]{0:T(128)} %bitcast.refs_0_.vel_ref, f32[5,8,128]{2,1,0:T(8,128)S(1)} %add.55.refs_1_, f32[4,16,8,128]{3,2,1,0:T(8,128)S(1)} %get-tuple-element.23.refs_2_, f32[4,16,8,128]{3,2,1,0:T(8,128)S(1)} %get-tuple-element.24.refs_3_), custom_call_target="tpu_custom_call" | custom-call | tf_op jit(solution)/shard_map/relax_last/pallas_call | solution.py:254
  (12 shorter events, 0.1 us)
Async XLA Ops:
  0.0 1.0 %copy-start = (f32[128,4,256]{2,1,0:T(4,128)S(1)}, f32[128,4,256]{2,1,0:T(4,128)}, u32[]{:S(2)}) copy-start(f32[128,4,256]{2,1,0:T(4,128)} %param.1) | copy-start | bytes 1572868
  1.6 15.8 %collective-permute-start = (f32[4,16,8,128]{3,2,1,0:T(8,128)S(1)}, f32[4,16,8,128]{3,2,1,0:T(8,128)S(1)}, u32[]{:S(2)}, u32[]{:S(2)}) collective-permute-start(f32[4,16,8,128]{3,2,1,0:T(8,128)S(1)} %pack_up.1.up0), channel_id=1, source_target_pairs={{0,1},{1,2},{2,3},{3,4},{4,5},{5,6},{6,7},{7,0},{8,9},{9,10},{10,1... | collective-permute-start | bytes 786440 | tf_op jit(solution)/shard_map/ppermute | solution.py:304
  3.3 14.1 %collective-permute-start.2 = (f32[4,16,8,128]{3,2,1,0:T(8,128)S(1)}, f32[4,16,8,128]{3,2,1,0:T(8,128)S(1)}, u32[]{:S(2)}, u32[]{:S(2)}) collective-permute-start(f32[4,16,8,128]{3,2,1,0:T(8,128)S(1)} %pack_down.1.down0), channel_id=1, source_target_pairs={{0,7},{1,0},{2,1},{3,2},{4,3},{5,4},{6,5},{7,6},{8,15},{9,8},{10,9... | collective-permute-start | bytes 786440 | tf_op jit(solution)/shard_map/ppermute | solution.py:304
  5.8 11.6 %collective-permute-start.3 = (f32[2,16,8,128]{3,2,1,0:T(8,128)S(1)}, f32[2,16,8,128]{3,2,1,0:T(8,128)S(1)}, u32[]{:S(2)}, u32[]{:S(2)}) collective-permute-start(f32[2,16,8,128]{3,2,1,0:T(8,128)S(1)} %slice.9), channel_id=1, source_target_pairs={{0,6},{1,7},{2,0},{3,1},{4,2},{5,3},{6,4},{7,5},{8,14},{9,15},{10,... | collective-permute-start | bytes 393224 | tf_op jit(solution)/shard_map/ppermute | solution.py:304
  6.7 10.8 %collective-permute-start.1 = (f32[2,16,8,128]{3,2,1,0:T(8,128)S(1)}, f32[2,16,8,128]{3,2,1,0:T(8,128)S(1)}, u32[]{:S(2)}, u32[]{:S(2)}) collective-permute-start(f32[2,16,8,128]{3,2,1,0:T(8,128)S(1)} %slice.8), channel_id=1, source_target_pairs={{0,2},{1,3},{2,4},{3,5},{4,6},{5,7},{6,0},{7,1},{8,10},{9,11},{10,... | collective-permute-start | bytes 393224 | tf_op jit(solution)/shard_map/ppermute | solution.py:304
  19.7 3.2 %collective-permute-start.6 = (f32[5,8,128]{2,1,0:T(8,128)S(1)}, f32[5,8,128]{2,1,0:T(8,128)S(1)}, u32[]{:S(2)}, u32[]{:S(2)}) collective-permute-start(f32[5,8,128]{2,1,0:T(8,128)S(1)} %get-tuple-element.15), channel_id=1, source_target_pairs={{0,24},{8,16},{16,8},{24,0},{32,56},{40,48},{48,40},{56,32},{64,88... | collective-permute-start | bytes 61448 | tf_op jit(solution)/shard_map/ppermute | solution.py:309
  19.7 4.0 %collective-permute-start.5 = (f32[5,8,128]{2,1,0:T(8,128)S(1)}, f32[5,8,128]{2,1,0:T(8,128)S(1)}, u32[]{:S(2)}, u32[]{:S(2)}) collective-permute-start(f32[5,8,128]{2,1,0:T(8,128)S(1)} %get-tuple-element.15), channel_id=1, source_target_pairs={{0,16},{8,24},{16,0},{24,8},{32,48},{40,56},{48,32},{56,40},{64,80... | collective-permute-start | bytes 61448 | tf_op jit(solution)/shard_map/ppermute | solution.py:309
  20.7 3.0 %collective-permute-start.4 = (f32[5,8,128]{2,1,0:T(8,128)S(1)}, f32[5,8,128]{2,1,0:T(8,128)S(1)}, u32[]{:S(2)}, u32[]{:S(2)}) collective-permute-start(f32[5,8,128]{2,1,0:T(8,128)S(1)} %get-tuple-element.15), channel_id=1, source_target_pairs={{0,8},{8,0},{16,24},{24,16},{32,40},{40,32},{48,56},{56,48},{64,72... | collective-permute-start | bytes 61448 | tf_op jit(solution)/shard_map/ppermute | solution.py:309
  23.7 6.5 %collective-permute-start.9 = (f32[5,8,128]{2,1,0:T(8,128)S(1)}, f32[5,8,128]{2,1,0:T(8,128)S(1)}, u32[]{:S(2)}, u32[]{:S(2)}) collective-permute-start(f32[5,8,128]{2,1,0:T(8,128)S(1)} %add_add_fusion.3), channel_id=1, source_target_pairs={{0,96},{8,104},{16,112},{24,120},{32,64},{40,72},{48,80},{56,88},{... | collective-permute-start | bytes 61448 | tf_op jit(solution)/shard_map/ppermute | solution.py:309
  28.4 4.7 %collective-permute-start.8 = (f32[5,8,128]{2,1,0:T(8,128)S(1)}, f32[5,8,128]{2,1,0:T(8,128)S(1)}, u32[]{:S(2)}, u32[]{:S(2)}) collective-permute-start(f32[5,8,128]{2,1,0:T(8,128)S(1)} %add_add_fusion.3), channel_id=1, source_target_pairs={{0,64},{8,72},{16,80},{24,88},{32,96},{40,104},{48,112},{56,120},{... | collective-permute-start | bytes 61448 | tf_op jit(solution)/shard_map/ppermute | solution.py:309
  28.4 4.7 %collective-permute-start.7 = (f32[5,8,128]{2,1,0:T(8,128)S(1)}, f32[5,8,128]{2,1,0:T(8,128)S(1)}, u32[]{:S(2)}, u32[]{:S(2)}) collective-permute-start(f32[5,8,128]{2,1,0:T(8,128)S(1)} %add_add_fusion.3), channel_id=1, source_target_pairs={{0,32},{8,40},{16,48},{24,56},{32,0},{40,8},{48,16},{56,24},{64,96... | collective-permute-start | bytes 61448 | tf_op jit(solution)/shard_map/ppermute | solution.py:309
  33.1 5.1 %collective-permute-start.10 = (f32[5,8,128]{2,1,0:T(8,128)S(1)}, f32[5,8,128]{2,1,0:T(8,128)S(1)}, u32[]{:S(2)}, u32[]{:S(2)}) collective-permute-start(f32[5,8,128]{2,1,0:T(8,128)S(1)} %add_add_fusion.2), channel_id=1, source_target_pairs={{0,224},{8,232},{16,240},{24,248},{32,192},{40,200},{48,208},{56,2... | collective-permute-start | bytes 61448 | tf_op jit(solution)/shard_map/ppermute | solution.py:309
  38.8 13.9 %collective-permute-start.11 = (f32[4,16,8,128]{3,2,1,0:T(8,128)S(1)}, f32[4,16,8,128]{3,2,1,0:T(8,128)S(1)}, u32[]{:S(2)}, u32[]{:S(2)}) collective-permute-start(f32[4,16,8,128]{3,2,1,0:T(8,128)S(1)} %get-tuple-element.18.up0), channel_id=1, source_target_pairs={{0,1},{1,2},{2,3},{3,4},{4,5},{5,6},{6,7},{7,0},{8,9},{9,10},{10,1... | collective-permute-start | bytes 786440 | tf_op jit(solution)/shard_map/ppermute | solution.py:304
  40.3 12.4 %collective-permute-start.13 = (f32[4,16,8,128]{3,2,1,0:T(8,128)S(1)}, f32[4,16,8,128]{3,2,1,0:T(8,128)S(1)}, u32[]{:S(2)}, u32[]{:S(2)}) collective-permute-start(f32[4,16,8,128]{3,2,1,0:T(8,128)S(1)} %get-tuple-element.20.down0), channel_id=1, source_target_pairs={{0,7},{1,0},{2,1},{3,2},{4,3},{5,4},{6,5},{7,6},{8,15},{9,8},{10,9... | collective-permute-start | bytes 786440 | tf_op jit(solution)/shard_map/ppermute | solution.py:304
  42.4 5.0 %collective-permute-start.12 = (f32[2,16,8,128]{3,2,1,0:T(8,128)S(1)}, f32[2,16,8,128]{3,2,1,0:T(8,128)S(1)}, u32[]{:S(2)}, u32[]{:S(2)}) collective-permute-start(f32[2,16,8,128]{3,2,1,0:T(8,128)S(1)} %get-tuple-element.19), channel_id=1, source_target_pairs={{0,2},{1,3},{2,4},{3,5},{4,6},{5,7},{6,0},{7,1},{8,10},{9,11},{10,... | collective-permute-start | bytes 393224 | tf_op jit(solution)/shard_map/ppermute | solution.py:304
  43.1 9.6 %collective-permute-start.14 = (f32[2,16,8,128]{3,2,1,0:T(8,128)S(1)}, f32[2,16,8,128]{3,2,1,0:T(8,128)S(1)}, u32[]{:S(2)}, u32[]{:S(2)}) collective-permute-start(f32[2,16,8,128]{3,2,1,0:T(8,128)S(1)} %get-tuple-element.21), channel_id=1, source_target_pairs={{0,6},{1,7},{2,0},{3,1},{4,2},{5,3},{6,4},{7,5},{8,14},{9,15},{10,... | collective-permute-start | bytes 393224 | tf_op jit(solution)/shard_map/ppermute | solution.py:304
  55.0 3.2 %collective-permute-start.17 = (f32[5,8,128]{2,1,0:T(8,128)S(1)}, f32[5,8,128]{2,1,0:T(8,128)S(1)}, u32[]{:S(2)}, u32[]{:S(2)}) collective-permute-start(f32[5,8,128]{2,1,0:T(8,128)S(1)} %get-tuple-element.22), channel_id=1, source_target_pairs={{0,24},{8,16},{16,8},{24,0},{32,56},{40,48},{48,40},{56,32},{64,88... | collective-permute-start | bytes 61448 | tf_op jit(solution)/shard_map/ppermute | solution.py:309
  55.0 4.0 %collective-permute-start.16 = (f32[5,8,128]{2,1,0:T(8,128)S(1)}, f32[5,8,128]{2,1,0:T(8,128)S(1)}, u32[]{:S(2)}, u32[]{:S(2)}) collective-permute-start(f32[5,8,128]{2,1,0:T(8,128)S(1)} %get-tuple-element.22), channel_id=1, source_target_pairs={{0,16},{8,24},{16,0},{24,8},{32,48},{40,56},{48,32},{56,40},{64,80... | collective-permute-start | bytes 61448 | tf_op jit(solution)/shard_map/ppermute | solution.py:309
  56.0 3.0 %collective-permute-start.15 = (f32[5,8,128]{2,1,0:T(8,128)S(1)}, f32[5,8,128]{2,1,0:T(8,128)S(1)}, u32[]{:S(2)}, u32[]{:S(2)}) collective-permute-start(f32[5,8,128]{2,1,0:T(8,128)S(1)} %get-tuple-element.22), channel_id=1, source_target_pairs={{0,8},{8,0},{16,24},{24,16},{32,40},{40,32},{48,56},{56,48},{64,72... | collective-permute-start | bytes 61448 | tf_op jit(solution)/shard_map/ppermute | solution.py:309
  59.1 5.8 %collective-permute-start.20 = (f32[5,8,128]{2,1,0:T(8,128)S(1)}, f32[5,8,128]{2,1,0:T(8,128)S(1)}, u32[]{:S(2)}, u32[]{:S(2)}) collective-permute-start(f32[5,8,128]{2,1,0:T(8,128)S(1)} %add_add_fusion.1), channel_id=1, source_target_pairs={{0,96},{8,104},{16,112},{24,120},{32,64},{40,72},{48,80},{56,88},{... | collective-permute-start | bytes 61448 | tf_op jit(solution)/shard_map/ppermute | solution.py:309
  61.2 4.7 %collective-permute-start.19 = (f32[5,8,128]{2,1,0:T(8,128)S(1)}, f32[5,8,128]{2,1,0:T(8,128)S(1)}, u32[]{:S(2)}, u32[]{:S(2)}) collective-permute-start(f32[5,8,128]{2,1,0:T(8,128)S(1)} %add_add_fusion.1), channel_id=1, source_target_pairs={{0,64},{8,72},{16,80},{24,88},{32,96},{40,104},{48,112},{56,120},{... | collective-permute-start | bytes 61448 | tf_op jit(solution)/shard_map/ppermute | solution.py:309
  62.8 3.8 %collective-permute-start.18 = (f32[5,8,128]{2,1,0:T(8,128)S(1)}, f32[5,8,128]{2,1,0:T(8,128)S(1)}, u32[]{:S(2)}, u32[]{:S(2)}) collective-permute-start(f32[5,8,128]{2,1,0:T(8,128)S(1)} %add_add_fusion.1), channel_id=1, source_target_pairs={{0,32},{8,40},{16,48},{24,56},{32,0},{40,8},{48,16},{56,24},{64,96... | collective-permute-start | bytes 61448 | tf_op jit(solution)/shard_map/ppermute | solution.py:309
  66.6 5.7 %collective-permute-start.21 = (f32[5,8,128]{2,1,0:T(8,128)S(1)}, f32[5,8,128]{2,1,0:T(8,128)S(1)}, u32[]{:S(2)}, u32[]{:S(2)}) collective-permute-start(f32[5,8,128]{2,1,0:T(8,128)S(1)} %add_add_fusion), channel_id=1, source_target_pairs={{0,224},{8,232},{16,240},{24,248},{32,192},{40,200},{48,208},{56,2... | collective-permute-start | bytes 61448 | tf_op jit(solution)/shard_map/ppermute | solution.py:309

commit v5 on v4

--- a/solution.py
+++ b/solution.py
@@ -310,7 +310,7 @@
 
 
 def summed_over_velocities(value):
-    for step in (1, 4):
+    for step in (4, 1):
         value = value + sum(swapped_over(value, lambda i, k=k: i ^ (step * k)) for k in (1, 2, 3))
     return value + swapped_over(value, lambda i: 4 * (7 - i // 4) + i % 4)
 

time: 75.9 us -> 77.5 us (1.021)
  waiting for transfers between devices: 31.3 us -> 33 us
    ppermute x8, waiting for transfers between devices: 16.4 us -> 17.6 us  [passed_along(): lax.ppermute(value, 'gx', [(i, (i + by) % size) for i in range(size)])]
where the time goes in v5:
time: 77.5 us; the launch traced here: 76 us
  starting transfers between devices  33.5 us (43%)
  waiting for transfers between devices  33 us (43%)
  Pallas kernels  8.39 us (11%)
  local copies, waits for them, and re-layouts  1.06 us (1%)
    ppermute x14, starting transfers between devices, swapped_over(): return lax.ppermute(value, 'vel', [(i, partner(i)) for i in range(size)])  20.8 us
    ppermute x8, waiting for transfers between devices, passed_along(): lax.ppermute(value, 'gx', [(i, (i + by) % size) for i in range(size)])  17.6 us
    ppermute x14, waiting for transfers between devices, swapped_over(): return lax.ppermute(value, 'vel', [(i, partner(i)) for i in range(size)])  15.4 us
    ppermute x8, starting transfers between devices, passed_along(): lax.ppermute(value, 'gx', [(i, (i + by) % size) for i in range(size)])  12.7 us
    pallas_call x6, Pallas kernels, call(): pl.pallas_call(body, in_specs=[smem()] + [vmem()] * len(operands), out_sp...  8.39 us
  transfers between devices with their start and end apart: 22, of which 14 were waited for; matrix products, arithmetic and copies ran while one was open for 0% of the time, Pallas kernels for 1%

profile of v5, /device:TPU:30, one launch (start us, length us, event | category | flops | bytes accessed | tf_op | source)
XLA Modules:
  0.0 76.0 jit_solution(2916661326704478960)
XLA Ops:
  0.0 1.0 %copy-done = f32[128,4,256]{2,1,0:T(4,128)S(1)} copy-done((f32[128,4,256]{2,1,0:T(4,128)S(1)}, f32[128,4,256]{2,1,0:T(4,128)}, u32[]{:S(2)}) %copy-start) | copy-done | bytes 524312
  1.0 0.5 pack_up.1.up0
  1.6 1.1 %collective-permute-start = (f32[4,16,8,128]{3,2,1,0:T(8,128)S(1)}, f32[4,16,8,128]{3,2,1,0:T(8,128)S(1)}, u32[]{:S(2)}, u32[]{:S(2)}) collective-permute-start(f32[4,16,8,128]{3,2,1,0:T(8,128)S(1)} %pack_up.1.up0), channel_id=1, source_target_pairs={{0,1},{1,2},{2,3},{3,4},{4,5},{5,6},{6,7},{7,0},{8,9},{9,10},{10,1... | collective-permute-start | bytes 786440 | tf_op jit(solution)/shard_map/ppermute | solution.py:304
  2.7 0.5 pack_down.1.down0
  3.3 2.5 %collective-permute-start.2 = (f32[4,16,8,128]{3,2,1,0:T(8,128)S(1)}, f32[4,16,8,128]{3,2,1,0:T(8,128)S(1)}, u32[]{:S(2)}, u32[]{:S(2)}) collective-permute-start(f32[4,16,8,128]{3,2,1,0:T(8,128)S(1)} %pack_down.1.down0), channel_id=1, source_target_pairs={{0,7},{1,0},{2,1},{3,2},{4,3},{5,4},{6,5},{7,6},{8,15},{9,8},{10,9... | collective-permute-start | bytes 786440 | tf_op jit(solution)/shard_map/ppermute | solution.py:304
  5.8 0.8 %collective-permute-start.3 = (f32[2,16,8,128]{3,2,1,0:T(8,128)S(1)}, f32[2,16,8,128]{3,2,1,0:T(8,128)S(1)}, u32[]{:S(2)}, u32[]{:S(2)}) collective-permute-start(f32[2,16,8,128]{3,2,1,0:T(8,128)S(1)} %slice.9), channel_id=1, source_target_pairs={{0,6},{1,7},{2,0},{3,1},{4,2},{5,3},{6,4},{7,5},{8,14},{9,15},{10,... | collective-permute-start | bytes 393224 | tf_op jit(solution)/shard_map/ppermute | solution.py:304
  6.7 2.6 %collective-permute-start.1 = (f32[2,16,8,128]{3,2,1,0:T(8,128)S(1)}, f32[2,16,8,128]{3,2,1,0:T(8,128)S(1)}, u32[]{:S(2)}, u32[]{:S(2)}) collective-permute-start(f32[2,16,8,128]{3,2,1,0:T(8,128)S(1)} %slice.8), channel_id=1, source_target_pairs={{0,2},{1,3},{2,4},{3,5},{4,6},{5,7},{6,0},{7,1},{8,10},{9,11},{10,... | collective-permute-start | bytes 393224 | tf_op jit(solution)/shard_map/ppermute | solution.py:304
  9.2 8.2 %collective-permute-done.3.down2 = f32[2,16,8,128]{3,2,1,0:T(8,128)S(1)} collective-permute-done((f32[2,16,8,128]{3,2,1,0:T(8,128)S(1)}, f32[2,16,8,128]{3,2,1,0:T(8,128)S(1)}, u32[]{:S(2)}, u32[]{:S(2)}) %collective-permute-start.3) | collective-permute-done | bytes 131104 | tf_op jit(solution)/shard_map/ppermute | solution.py:304
  17.4 0.0 collective-permute-done.1.up2
  17.4 0.0 collective-permute-done.up1
  17.4 0.0 collective-permute-done.2.down1
  17.4 2.3 %stream.2 = (f32[4,16,8,128]{3,2,1,0:T(8,128)S(1)}, f32[4,16,8,128]{3,2,1,0:T(8,128)S(1)}, f32[5,8,128]{2,1,0:T(8,128)S(1)}) custom-call(s32[1]{0:T(128)} %bitcast.refs_0_.vel_ref, f32[4,16,8,128]{3,2,1,0:T(8,128)S(1)} %pack_up.1.up0, f32[4,16,8,128]{3,2,1,0:T(8,128)S(1)} %collective-permute-done.up1, f32[2,16,8,128]{3,2,1,0:T(8,128)S(1)} %collective-permute-done.1.up2, ...), custom_call_target="tpu_custom_call" | custom-call | tf_op jit(solution)/shard_map/stream/pallas_call | solution.py:254
  19.7 4.7 %collective-permute-start.6 = (f32[5,8,128]{2,1,0:T(8,128)S(1)}, f32[5,8,128]{2,1,0:T(8,128)S(1)}, u32[]{:S(2)}, u32[]{:S(2)}) collective-permute-start(f32[5,8,128]{2,1,0:T(8,128)S(1)} %get-tuple-element.15), channel_id=1, source_target_pairs={{0,96},{8,104},{16,112},{24,120},{32,64},{40,72},{48,80},{56,88},{... | collective-permute-start | bytes 61448 | tf_op jit(solution)/shard_map/ppermute | solution.py:309
  24.3 0.0 collective-permute-start.5
  24.3 0.7 collective-permute-start.4
  25.0 1.1 %collective-permute-done.6 = f32[5,8,128]{2,1,0:T(8,128)S(1)} collective-permute-done((f32[5,8,128]{2,1,0:T(8,128)S(1)}, f32[5,8,128]{2,1,0:T(8,128)S(1)}, u32[]{:S(2)}, u32[]{:S(2)}) %collective-permute-start.6) | collective-permute-done | bytes 20512 | tf_op jit(solution)/shard_map/ppermute | solution.py:309
  26.1 2.9 %collective-permute-done.5 = f32[5,8,128]{2,1,0:T(8,128)S(1)} collective-permute-done((f32[5,8,128]{2,1,0:T(8,128)S(1)}, f32[5,8,128]{2,1,0:T(8,128)S(1)}, u32[]{:S(2)}, u32[]{:S(2)}) %collective-permute-start.5) | collective-permute-done | bytes 20512 | tf_op jit(solution)/shard_map/ppermute | solution.py:309
  29.0 0.0 collective-permute-done.4
  29.0 0.1 collective-permute-start.9
  29.1 0.9 %collective-permute-start.8 = (f32[5,8,128]{2,1,0:T(8,128)S(1)}, f32[5,8,128]{2,1,0:T(8,128)S(1)}, u32[]{:S(2)}, u32[]{:S(2)}) collective-permute-start(f32[5,8,128]{2,1,0:T(8,128)S(1)} %add_add_fusion.3), channel_id=1, source_target_pairs={{0,16},{8,24},{16,0},{24,8},{32,48},{40,56},{48,32},{56,40},{64,80... | collective-permute-start | bytes 61448 | tf_op jit(solution)/shard_map/ppermute | solution.py:309
  30.1 0.9 %collective-permute-start.7 = (f32[5,8,128]{2,1,0:T(8,128)S(1)}, f32[5,8,128]{2,1,0:T(8,128)S(1)}, u32[]{:S(2)}, u32[]{:S(2)}) collective-permute-start(f32[5,8,128]{2,1,0:T(8,128)S(1)} %add_add_fusion.3), channel_id=1, source_target_pairs={{0,8},{8,0},{16,24},{24,16},{32,40},{40,32},{48,56},{56,48},{64,72... | collective-permute-start | bytes 61448 | tf_op jit(solution)/shard_map/ppermute | solution.py:309
  31.0 1.3 %collective-permute-done.9 = f32[5,8,128]{2,1,0:T(8,128)S(1)} collective-permute-done((f32[5,8,128]{2,1,0:T(8,128)S(1)}, f32[5,8,128]{2,1,0:T(8,128)S(1)}, u32[]{:S(2)}, u32[]{:S(2)}) %collective-permute-start.9) | collective-permute-done | bytes 20512 | tf_op jit(solution)/shard_map/ppermute | solution.py:309
  32.3 0.8 %collective-permute-done.8 = f32[5,8,128]{2,1,0:T(8,128)S(1)} collective-permute-done((f32[5,8,128]{2,1,0:T(8,128)S(1)}, f32[5,8,128]{2,1,0:T(8,128)S(1)}, u32[]{:S(2)}, u32[]{:S(2)}) %collective-permute-start.8) | collective-permute-done | bytes 20512 | tf_op jit(solution)/shard_map/ppermute | solution.py:309
  33.1 0.0 collective-permute-done.7
  33.1 3.2 %collective-permute-start.10 = (f32[5,8,128]{2,1,0:T(8,128)S(1)}, f32[5,8,128]{2,1,0:T(8,128)S(1)}, u32[]{:S(2)}, u32[]{:S(2)}) collective-permute-start(f32[5,8,128]{2,1,0:T(8,128)S(1)} %add_add_fusion.2), channel_id=1, source_target_pairs={{0,224},{8,232},{16,240},{24,248},{32,192},{40,200},{48,208},{56,2... | collective-permute-start | bytes 61448 | tf_op jit(solution)/shard_map/ppermute | solution.py:309
  36.3 1.9 %collective-permute-done.10 = f32[5,8,128]{2,1,0:T(8,128)S(1)} collective-permute-done((f32[5,8,128]{2,1,0:T(8,128)S(1)}, f32[5,8,128]{2,1,0:T(8,128)S(1)}, u32[]{:S(2)}, u32[]{:S(2)}) %collective-permute-start.10) | collective-permute-done | bytes 20512 | tf_op jit(solution)/shard_map/ppermute | solution.py:309
  38.2 0.6 relax.1
  38.8 1.5 %collective-permute-start.11 = (f32[4,16,8,128]{3,2,1,0:T(8,128)S(1)}, f32[4,16,8,128]{3,2,1,0:T(8,128)S(1)}, u32[]{:S(2)}, u32[]{:S(2)}) collective-permute-start(f32[4,16,8,128]{3,2,1,0:T(8,128)S(1)} %get-tuple-element.18.up0), channel_id=1, source_target_pairs={{0,1},{1,2},{2,3},{3,4},{4,5},{5,6},{6,7},{7,0},{8,9},{9,10},{10,1... | collective-permute-start | bytes 786440 | tf_op jit(solution)/shard_map/ppermute | solution.py:304
  40.3 2.1 %collective-permute-start.13 = (f32[4,16,8,128]{3,2,1,0:T(8,128)S(1)}, f32[4,16,8,128]{3,2,1,0:T(8,128)S(1)}, u32[]{:S(2)}, u32[]{:S(2)}) collective-permute-start(f32[4,16,8,128]{3,2,1,0:T(8,128)S(1)} %get-tuple-element.20.down0), channel_id=1, source_target_pairs={{0,7},{1,0},{2,1},{3,2},{4,3},{5,4},{6,5},{7,6},{8,15},{9,8},{10,9... | collective-permute-start | bytes 786440 | tf_op jit(solution)/shard_map/ppermute | solution.py:304
  42.4 0.6 collective-permute-start.12
  43.1 1.4 %collective-permute-start.14 = (f32[2,16,8,128]{3,2,1,0:T(8,128)S(1)}, f32[2,16,8,128]{3,2,1,0:T(8,128)S(1)}, u32[]{:S(2)}, u32[]{:S(2)}) collective-permute-start(f32[2,16,8,128]{3,2,1,0:T(8,128)S(1)} %get-tuple-element.21), channel_id=1, source_target_pairs={{0,6},{1,7},{2,0},{3,1},{4,2},{5,3},{6,4},{7,5},{8,14},{9,15},{10,... | collective-permute-start | bytes 393224 | tf_op jit(solution)/shard_map/ppermute | solution.py:304
  44.4 2.9 %collective-permute-done.12.up2 = f32[2,16,8,128]{3,2,1,0:T(8,128)S(1)} collective-permute-done((f32[2,16,8,128]{3,2,1,0:T(8,128)S(1)}, f32[2,16,8,128]{3,2,1,0:T(8,128)S(1)}, u32[]{:S(2)}, u32[]{:S(2)}) %collective-permute-start.12) | collective-permute-done | bytes 131104 | tf_op jit(solution)/shard_map/ppermute | solution.py:304
  47.4 6.4 %collective-permute-done.14.down2 = f32[2,16,8,128]{3,2,1,0:T(8,128)S(1)} collective-permute-done((f32[2,16,8,128]{3,2,1,0:T(8,128)S(1)}, f32[2,16,8,128]{3,2,1,0:T(8,128)S(1)}, u32[]{:S(2)}, u32[]{:S(2)}) %collective-permute-start.14) | collective-permute-done | bytes 131104 | tf_op jit(solution)/shard_map/ppermute | solution.py:304
  53.8 2.3 %stream.3 = (f32[4,16,8,128]{3,2,1,0:T(8,128)S(1)}, f32[4,16,8,128]{3,2,1,0:T(8,128)S(1)}, f32[5,8,128]{2,1,0:T(8,128)S(1)}) custom-call(s32[1]{0:T(128)} %bitcast.refs_0_.vel_ref, f32[4,16,8,128]{3,2,1,0:T(8,128)S(1)} %get-tuple-element.18.up0, f32[4,16,8,128]{3,2,1,0:T(8,128)S(1)} %collective-permute-done.11.up1, ...), custom_call_target="tpu_custom_call" | custom-call | tf_op jit(solution)/shard_map/stream/pallas_call | solution.py:254
  56.1 2.0 %collective-permute-start.17 = (f32[5,8,128]{2,1,0:T(8,128)S(1)}, f32[5,8,128]{2,1,0:T(8,128)S(1)}, u32[]{:S(2)}, u32[]{:S(2)}) collective-permute-start(f32[5,8,128]{2,1,0:T(8,128)S(1)} %get-tuple-element.22), channel_id=1, source_target_pairs={{0,96},{8,104},{16,112},{24,120},{32,64},{40,72},{48,80},{56,88},{... | collective-permute-start | bytes 61448 | tf_op jit(solution)/shard_map/ppermute | solution.py:309
  58.1 2.0 %collective-permute-start.16 = (f32[5,8,128]{2,1,0:T(8,128)S(1)}, f32[5,8,128]{2,1,0:T(8,128)S(1)}, u32[]{:S(2)}, u32[]{:S(2)}) collective-permute-start(f32[5,8,128]{2,1,0:T(8,128)S(1)} %get-tuple-element.22), channel_id=1, source_target_pairs={{0,64},{8,72},{16,80},{24,88},{32,96},{40,104},{48,112},{56,120},{... | collective-permute-start | bytes 61448 | tf_op jit(solution)/shard_map/ppermute | solution.py:309
  60.1 0.4 collective-permute-start.15
  60.6 1.2 %collective-permute-done.17 = f32[5,8,128]{2,1,0:T(8,128)S(1)} collective-permute-done((f32[5,8,128]{2,1,0:T(8,128)S(1)}, f32[5,8,128]{2,1,0:T(8,128)S(1)}, u32[]{:S(2)}, u32[]{:S(2)}) %collective-permute-start.17) | collective-permute-done | bytes 20512 | tf_op jit(solution)/shard_map/ppermute | solution.py:309
  61.8 1.0 %collective-permute-done.16 = f32[5,8,128]{2,1,0:T(8,128)S(1)} collective-permute-done((f32[5,8,128]{2,1,0:T(8,128)S(1)}, f32[5,8,128]{2,1,0:T(8,128)S(1)}, u32[]{:S(2)}, u32[]{:S(2)}) %collective-permute-start.16) | collective-permute-done | bytes 20512 | tf_op jit(solution)/shard_map/ppermute | solution.py:309
  62.8 1.1 %collective-permute-done.15 = f32[5,8,128]{2,1,0:T(8,128)S(1)} collective-permute-done((f32[5,8,128]{2,1,0:T(8,128)S(1)}, f32[5,8,128]{2,1,0:T(8,128)S(1)}, u32[]{:S(2)}, u32[]{:S(2)}) %collective-permute-start.15) | collective-permute-done | bytes 20512 | tf_op jit(solution)/shard_map/ppermute | solution.py:309
  63.9 0.1 collective-permute-start.20
  64.0 0.9 %collective-permute-start.19 = (f32[5,8,128]{2,1,0:T(8,128)S(1)}, f32[5,8,128]{2,1,0:T(8,128)S(1)}, u32[]{:S(2)}, u32[]{:S(2)}) collective-permute-start(f32[5,8,128]{2,1,0:T(8,128)S(1)} %add_add_fusion.1), channel_id=1, source_target_pairs={{0,16},{8,24},{16,0},{24,8},{32,48},{40,56},{48,32},{56,40},{64,80... | collective-permute-start | bytes 61448 | tf_op jit(solution)/shard_map/ppermute | solution.py:309
  65.0 0.9 %collective-permute-start.18 = (f32[5,8,128]{2,1,0:T(8,128)S(1)}, f32[5,8,128]{2,1,0:T(8,128)S(1)}, u32[]{:S(2)}, u32[]{:S(2)}) collective-permute-start(f32[5,8,128]{2,1,0:T(8,128)S(1)} %add_add_fusion.1), channel_id=1, source_target_pairs={{0,8},{8,0},{16,24},{24,16},{32,40},{40,32},{48,56},{56,48},{64,72... | collective-permute-start | bytes 61448 | tf_op jit(solution)/shard_map/ppermute | solution.py:309
  65.9 1.3 %collective-permute-done.20 = f32[5,8,128]{2,1,0:T(8,128)S(1)} collective-permute-done((f32[5,8,128]{2,1,0:T(8,128)S(1)}, f32[5,8,128]{2,1,0:T(8,128)S(1)}, u32[]{:S(2)}, u32[]{:S(2)}) %collective-permute-start.20) | collective-permute-done | bytes 20512 | tf_op jit(solution)/shard_map/ppermute | solution.py:309
  67.2 0.8 %collective-permute-done.19 = f32[5,8,128]{2,1,0:T(8,128)S(1)} collective-permute-done((f32[5,8,128]{2,1,0:T(8,128)S(1)}, f32[5,8,128]{2,1,0:T(8,128)S(1)}, u32[]{:S(2)}, u32[]{:S(2)}) %collective-permute-start.19) | collective-permute-done | bytes 20512 | tf_op jit(solution)/shard_map/ppermute | solution.py:309
  68.0 3.9 %collective-permute-start.21 = (f32[5,8,128]{2,1,0:T(8,128)S(1)}, f32[5,8,128]{2,1,0:T(8,128)S(1)}, u32[]{:S(2)}, u32[]{:S(2)}) collective-permute-start(f32[5,8,128]{2,1,0:T(8,128)S(1)} %add_add_fusion), channel_id=1, source_target_pairs={{0,224},{8,232},{16,240},{24,248},{32,192},{40,200},{48,208},{56,2... | collective-permute-start | bytes 61448 | tf_op jit(solution)/shard_map/ppermute | solution.py:309
  72.0 1.9 %collective-permute-done.21 = f32[5,8,128]{2,1,0:T(8,128)S(1)} collective-permute-done((f32[5,8,128]{2,1,0:T(8,128)S(1)}, f32[5,8,128]{2,1,0:T(8,128)S(1)}, u32[]{:S(2)}, u32[]{:S(2)}) %collective-permute-start.21) | collective-permute-done | bytes 20512 | tf_op jit(solution)/shard_map/ppermute | solution.py:309
  73.9 2.1 %relax_last.1 = f32[1024,128]{1,0:T(8,128)} custom-call(s32[1]{0:T(128)} %bitcast.refs_0_.vel_ref, f32[5,8,128]{2,1,0:T(8,128)S(1)} %add.55.refs_1_, f32[4,16,8,128]{3,2,1,0:T(8,128)S(1)} %get-tuple-element.23.refs_2_, f32[4,16,8,128]{3,2,1,0:T(8,128)S(1)} %get-tuple-element.24.refs_3_), custom_call_target="tpu_custom_call" | custom-call | tf_op jit(solution)/shard_map/relax_last/pallas_call | solution.py:254
  (12 shorter events, 0.1 us)
Async XLA Ops:
  0.0 1.0 %copy-start = (f32[128,4,256]{2,1,0:T(4,128)S(1)}, f32[128,4,256]{2,1,0:T(4,128)}, u32[]{:S(2)}) copy-start(f32[128,4,256]{2,1,0:T(4,128)} %param.1) | copy-start | bytes 1572868
  1.6 15.8 %collective-permute-start = (f32[4,16,8,128]{3,2,1,0:T(8,128)S(1)}, f32[4,16,8,128]{3,2,1,0:T(8,128)S(1)}, u32[]{:S(2)}, u32[]{:S(2)}) collective-permute-start(f32[4,16,8,128]{3,2,1,0:T(8,128)S(1)} %pack_up.1.up0), channel_id=1, source_target_pairs={{0,1},{1,2},{2,3},{3,4},{4,5},{5,6},{6,7},{7,0},{8,9},{9,10},{10,1... | collective-permute-start | bytes 786440 | tf_op jit(solution)/shard_map/ppermute | solution.py:304
  3.3 14.1 %collective-permute-start.2 = (f32[4,16,8,128]{3,2,1,0:T(8,128)S(1)}, f32[4,16,8,128]{3,2,1,0:T(8,128)S(1)}, u32[]{:S(2)}, u32[]{:S(2)}) collective-permute-start(f32[4,16,8,128]{3,2,1,0:T(8,128)S(1)} %pack_down.1.down0), channel_id=1, source_target_pairs={{0,7},{1,0},{2,1},{3,2},{4,3},{5,4},{6,5},{7,6},{8,15},{9,8},{10,9... | collective-permute-start | bytes 786440 | tf_op jit(solution)/shard_map/ppermute | solution.py:304
  5.8 11.6 %collective-permute-start.3 = (f32[2,16,8,128]{3,2,1,0:T(8,128)S(1)}, f32[2,16,8,128]{3,2,1,0:T(8,128)S(1)}, u32[]{:S(2)}, u32[]{:S(2)}) collective-permute-start(f32[2,16,8,128]{3,2,1,0:T(8,128)S(1)} %slice.9), channel_id=1, source_target_pairs={{0,6},{1,7},{2,0},{3,1},{4,2},{5,3},{6,4},{7,5},{8,14},{9,15},{10,... | collective-permute-start | bytes 393224 | tf_op jit(solution)/shard_map/ppermute | solution.py:304
  6.7 10.8 %collective-permute-start.1 = (f32[2,16,8,128]{3,2,1,0:T(8,128)S(1)}, f32[2,16,8,128]{3,2,1,0:T(8,128)S(1)}, u32[]{:S(2)}, u32[]{:S(2)}) collective-permute-start(f32[2,16,8,128]{3,2,1,0:T(8,128)S(1)} %slice.8), channel_id=1, source_target_pairs={{0,2},{1,3},{2,4},{3,5},{4,6},{5,7},{6,0},{7,1},{8,10},{9,11},{10,... | collective-permute-start | bytes 393224 | tf_op jit(solution)/shard_map/ppermute | solution.py:304
  19.7 6.4 %collective-permute-start.6 = (f32[5,8,128]{2,1,0:T(8,128)S(1)}, f32[5,8,128]{2,1,0:T(8,128)S(1)}, u32[]{:S(2)}, u32[]{:S(2)}) collective-permute-start(f32[5,8,128]{2,1,0:T(8,128)S(1)} %get-tuple-element.15), channel_id=1, source_target_pairs={{0,96},{8,104},{16,112},{24,120},{32,64},{40,72},{48,80},{56,88},{... | collective-permute-start | bytes 61448 | tf_op jit(solution)/shard_map/ppermute | solution.py:309
  24.3 4.7 %collective-permute-start.5 = (f32[5,8,128]{2,1,0:T(8,128)S(1)}, f32[5,8,128]{2,1,0:T(8,128)S(1)}, u32[]{:S(2)}, u32[]{:S(2)}) collective-permute-start(f32[5,8,128]{2,1,0:T(8,128)S(1)} %get-tuple-element.15), channel_id=1, source_target_pairs={{0,64},{8,72},{16,80},{24,88},{32,96},{40,104},{48,112},{56,120},{... | collective-permute-start | bytes 61448 | tf_op jit(solution)/shard_map/ppermute | solution.py:309
  24.3 4.7 %collective-permute-start.4 = (f32[5,8,128]{2,1,0:T(8,128)S(1)}, f32[5,8,128]{2,1,0:T(8,128)S(1)}, u32[]{:S(2)}, u32[]{:S(2)}) collective-permute-start(f32[5,8,128]{2,1,0:T(8,128)S(1)} %get-tuple-element.15), channel_id=1, source_target_pairs={{0,32},{8,40},{16,48},{24,56},{32,0},{40,8},{48,16},{56,24},{64,96... | collective-permute-start | bytes 61448 | tf_op jit(solution)/shard_map/ppermute | solution.py:309
  29.0 3.3 %collective-permute-start.9 = (f32[5,8,128]{2,1,0:T(8,128)S(1)}, f32[5,8,128]{2,1,0:T(8,128)S(1)}, u32[]{:S(2)}, u32[]{:S(2)}) collective-permute-start(f32[5,8,128]{2,1,0:T(8,128)S(1)} %add_add_fusion.3), channel_id=1, source_target_pairs={{0,24},{8,16},{16,8},{24,0},{32,56},{40,48},{48,40},{56,32},{64,88... | collective-permute-start | bytes 61448 | tf_op jit(solution)/shard_map/ppermute | solution.py:309
  29.1 4.0 %collective-permute-start.8 = (f32[5,8,128]{2,1,0:T(8,128)S(1)}, f32[5,8,128]{2,1,0:T(8,128)S(1)}, u32[]{:S(2)}, u32[]{:S(2)}) collective-permute-start(f32[5,8,128]{2,1,0:T(8,128)S(1)} %add_add_fusion.3), channel_id=1, source_target_pairs={{0,16},{8,24},{16,0},{24,8},{32,48},{40,56},{48,32},{56,40},{64,80... | collective-permute-start | bytes 61448 | tf_op jit(solution)/shard_map/ppermute | solution.py:309
  30.1 3.0 %collective-permute-start.7 = (f32[5,8,128]{2,1,0:T(8,128)S(1)}, f32[5,8,128]{2,1,0:T(8,128)S(1)}, u32[]{:S(2)}, u32[]{:S(2)}) collective-permute-start(f32[5,8,128]{2,1,0:T(8,128)S(1)} %add_add_fusion.3), channel_id=1, source_target_pairs={{0,8},{8,0},{16,24},{24,16},{32,40},{40,32},{48,56},{56,48},{64,72... | collective-permute-start | bytes 61448 | tf_op jit(solution)/shard_map/ppermute | solution.py:309
  33.1 5.1 %collective-permute-start.10 = (f32[5,8,128]{2,1,0:T(8,128)S(1)}, f32[5,8,128]{2,1,0:T(8,128)S(1)}, u32[]{:S(2)}, u32[]{:S(2)}) collective-permute-start(f32[5,8,128]{2,1,0:T(8,128)S(1)} %add_add_fusion.2), channel_id=1, source_target_pairs={{0,224},{8,232},{16,240},{24,248},{32,192},{40,200},{48,208},{56,2... | collective-permute-start | bytes 61448 | tf_op jit(solution)/shard_map/ppermute | solution.py:309
  38.8 15.0 %collective-permute-start.11 = (f32[4,16,8,128]{3,2,1,0:T(8,128)S(1)}, f32[4,16,8,128]{3,2,1,0:T(8,128)S(1)}, u32[]{:S(2)}, u32[]{:S(2)}) collective-permute-start(f32[4,16,8,128]{3,2,1,0:T(8,128)S(1)} %get-tuple-element.18.up0), channel_id=1, source_target_pairs={{0,1},{1,2},{2,3},{3,4},{4,5},{5,6},{6,7},{7,0},{8,9},{9,10},{10,1... | collective-permute-start | bytes 786440 | tf_op jit(solution)/shard_map/ppermute | solution.py:304
  40.3 13.5 %collective-permute-start.13 = (f32[4,16,8,128]{3,2,1,0:T(8,128)S(1)}, f32[4,16,8,128]{3,2,1,0:T(8,128)S(1)}, u32[]{:S(2)}, u32[]{:S(2)}) collective-permute-start(f32[4,16,8,128]{3,2,1,0:T(8,128)S(1)} %get-tuple-element.20.down0), channel_id=1, source_target_pairs={{0,7},{1,0},{2,1},{3,2},{4,3},{5,4},{6,5},{7,6},{8,15},{9,8},{10,9... | collective-permute-start | bytes 786440 | tf_op jit(solution)/shard_map/ppermute | solution.py:304
  42.4 5.0 %collective-permute-start.12 = (f32[2,16,8,128]{3,2,1,0:T(8,128)S(1)}, f32[2,16,8,128]{3,2,1,0:T(8,128)S(1)}, u32[]{:S(2)}, u32[]{:S(2)}) collective-permute-start(f32[2,16,8,128]{3,2,1,0:T(8,128)S(1)} %get-tuple-element.19), channel_id=1, source_target_pairs={{0,2},{1,3},{2,4},{3,5},{4,6},{5,7},{6,0},{7,1},{8,10},{9,11},{10,... | collective-permute-start | bytes 393224 | tf_op jit(solution)/shard_map/ppermute | solution.py:304
  43.1 10.8 %collective-permute-start.14 = (f32[2,16,8,128]{3,2,1,0:T(8,128)S(1)}, f32[2,16,8,128]{3,2,1,0:T(8,128)S(1)}, u32[]{:S(2)}, u32[]{:S(2)}) collective-permute-start(f32[2,16,8,128]{3,2,1,0:T(8,128)S(1)} %get-tuple-element.21), channel_id=1, source_target_pairs={{0,6},{1,7},{2,0},{3,1},{4,2},{5,3},{6,4},{7,5},{8,14},{9,15},{10,... | collective-permute-start | bytes 393224 | tf_op jit(solution)/shard_map/ppermute | solution.py:304
  56.1 5.6 %collective-permute-start.17 = (f32[5,8,128]{2,1,0:T(8,128)S(1)}, f32[5,8,128]{2,1,0:T(8,128)S(1)}, u32[]{:S(2)}, u32[]{:S(2)}) collective-permute-start(f32[5,8,128]{2,1,0:T(8,128)S(1)} %get-tuple-element.22), channel_id=1, source_target_pairs={{0,96},{8,104},{16,112},{24,120},{32,64},{40,72},{48,80},{56,88},{... | collective-permute-start | bytes 61448 | tf_op jit(solution)/shard_map/ppermute | solution.py:309
  58.1 4.7 %collective-permute-start.16 = (f32[5,8,128]{2,1,0:T(8,128)S(1)}, f32[5,8,128]{2,1,0:T(8,128)S(1)}, u32[]{:S(2)}, u32[]{:S(2)}) collective-permute-start(f32[5,8,128]{2,1,0:T(8,128)S(1)} %get-tuple-element.22), channel_id=1, source_target_pairs={{0,64},{8,72},{16,80},{24,88},{32,96},{40,104},{48,112},{56,120},{... | collective-permute-start | bytes 61448 | tf_op jit(solution)/shard_map/ppermute | solution.py:309
  60.1 3.8 %collective-permute-start.15 = (f32[5,8,128]{2,1,0:T(8,128)S(1)}, f32[5,8,128]{2,1,0:T(8,128)S(1)}, u32[]{:S(2)}, u32[]{:S(2)}) collective-permute-start(f32[5,8,128]{2,1,0:T(8,128)S(1)} %get-tuple-element.22), channel_id=1, source_target_pairs={{0,32},{8,40},{16,48},{24,56},{32,0},{40,8},{48,16},{56,24},{64,96... | collective-permute-start | bytes 61448 | tf_op jit(solution)/shard_map/ppermute | solution.py:309
  63.9 3.3 %collective-permute-start.20 = (f32[5,8,128]{2,1,0:T(8,128)S(1)}, f32[5,8,128]{2,1,0:T(8,128)S(1)}, u32[]{:S(2)}, u32[]{:S(2)}) collective-permute-start(f32[5,8,128]{2,1,0:T(8,128)S(1)} %add_add_fusion.1), channel_id=1, source_target_pairs={{0,24},{8,16},{16,8},{24,0},{32,56},{40,48},{48,40},{56,32},{64,88... | collective-permute-start | bytes 61448 | tf_op jit(solution)/shard_map/ppermute | solution.py:309
  64.0 4.0 %collective-permute-start.19 = (f32[5,8,128]{2,1,0:T(8,128)S(1)}, f32[5,8,128]{2,1,0:T(8,128)S(1)}, u32[]{:S(2)}, u32[]{:S(2)}) collective-permute-start(f32[5,8,128]{2,1,0:T(8,128)S(1)} %add_add_fusion.1), channel_id=1, source_target_pairs={{0,16},{8,24},{16,0},{24,8},{32,48},{40,56},{48,32},{56,40},{64,80... | collective-permute-start | bytes 61448 | tf_op jit(solution)/shard_map/ppermute | solution.py:309
  65.0 3.0 %collective-permute-start.18 = (f32[5,8,128]{2,1,0:T(8,128)S(1)}, f32[5,8,128]{2,1,0:T(8,128)S(1)}, u32[]{:S(2)}, u32[]{:S(2)}) collective-permute-start(f32[5,8,128]{2,1,0:T(8,128)S(1)} %add_add_fusion.1), channel_id=1, source_target_pairs={{0,8},{8,0},{16,24},{24,16},{32,40},{40,32},{48,56},{56,48},{64,72... | collective-permute-start | bytes 61448 | tf_op jit(solution)/shard_map/ppermute | solution.py:309
  68.0 5.8 %collective-permute-start.21 = (f32[5,8,128]{2,1,0:T(8,128)S(1)}, f32[5,8,128]{2,1,0:T(8,128)S(1)}, u32[]{:S(2)}, u32[]{:S(2)}) collective-permute-start(f32[5,8,128]{2,1,0:T(8,128)S(1)} %add_add_fusion), channel_id=1, source_target_pairs={{0,224},{8,232},{16,240},{24,248},{32,192},{40,200},{48,208},{56,2... | collective-permute-start | bytes 61448 | tf_op jit(solution)/shard_map/ppermute | solution.py:309
